TPU v7x, 512 devices: a 4x2x32 block of a 4x8x32 slice. The times are simulated.
512 devices in a mesh: grp: 2 (over y), row: 32 (over z), col: 4 (over x), frm: 2 (over core).
Axes of the slice: x: 4, y: 2, z: 32, core: 2. Of those that a mesh axis runs over, the one named last changes fastest.
The devices are a block of a 4x8x32 slice.
Arguments:
- latent: bfloat16 [4, 128, 640, 256], P(('grp', 'frm'), 'row', 'col'), parts along dimension 0, may hold values from -6 to 6
- proj_weight: bfloat16 [256, 128], replicated, may hold values from -0.375 to 0.375
- proj_bias: float32 [128], replicated, may hold values from -3 to 3
- cache_one: bfloat16 [4, 256, 1280, 128], P(('grp', 'frm'), 'row', 'col'), parts along dimension 0, may hold values from -6 to 6
- cache_two: bfloat16 [4, 256, 1280, 128], P(('grp', 'frm'), 'row', 'col'), parts along dimension 0, may hold values from -6 to 6
- conv_one: bfloat16 [3, 3, 3, 128, 128], replicated, may hold values from -0.109375 to 0.109375
- bias_one: float32 [128], replicated, may hold values from -3 to 3
- conv_two: bfloat16 [3, 3, 3, 128, 128], replicated, may hold values from -0.109375 to 0.109375
- bias_two: float32 [128], replicated, may hold values from -3 to 3
Outputs:
- decoded: bfloat16 [4, 256, 1280, 128], P(('grp', 'frm'), 'row', 'col'), parts along dimension 0
There are 2 independent parts, one for each index of `grp`. A program takes and returns all parts, laid end to end along the dimension named above; an argument that names none is the same for every part. Nothing has to cross between parts.
All inputs are finite; a program needn't handle non-finite values.
Results may differ from a plain program's by a relative error of at most 0.0044.
Values may be sent and summed in bfloat16 or wider, within the bound.
No kernel may reach another device: no remote copies, remote signals or barrier semaphores. Data moves between devices by JAX's collectives and lax.ppermute only.
A program may use at most 64 MiB of HBM per device.

v0:
```python
import jax
import jax.numpy as jnp
from jax import lax
from jax.sharding import PartitionSpec as P


def padded_2(cells, sides, width):
    for axis, dim in sides:
        count = lax.axis_size(axis)
        ends = count - 1
        head = lax.slice_in_dim(cells, 0, width, axis=dim)
        tail = lax.slice_in_dim(cells, cells.shape[dim] - width, cells.shape[dim], axis=dim)
        cells = jnp.concatenate(
            [
                lax.ppermute(tail, axis, [(i, (i + 1) % count) for i in range(ends)]),
                cells,
                lax.ppermute(head, axis, [((i + 1) % count, i) for i in range(ends)]),
            ],
            axis=dim,
        )
    return cells


def from_partner(x, axis, stride):
    return lax.ppermute(x, axis, [(i, i ^ 1 << stride) for i in range(lax.axis_size(axis))])


def neighbour_frames(cached, current):
    leading = lax.axis_index("frm") == 0
    paired = jnp.stack([cached, current])
    rimmed = padded_2(paired, (("row", 1), ("col", 2)), 1)
    payload = jnp.where(leading, rimmed[1], rimmed[0])
    middle = from_partner(payload, "frm", 0)
    padded = jnp.stack([rimmed[0], middle, rimmed[1]])
    return padded


def causal_conv(padded, weight, bias):
    tile_rows, tile_cols, channels = (padded.shape[1] - 2, padded.shape[2] - 2, padded.shape[3])
    folded = weight.reshape(3, 3, 3 * channels, weight.shape[-1])
    summed = jnp.zeros((tile_rows * tile_cols, weight.shape[-1]), jnp.float32)
    for frame_step in range(3):
        for row_step in range(3):
            stencil = jnp.concatenate(
                [
                    padded[
                        frame_step, row_step : row_step + tile_rows, col_step : col_step + tile_cols
                    ]
                    for col_step in range(3)
                ],
                axis=-1,
            ).reshape(tile_rows * tile_cols, 3 * channels)
            summed = summed + jnp.dot(
                stencil, folded[frame_step, row_step], preferred_element_type=jnp.float32
            )
    return (summed + bias).reshape(tile_rows, tile_cols, -1)


def per_device(
    latent, proj_weight, proj_bias, cache_one, cache_two, conv_one, bias_one, conv_two, bias_two
):
    coarse = latent[0]
    half_rows, half_cols, widths = coarse.shape
    projected = (
        jnp.dot(
            coarse.reshape(half_rows * half_cols, widths),
            proj_weight,
            preferred_element_type=jnp.float32,
        )
        + proj_bias
    )
    projected = projected.reshape(half_rows, half_cols, -1).astype(jnp.bfloat16)
    upsampled = jnp.repeat(jnp.repeat(projected, 2, axis=0), 2, axis=1)
    act_one = jax.nn.silu(upsampled.astype(jnp.float32)).astype(jnp.bfloat16)
    first_out = causal_conv(neighbour_frames(cache_one[0], act_one), conv_one, bias_one)
    act_two = jax.nn.silu(first_out).astype(jnp.bfloat16)
    second_out = causal_conv(neighbour_frames(cache_two[0], act_two), conv_two, bias_two)
    decoded = (upsampled.astype(jnp.float32) + second_out).astype(jnp.bfloat16)
    return decoded[None]


def solution(mesh):
    placed = (
        P(("grp", "frm"), "row", "col", None),
        P(),
        P(),
        P(("grp", "frm"), "row", "col", None),
        P(("grp", "frm"), "row", "col", None),
        P(),
        P(),
        P(),
        P(),
    )
    return jax.shard_map(
        per_device,
        mesh=mesh,
        in_specs=placed,
        out_specs=P(("grp", "frm"), "row", "col", None),
        check_vma=False,
    )
```

profile of v0, /device:TPU:33, one launch (start us, length us, event | category | flops | bytes accessed | tf_op | source)
XLA Modules:
  0.0 107.4 jit_solution(7562897018821834)
XLA Ops:
  0.0 1.0 copy-done
  1.0 1.1 %fusion.94 = bf16[640,128]{1,0:T(8,128)(2,1)S(1)} fusion(bf16[640,256]{1,0:T(8,128)(2,1)S(1)} %bitcast.126, bf16[256,128]{1,0:T(8,128)(2,1)} %param.10, f32[128]{0:T(128)} %param.11), kind=kOutput, calls=%fused_computation.122 | convolution fusion | flops 42106880 | bytes 557568 | tf_op jit(solution)/shard_map/dot_general | solution.py:65
  3.2 1.3 %collective-permute-start.1 = (bf16[2,1,320,128]{3,2,1,0:T(8,128)(2,1)S(1)}, bf16[2,1,320,128]{3,2,1,0:T(8,128)(2,1)S(1)}, u32[]{:S(2)}, u32[]{:S(2)}) collective-permute-start(bf16[2,1,320,128]{3,2,1,0:T(8,128)(2,1)S(1)} %get-tuple-element.52), channel_id=1, source_target_pairs={{8,0},{16,8},{24,16},{32,24},{40,32},{48,40},{56,48},{64,56},{72,6... | collective-permute-start | bytes 491528 | tf_op jit(solution)/shard_map/ppermute | solution.py:17
  4.6 5.9 %collective-permute-start = (bf16[2,1,320,128]{3,2,1,0:T(8,128)(2,1)S(1)}, bf16[2,1,320,128]{3,2,1,0:T(8,128)(2,1)S(1)}, u32[]{:S(2)}, u32[]{:S(2)}) collective-permute-start(bf16[2,1,320,128]{3,2,1,0:T(8,128)(2,1)S(1)} %get-tuple-element.51), channel_id=1, source_target_pairs={{0,8},{8,16},{16,24},{24,32},{32,40},{40,48},{48,56},{56,64},{64,7... | collective-permute-start | bytes 491528 | tf_op jit(solution)/shard_map/ppermute | solution.py:15
  10.5 1.2 %multiply_convert_fusion.2 = bf16[2560,128]{1,0:T(8,128)(2,1)} fusion(f32[2560,128]{1,0:T(8,128)S(1)} %bitcast.130), kind=kLoop, calls=%fused_computation.119 | loop fusion | flops 1638400 | bytes 1966080 | tf_op jit(solution)/shard_map/convert_element_type | solution.py:74
  11.6 1.2 %collective-permute-done = bf16[2,1,320,128]{3,2,1,0:T(8,128)(2,1)S(1)} collective-permute-done((bf16[2,1,320,128]{3,2,1,0:T(8,128)(2,1)S(1)}, bf16[2,1,320,128]{3,2,1,0:T(8,128)(2,1)S(1)}, u32[]{:S(2)}, u32[]{:S(2)}) %collective-permute-start) | collective-permute-done | bytes 163872 | tf_op jit(solution)/shard_map/ppermute | solution.py:15
  12.8 3.9 %collective-permute-start.2 = (bf16[2,10,1,128]{3,2,1,0:T(2,128)(2,1)S(1)}, bf16[2,10,1,128]{3,2,1,0:T(2,128)(2,1)S(1)}, u32[]{:S(2)}, u32[]{:S(2)}) collective-permute-start(bf16[2,10,1,128]{3,2,1,0:T(2,128)(2,1)S(1)} %get-tuple-element.35), channel_id=1, source_target_pairs={{0,2},{2,4},{4,6},{1,3},{3,5},{5,7},{8,10},{10,12},{12,14},{9,11},... | collective-permute-start | bytes 15368 | tf_op jit(solution)/shard_map/ppermute | solution.py:15
  16.7 1.3 %collective-permute-start.3 = (bf16[2,10,1,128]{3,2,1,0:T(2,128)(2,1)S(1)}, bf16[2,10,1,128]{3,2,1,0:T(2,128)(2,1)S(1)}, u32[]{:S(2)}, u32[]{:S(2)}) collective-permute-start(bf16[2,10,1,128]{3,2,1,0:T(2,128)(2,1)S(1)} %get-tuple-element.36), channel_id=1, source_target_pairs={{2,0},{4,2},{6,4},{3,1},{5,3},{7,5},{10,8},{12,10},{14,12},{11,9},... | collective-permute-start | bytes 15368 | tf_op jit(solution)/shard_map/ppermute | solution.py:17
  18.4 2.8 %collective-permute-done.3 = bf16[2,10,1,128]{3,2,1,0:T(2,128)(2,1)S(1)} collective-permute-done((bf16[2,10,1,128]{3,2,1,0:T(2,128)(2,1)S(1)}, bf16[2,10,1,128]{3,2,1,0:T(2,128)(2,1)S(1)}, u32[]{:S(2)}, u32[]{:S(2)}) %collective-permute-start.3) | collective-permute-done | bytes 5152 | tf_op jit(solution)/shard_map/ppermute | solution.py:17
  21.8 41.1 %collective-permute-start.4 = (bf16[10,322,128]{2,1,0:T(8,128)(2,1)S(1)}, bf16[10,322,128]{2,1,0:T(8,128)(2,1)S(1)}, u32[]{:S(2)}, u32[]{:S(2)}) collective-permute-start(bf16[10,322,128]{2,1,0:T(8,128)(2,1)S(1)} %fusion.96), channel_id=1, source_target_pairs={{0,1},{1,0},{2,3},{3,2},{4,5},{5,4},{6,7},{7,6},{8,9},{9,8},{10,11... | collective-permute-start | bytes 2472968 | tf_op jit(solution)/shard_map/ppermute | solution.py:25
  63.0 1.7 %maximum_maximum_fusion = (bf16[2,10,321,128]{3,2,1,0:T(8,128)(2,1)S(1)}, bf16[2,10,321,128]{3,2,1,0:T(8,128)(2,1)S(1)}) fusion(bf16[2,1,320,128]{3,2,1,0:T(8,128)(2,1)S(1)} %collective-permute-done.1, bf16[1,8,320,128]{3,2,1,0:T(8,128)(2,1)S(1)} %multiply_convert_fusion.3, bf16[1,8,320,128]{3,2,1,0:T(8,128)(2,1)S(1)} %copy-done.2, ...), kind=kLoop, calls=%fused_computation.110 | loop fusion | flops 16435200 | bytes 4935680 | tf_op jit(solution)/shard_map/concatenate | solution.py:13
  64.7 1.4 %fusion.117 = (bf16[1,8,320,128]{3,2,1,0:T(8,128)(2,1)S(1)}, bf16[1,8,320,128]{3,2,1,0:T(8,128)(2,1)S(1)}, bf16[1,8,320,128]{3,2,1,0:T(8,128)(2,1)S(1)}, bf16[1,...) fusion(bf16[2,10,321,128]{3,2,1,0:T(8,128)(2,1)S(1)} %get-tuple, ...), kind=kLoop, calls=%fused_computation.189 | loop fusion | bytes 15728640 | tf_op jit(solution)/shard_map/slice | solution.py:46
  66.9 0.7 convolution_add_fusion.15
  67.6 0.7 convolution_add_fusion.14
  68.3 1.1 %fusion.120 = (bf16[1,8,320,128]{3,2,1,0:T(8,128)(2,1)S(1)}, bf16[1,8,320,128]{3,2,1,0:T(8,128)(2,1)S(1)}, bf16[1,8,320,128]{3,2,1,0:T(8,128)(2,1)S(1)}, bf16[1,...) fusion(bf16[1,10,322,128]{3,2,1,0:T(8,128)(2,1)S(1)} %bitcast.127), kind=kLoop, calls=%fused_computation.192 | loop fusion | bytes 11796480 | tf_op jit(solution)/shard_map/slice | solution.py:46
  73.2 0.8 multiply_convert_fusion
  74.4 0.7 copy-done.3
  75.1 1.3 %collective-permute-start.6 = (bf16[2,1,320,128]{3,2,1,0:T(8,128)(2,1)S(1)}, bf16[2,1,320,128]{3,2,1,0:T(8,128)(2,1)S(1)}, u32[]{:S(2)}, u32[]{:S(2)}) collective-permute-start(bf16[2,1,320,128]{3,2,1,0:T(8,128)(2,1)S(1)} %get-tuple-element.48), channel_id=1, source_target_pairs={{8,0},{16,8},{24,16},{32,24},{40,32},{48,40},{56,48},{64,56},{72,6... | collective-permute-start | bytes 491528 | tf_op jit(solution)/shard_map/ppermute | solution.py:17
  76.4 4.8 %collective-permute-start.5 = (bf16[2,1,320,128]{3,2,1,0:T(8,128)(2,1)S(1)}, bf16[2,1,320,128]{3,2,1,0:T(8,128)(2,1)S(1)}, u32[]{:S(2)}, u32[]{:S(2)}) collective-permute-start(bf16[2,1,320,128]{3,2,1,0:T(8,128)(2,1)S(1)} %get-tuple-element.47), channel_id=1, source_target_pairs={{0,8},{8,16},{16,24},{24,32},{32,40},{40,48},{48,56},{56,64},{64,7... | collective-permute-start | bytes 491528 | tf_op jit(solution)/shard_map/ppermute | solution.py:15
  81.2 2.6 %collective-permute-done.6 = bf16[2,1,320,128]{3,2,1,0:T(8,128)(2,1)S(1)} collective-permute-done((bf16[2,1,320,128]{3,2,1,0:T(8,128)(2,1)S(1)}, bf16[2,1,320,128]{3,2,1,0:T(8,128)(2,1)S(1)}, u32[]{:S(2)}, u32[]{:S(2)}) %collective-permute-start.6) | collective-permute-done | bytes 163872 | tf_op jit(solution)/shard_map/ppermute | solution.py:17
  83.8 0.9 collective-permute-done.5
  84.8 1.4 %collective-permute-start.7 = (bf16[2,10,1,128]{3,2,1,0:T(2,128)(2,1)S(1)}, bf16[2,10,1,128]{3,2,1,0:T(2,128)(2,1)S(1)}, u32[]{:S(2)}, u32[]{:S(2)}) collective-permute-start(bf16[2,10,1,128]{3,2,1,0:T(2,128)(2,1)S(1)} %get-tuple-element.31), channel_id=1, source_target_pairs={{0,2},{2,4},{4,6},{1,3},{3,5},{5,7},{8,10},{10,12},{12,14},{9,11},... | collective-permute-start | bytes 15368 | tf_op jit(solution)/shard_map/ppermute | solution.py:15
  86.2 1.5 %collective-permute-start.8 = (bf16[2,10,1,128]{3,2,1,0:T(2,128)(2,1)S(1)}, bf16[2,10,1,128]{3,2,1,0:T(2,128)(2,1)S(1)}, u32[]{:S(2)}, u32[]{:S(2)}) collective-permute-start(bf16[2,10,1,128]{3,2,1,0:T(2,128)(2,1)S(1)} %get-tuple-element.32), channel_id=1, source_target_pairs={{2,0},{4,2},{6,4},{3,1},{5,3},{7,5},{10,8},{12,10},{14,12},{11,9},... | collective-permute-start | bytes 15368 | tf_op jit(solution)/shard_map/ppermute | solution.py:17
  88.0 2.6 %collective-permute-done.8 = bf16[2,10,1,128]{3,2,1,0:T(2,128)(2,1)S(1)} collective-permute-done((bf16[2,10,1,128]{3,2,1,0:T(2,128)(2,1)S(1)}, bf16[2,10,1,128]{3,2,1,0:T(2,128)(2,1)S(1)}, u32[]{:S(2)}, u32[]{:S(2)}) %collective-permute-start.8) | collective-permute-done | bytes 5152 | tf_op jit(solution)/shard_map/ppermute | solution.py:17
  90.6 1.7 %maximum_maximum_fusion.1 = (bf16[2,10,321,128]{3,2,1,0:T(8,128)(2,1)S(1)}, bf16[2,10,321,128]{3,2,1,0:T(8,128)(2,1)S(1)}) fusion(bf16[2,1,320,128]{3,2,1,0:T(8,128)(2,1)S(1)} %collective-permute-done.6, bf16[1,8,320,128]{3,2,1,0:T(8,128)(2,1)S(1)} %multiply_convert_fusion.1, bf16[1,8,320,128]{3,2,1,0:T(8,128)(2,1)S(1)} %copy-done.3, ...), kind=kLoop, calls=%fused_computation.113 | loop fusion | flops 16435200 | bytes 4935680 | tf_op jit(solution)/shard_map/concatenate | solution.py:13
  92.3 0.7 fusion.116
  93.0 0.9 fusion.115
  94.6 4.4 %collective-permute-start.9 = (bf16[10,322,128]{2,1,0:T(8,128)(2,1)S(1)}, bf16[10,322,128]{2,1,0:T(8,128)(2,1)S(1)}, u32[]{:S(2)}, u32[]{:S(2)}) collective-permute-start(bf16[10,322,128]{2,1,0:T(8,128)(2,1)S(1)} %fusion.95), channel_id=1, source_target_pairs={{0,1},{1,0},{2,3},{3,2},{4,5},{5,4},{6,7},{7,6},{8,9},{9,8},{10,11... | collective-permute-start | bytes 2472968 | tf_op jit(solution)/shard_map/ppermute | solution.py:25
  99.7 0.7 convolution_add_fusion.7
  100.4 0.7 convolution_add_fusion.6
  101.1 1.1 %fusion.119 = (bf16[1,8,320,128]{3,2,1,0:T(8,128)(2,1)S(1)}, bf16[1,8,320,128]{3,2,1,0:T(8,128)(2,1)S(1)}, bf16[1,8,320,128]{3,2,1,0:T(8,128)(2,1)S(1)}, bf16[1,...) fusion(bf16[1,10,322,128]{3,2,1,0:T(8,128)(2,1)S(1)} %bitcast.128), kind=kLoop, calls=%fused_computation.191 | loop fusion | bytes 11796480 | tf_op jit(solution)/shard_map/slice | solution.py:46
  106.4 1.0 add_convert_fusion
  (48 shorter events, 12.7 us)
Async XLA Ops:
  0.0 1.0 copy-start
  2.1 1.1 %copy-start.2 = (bf16[1,8,320,128]{3,2,1,0:T(8,128)(2,1)S(1)}, bf16[1,8,320,128]{3,2,1,0:T(8,128)(2,1)}, u32[]{:S(2)}) copy-start(bf16[1,8,320,128]{3,2,1,0:T(8,128)(2,1)} %param.12) | copy-start | bytes 1966084
  3.2 8.4 %collective-permute-start.1 = (bf16[2,1,320,128]{3,2,1,0:T(8,128)(2,1)S(1)}, bf16[2,1,320,128]{3,2,1,0:T(8,128)(2,1)S(1)}, u32[]{:S(2)}, u32[]{:S(2)}) collective-permute-start(bf16[2,1,320,128]{3,2,1,0:T(8,128)(2,1)S(1)} %get-tuple-element.52), channel_id=1, source_target_pairs={{8,0},{16,8},{24,16},{32,24},{40,32},{48,40},{56,48},{64,56},{72,6... | collective-permute-start | bytes 491528 | tf_op jit(solution)/shard_map/ppermute | solution.py:17
  4.6 8.2 %collective-permute-start = (bf16[2,1,320,128]{3,2,1,0:T(8,128)(2,1)S(1)}, bf16[2,1,320,128]{3,2,1,0:T(8,128)(2,1)S(1)}, u32[]{:S(2)}, u32[]{:S(2)}) collective-permute-start(bf16[2,1,320,128]{3,2,1,0:T(8,128)(2,1)S(1)} %get-tuple-element.51), channel_id=1, source_target_pairs={{0,8},{8,16},{16,24},{24,32},{32,40},{40,48},{48,56},{56,64},{64,7... | collective-permute-start | bytes 491528 | tf_op jit(solution)/shard_map/ppermute | solution.py:15
  12.8 5.5 %collective-permute-start.2 = (bf16[2,10,1,128]{3,2,1,0:T(2,128)(2,1)S(1)}, bf16[2,10,1,128]{3,2,1,0:T(2,128)(2,1)S(1)}, u32[]{:S(2)}, u32[]{:S(2)}) collective-permute-start(bf16[2,10,1,128]{3,2,1,0:T(2,128)(2,1)S(1)} %get-tuple-element.35), channel_id=1, source_target_pairs={{0,2},{2,4},{4,6},{1,3},{3,5},{5,7},{8,10},{10,12},{12,14},{9,11},... | collective-permute-start | bytes 15368 | tf_op jit(solution)/shard_map/ppermute | solution.py:15
  16.7 4.4 %collective-permute-start.3 = (bf16[2,10,1,128]{3,2,1,0:T(2,128)(2,1)S(1)}, bf16[2,10,1,128]{3,2,1,0:T(2,128)(2,1)S(1)}, u32[]{:S(2)}, u32[]{:S(2)}) collective-permute-start(bf16[2,10,1,128]{3,2,1,0:T(2,128)(2,1)S(1)} %get-tuple-element.36), channel_id=1, source_target_pairs={{2,0},{4,2},{6,4},{3,1},{5,3},{7,5},{10,8},{12,10},{14,12},{11,9},... | collective-permute-start | bytes 15368 | tf_op jit(solution)/shard_map/ppermute | solution.py:17
  21.8 46.4 %collective-permute-start.4 = (bf16[10,322,128]{2,1,0:T(8,128)(2,1)S(1)}, bf16[10,322,128]{2,1,0:T(8,128)(2,1)S(1)}, u32[]{:S(2)}, u32[]{:S(2)}) collective-permute-start(bf16[10,322,128]{2,1,0:T(8,128)(2,1)S(1)} %fusion.96), channel_id=1, source_target_pairs={{0,1},{1,0},{2,3},{3,2},{4,5},{5,4},{6,7},{7,6},{8,9},{9,8},{10,11... | collective-permute-start | bytes 2472968 | tf_op jit(solution)/shard_map/ppermute | solution.py:25
  64.7 1.5 %copy-start.5 = (bf16[3,3,3,128,128]{4,3,2,1,0:T(8,128)(2,1)S(1)}, bf16[3,3,3,128,128]{4,3,2,1,0:T(8,128)(2,1)}, u32[]{:S(2)}) copy-start(bf16[3,3,3,128,128]{4,3,2,1,0:T(8,128)(2,1)} %param.14) | copy-start | bytes 2654212
  71.4 1.1 %copy-start.4 = (bf16[2560,128]{1,0:T(8,128)(2,1)S(1)}, bf16[2560,128]{1,0:T(8,128)(2,1)}, u32[]{:S(2)}) copy-start(bf16[2560,128]{1,0:T(8,128)(2,1)} %multiply_convert_fusion.2) | copy-start | bytes 1966084
  72.5 0.7 copy-start.7
  74.0 1.1 %copy-start.3 = (bf16[1,8,320,128]{3,2,1,0:T(8,128)(2,1)S(1)}, bf16[1,8,320,128]{3,2,1,0:T(8,128)(2,1)}, u32[]{:S(2)}) copy-start(bf16[1,8,320,128]{3,2,1,0:T(8,128)(2,1)} %param.13) | copy-start | bytes 1966084
  75.1 8.7 %collective-permute-start.6 = (bf16[2,1,320,128]{3,2,1,0:T(8,128)(2,1)S(1)}, bf16[2,1,320,128]{3,2,1,0:T(8,128)(2,1)S(1)}, u32[]{:S(2)}, u32[]{:S(2)}) collective-permute-start(bf16[2,1,320,128]{3,2,1,0:T(8,128)(2,1)S(1)} %get-tuple-element.48), channel_id=1, source_target_pairs={{8,0},{16,8},{24,16},{32,24},{40,32},{48,40},{56,48},{64,56},{72,6... | collective-permute-start | bytes 491528 | tf_op jit(solution)/shard_map/ppermute | solution.py:17
  76.4 8.3 %collective-permute-start.5 = (bf16[2,1,320,128]{3,2,1,0:T(8,128)(2,1)S(1)}, bf16[2,1,320,128]{3,2,1,0:T(8,128)(2,1)S(1)}, u32[]{:S(2)}, u32[]{:S(2)}) collective-permute-start(bf16[2,1,320,128]{3,2,1,0:T(8,128)(2,1)S(1)} %get-tuple-element.47), channel_id=1, source_target_pairs={{0,8},{8,16},{16,24},{24,32},{32,40},{40,48},{48,56},{56,64},{64,7... | collective-permute-start | bytes 491528 | tf_op jit(solution)/shard_map/ppermute | solution.py:15
  84.8 3.2 %collective-permute-start.7 = (bf16[2,10,1,128]{3,2,1,0:T(2,128)(2,1)S(1)}, bf16[2,10,1,128]{3,2,1,0:T(2,128)(2,1)S(1)}, u32[]{:S(2)}, u32[]{:S(2)}) collective-permute-start(bf16[2,10,1,128]{3,2,1,0:T(2,128)(2,1)S(1)} %get-tuple-element.31), channel_id=1, source_target_pairs={{0,2},{2,4},{4,6},{1,3},{3,5},{5,7},{8,10},{10,12},{12,14},{9,11},... | collective-permute-start | bytes 15368 | tf_op jit(solution)/shard_map/ppermute | solution.py:15
  86.2 4.4 %collective-permute-start.8 = (bf16[2,10,1,128]{3,2,1,0:T(2,128)(2,1)S(1)}, bf16[2,10,1,128]{3,2,1,0:T(2,128)(2,1)S(1)}, u32[]{:S(2)}, u32[]{:S(2)}) collective-permute-start(bf16[2,10,1,128]{3,2,1,0:T(2,128)(2,1)S(1)} %get-tuple-element.32), channel_id=1, source_target_pairs={{2,0},{4,2},{6,4},{3,1},{5,3},{7,5},{10,8},{12,10},{14,12},{11,9},... | collective-permute-start | bytes 15368 | tf_op jit(solution)/shard_map/ppermute | solution.py:17
  94.5 4.5 %copy-start.6 = (bf16[3,3,3,128,128]{4,3,2,1,0:T(8,128)(2,1)S(1)}, bf16[3,3,3,128,128]{4,3,2,1,0:T(8,128)(2,1)}, u32[]{:S(2)}) copy-start(bf16[3,3,3,128,128]{4,3,2,1,0:T(8,128)(2,1)} %param.16) | copy-start | bytes 2654212
  94.6 6.5 %collective-permute-start.9 = (bf16[10,322,128]{2,1,0:T(8,128)(2,1)S(1)}, bf16[10,322,128]{2,1,0:T(8,128)(2,1)S(1)}, u32[]{:S(2)}, u32[]{:S(2)}) collective-permute-start(bf16[10,322,128]{2,1,0:T(8,128)(2,1)S(1)} %fusion.95), channel_id=1, source_target_pairs={{0,1},{1,0},{2,3},{3,2},{4,5},{5,4},{6,7},{7,6},{8,9},{9,8},{10,11... | collective-permute-start | bytes 2472968 | tf_op jit(solution)/shard_map/ppermute | solution.py:25
  105.0 0.7 copy-start.8
  105.7 1.7 %copy-start.1 = (bf16[1,4,160,256]{3,2,1,0:T(8,128)(2,1)S(1)}, bf16[1,4,160,256]{3,2,1,0:T(8,128)(2,1)}, u32[]{:S(2)}) copy-start(bf16[1,4,160,256]{3,2,1,0:T(8,128)(2,1)} %param.9) | copy-start | bytes 983044
where the time goes:
time: 108 us; the launch traced here: 107 us
  starting transfers between devices  66.8 us (62%)
  matrix products  13.4 us (12%)
  waiting for transfers between devices  10.1 us (9%)
  other arithmetic  8.4 us (8%)
  local copies, waits for them, and re-layouts  8.16 us (8%)
    ppermute x2, starting transfers between devices, from_partner(): lax.ppermute(x, axis, [(i, i ^ 1 << stride) for i in range(lax.axis_size(...  45.5 us
    ppermute x4, starting transfers between devices, padded_2(): lax.ppermute(tail, axis, [(i, (i + 1) % count) for i in range(ends)])  15.9 us
    dot_general x18, matrix products, causal_conv(): jnp.dot(stencil, folded[frame_step, row_step], preferred_element_type=jnp...  12.3 us
    ppermute x4, waiting for transfers between devices, padded_2(): lax.ppermute(head, axis, [((i + 1) % count, i) for i in range(ends)])  8.02 us
    ppermute x4, starting transfers between devices, padded_2(): lax.ppermute(head, axis, [((i + 1) % count, i) for i in range(ends)])  5.41 us
    slice x5, local copies, waits for them, and re-layouts, causal_conv(): padded[frame_step, row_step:row_step + tile_rows, col_step:col_step + til...  5.26 us
    concatenate x6, other arithmetic, padded_2(): jnp.concatenate([lax.ppermute(tail, axis, [(i, (i + 1) % count) for i in...  5.23 us
    unnamed x18, local copies, waits for them, and re-layouts  2.4 us
  transfers between devices with their start and end apart: 10, of which 5 were waited for; matrix products, arithmetic and copies ran while one was open for 8% of the time, Pallas kernels for 0%

commit v1 on v0

v1 whole, which is shorter than its diff:
```python
import functools

import jax
import jax.numpy as jnp
from jax import lax
from jax.experimental import pallas as pl
from jax.experimental.pallas import tpu as pltpu
from jax.sharding import PartitionSpec as P

B = 16
BF = jnp.bfloat16
F32 = jnp.float32
VMEM = pl.BlockSpec(memory_space=pltpu.VMEM)
SMEM = pl.BlockSpec(memory_space=pltpu.SMEM)


def call(body, outs, scratch=(), flops=0, nbytes=0, smem_first=False, n_in=0, name=None):
    return pl.pallas_call(
        body,
        out_shape=[jax.ShapeDtypeStruct(s, d) for s, d in outs],
        in_specs=[SMEM if smem_first and i == 0 else VMEM for i in range(n_in)],
        out_specs=[VMEM] * len(outs),
        scratch_shapes=list(scratch),
        cost_estimate=pl.CostEstimate(flops=flops, bytes_accessed=nbytes, transcendentals=0),
        compiler_params=pltpu.CompilerParams(vmem_limit_bytes=32 * 1024 * 1024),
        name=name,
    )


def silu(v):
    return v / (1.0 + jnp.exp(-v))


def first_kernel(latent, weight, bias, one, two, proj, act, row_up, row_dn, col_lf, col_rt, two_up, two_dn):
    rows, cols, _ = one.shape
    crows, ccols, _ = latent.shape
    for i in range(crows):
        p = jnp.dot(latent[i], weight[...], preferred_element_type=F32) + bias[...]
        p = p.astype(BF)
        proj[i] = p
        a = silu(p.astype(F32)).astype(BF)
        act[i] = a
        if i == 0:
            row_up[2 * cols :, :] = a
        if i == crows - 1:
            row_dn[2 * cols :, :] = a
        o = (rows + i) * B
        col_lf[o : o + B, :] = a[:B]
        col_rt[o : o + B, :] = a[ccols - B :]
    for k in range(2):
        row_up[k * cols : (k + 1) * cols, :] = one[k]
        row_dn[k * cols : (k + 1) * cols, :] = one[rows - 2 + k]
    two_up[...] = two[0]
    two_dn[...] = two[rows - 1]
    for i in range(rows):
        o, o2 = i * B, (rows + crows + i) * B
        col_lf[o : o + B, :] = one[i, :B]
        col_rt[o : o + B, :] = one[i, cols - B :]
        col_lf[o2 : o2 + B, :] = two[i, :B]
        col_rt[o2 : o2 + B, :] = two[i, cols - B :]


def corner_kernel(rows, crows, from_right, from_left, merged, up, dn):
    low = lax.broadcasted_iota(jnp.int32, (B, 128), 0) < B // 2

    def block(i):
        s = slice(i * B, (i + 1) * B)
        return jnp.where(low, from_right[s, :].astype(F32), from_left[s, :].astype(F32)).astype(BF)

    for i in range(2 * rows + crows):
        b = block(i)
        merged[i * B : (i + 1) * B, :] = b
        for dst, picks in ((up, (0, 1, rows, rows + crows)), (dn, (rows - 2, rows - 1, rows + crows - 1, 2 * rows + crows - 1))):
            if i in picks:
                k = picks.index(i)
                dst[k * B : (k + 1) * B, :] = b


def blocks_of(merged, above, below, first, count, corner_first, corners):
    get = lambda ref, i: ref[i * B : (i + 1) * B, :].astype(F32)
    return (
        [get(above, corner_first + k) for k in range(corners)]
        + [get(merged, first + i) for i in range(count)]
        + [get(below, corner_first + k) for k in range(corners)]
    )


def fill_frame(dst, interiors, blocks, cols):
    low = lax.broadcasted_iota(jnp.int32, (B, 128), 0) < B // 2
    zero = jnp.zeros((B, 128), F32)
    stride = cols + B
    n = len(interiors)
    dst[0:B, :] = jnp.where(low, zero, blocks[0]).astype(BF)
    for i in range(n):
        o = B + i * stride
        dst[o : o + cols, :] = interiors[i]()
        right = blocks[i]
        left = blocks[i + 1] if i + 1 < n else zero
        dst[o + cols : o + stride, :] = jnp.where(low, right, left).astype(BF)
    dst[B + n * stride :, :] = jnp.zeros((B, 128), BF)


def second_kernel(where_ref, one, act, merged, row_a, row_b, cor_a, cor_b, cache_frame, act_frame, send):
    rows, cols, _ = one.shape
    crows, ccols, _ = act.shape
    stride = cols + B
    blocks = blocks_of(merged, cor_a, cor_b, 0, rows, 0, 2)
    inter = (
        [functools.partial(lambda k: row_a[k * cols : (k + 1) * cols, :], k) for k in range(2)]
        + [functools.partial(lambda k: one[k], k) for k in range(rows)]
        + [functools.partial(lambda k: row_b[k * cols : (k + 1) * cols, :], k) for k in range(2)]
    )
    fill_frame(cache_frame, inter, blocks, cols)
    coarse = [row_a[2 * cols :, :]] + [act[i] for i in range(crows)] + [row_b[2 * cols :, :]]
    cblocks = blocks_of(merged, cor_a, cor_b, rows, crows, 2, 1)
    spread = (
        lax.broadcasted_iota(jnp.int32, (cols, ccols), 0) // 2 == lax.broadcasted_iota(jnp.int32, (cols, ccols), 1)
    ).astype(F32).astype(BF)
    low = lax.broadcasted_iota(jnp.int32, (B, 128), 0) < B // 2
    zero = jnp.zeros((1, 128), F32)
    last = [b[0:1] for b in cblocks], [b[B - 1 : B] for b in cblocks] + [zero]
    n = crows + 2
    act_frame[0:B, :] = jnp.where(low, 0.0, jnp.broadcast_to(last[1][0], (B, 128))).astype(BF)
    for m in range(0, n, 2):
        wide = jnp.dot(spread, jnp.concatenate([coarse[m], coarse[m + 1]], axis=1), preferred_element_type=F32).astype(BF)
        for h in range(2):
            for k in range(2):
                i = 2 * (m + h) + k
                o = B + i * stride
                act_frame[o : o + cols, :] = wide[:, h * 128 : (h + 1) * 128]
                right = jnp.broadcast_to(last[0][m + h], (B, 128))
                left = jnp.broadcast_to(last[1][m + h + k], (B, 128))
                act_frame[o + cols : o + stride, :] = jnp.where(low, right, left).astype(BF)
    act_frame[B + 2 * n * stride :, :] = jnp.zeros((B, 128), BF)
    leading = where_ref[0] == 0

    @pl.when(leading)
    def _():
        send[...] = act_frame[...]

    @pl.when(jnp.logical_not(leading))
    def _():
        send[...] = cache_frame[...]


def second_cache_kernel(two, merged, two_a, two_b, cor_a, cor_b, frame, *, first):
    rows, cols, _ = two.shape
    blocks = blocks_of(merged, cor_a, cor_b, first, rows, 3, 1)
    inter = [lambda: two_a[...]] + [functools.partial(lambda k: two[k], k) for k in range(rows)] + [lambda: two_b[...]]
    fill_frame(frame, inter, blocks, cols)


def taps_into(summed, frames, steps, weight, stride, chunk, k):
    lo = 0 if k == 0 else B + k * stride
    hi = B + (k + 1) * stride
    pieces, w01, w2 = [], [], []
    for ref, a in zip(frames, steps):
        for p in range(3):
            pieces.append(ref[lo + p * stride : hi + p * stride, :])
            w01.append(jnp.concatenate([weight[a, p, 0], weight[a, p, 1]], axis=1))
            w2.append(weight[a, p, 2])
    lhs = jnp.concatenate(pieces, axis=1)
    y01 = jnp.dot(lhs, jnp.concatenate(w01, axis=0), preferred_element_type=F32)
    y2 = jnp.dot(lhs, jnp.concatenate(w2, axis=0), preferred_element_type=F32)
    summed[8 + lo : 8 + hi, 0:256] = y01
    summed[8 + lo : 8 + hi, 256:384] = y2


def shifted(summed, lo, hi):
    return (
        summed[7 + lo : 7 + hi, 0:128] + summed[8 + lo : 8 + hi, 128:256] + summed[9 + lo : 9 + hi, 256:384]
    )


def conv_one_kernel(where_ref, cache, act, middle, weight, bias, two_frame, out, send, summed, *, cols, n_out):
    stride = cols + B
    frm, row, rows_n, col, cols_n = (where_ref[i] for i in range(5))
    t = lax.broadcasted_iota(jnp.int32, (B, 128), 0)
    keep_right = (col != cols_n - 1).astype(F32)
    keep_left = (col != 0).astype(F32)
    row_ok = [jnp.float32(1.0)] * n_out
    row_ok[0] = (row != 0).astype(F32)
    row_ok[-1] = (row != rows_n - 1).astype(F32)
    for k in range(n_out + 1):
        if k < n_out:
            taps_into(summed, (cache, middle, act), (0, 1, 2), weight, stride, None, k)
        lo = k * stride
        right = keep_right * row_ok[k - 1] if k > 0 else jnp.float32(0.0)
        left = keep_left * row_ok[k] if k < n_out else jnp.float32(0.0)
        keep = jnp.where(t == 0, right, jnp.where(t == B - 1, left, 0.0))
        v = shifted(summed, lo, lo + B) + bias[...]
        out[lo : lo + B, :] = jnp.where(keep > 0.0, silu(v), 0.0).astype(BF)
        if k < n_out:
            v = silu(shifted(summed, lo + B, lo + stride) + bias[...])
            if k in (0, n_out - 1):
                v = jnp.where(row_ok[k] > 0.0, v, 0.0)
            out[lo + B : lo + stride, :] = v.astype(BF)
    out[n_out * stride + B :, :] = jnp.zeros((B, 128), BF)

    @pl.when(frm == 0)
    def _():
        send[...] = out[...]

    @pl.when(frm != 0)
    def _():
        send[...] = two_frame[...]


def conv_two_kernel(cache, act, middle, weight, bias, proj, out, summed):
    n_out, cols, _ = out.shape
    ccols = proj.shape[1]
    stride = cols + B
    spread = (
        lax.broadcasted_iota(jnp.int32, (cols, ccols), 0) // 2 == lax.broadcasted_iota(jnp.int32, (cols, ccols), 1)
    ).astype(F32).astype(BF)
    for k in range(n_out):
        if k % 4 == 0:
            wide = jnp.dot(spread, jnp.concatenate([proj[k // 2], proj[k // 2 + 1]], axis=1), preferred_element_type=F32)
        taps_into(summed, (cache, middle, act), (0, 1, 2), weight, stride, None, k)
        lo = k * stride
        h = (k % 4) // 2
        v = shifted(summed, lo + B, lo + stride) + bias[...] + wide[:, h * 128 : (h + 1) * 128]
        out[k] = v.astype(BF)


def shift(x, axis, step):
    n = lax.axis_size(axis)
    return lax.ppermute(x, axis, [(i, i + step) for i in range(n) if 0 <= i + step < n])


def swap(x):
    return lax.ppermute(x, "frm", [(0, 1), (1, 0)])


def per_device(latent, proj_weight, proj_bias, cache_one, cache_two, conv_one, bias_one, conv_two, bias_two):
    latent, one, two = latent[0], cache_one[0], cache_two[0]
    rows, cols, ch = one.shape
    crows, ccols, _ = latent.shape
    stride = cols + B
    place = jnp.stack(
        [
            lax.axis_index("frm"),
            lax.axis_index("row"),
            jnp.int32(lax.axis_size("row")),
            lax.axis_index("col"),
            jnp.int32(lax.axis_size("col")),
        ]
    ).astype(jnp.int32)
    n_edge = (2 * rows + crows) * B
    proj, act, row_up, row_dn, col_lf, col_rt, two_up, two_dn = call(
        first_kernel,
        [
            ((crows, ccols, ch), BF),
            ((crows, ccols, ch), BF),
            ((2 * cols + ccols, ch), BF),
            ((2 * cols + ccols, ch), BF),
            ((n_edge, ch), BF),
            ((n_edge, ch), BF),
            ((cols, ch), BF),
            ((cols, ch), BF),
        ],
        n_in=5,
        flops=10**8,
        nbytes=2 * 10**6,
        name="first",
    )(latent, proj_weight, proj_bias.reshape(1, ch), one, two)
    from_right = shift(col_lf, "col", -1)
    from_left = shift(col_rt, "col", 1)
    row_b = shift(row_up, "row", -1)
    row_a = shift(row_dn, "row", 1)
    merged, cor_up, cor_dn = call(
        functools.partial(corner_kernel, rows, crows),
        [((n_edge, ch), BF), ((4 * B, ch), BF), ((4 * B, ch), BF)],
        n_in=2,
        flops=10**6,
        nbytes=2 * 10**5,
        name="corner",
    )(from_right, from_left)
    cor_b = shift(cor_up, "row", -1)
    cor_a = shift(cor_dn, "row", 1)
    two_b = shift(two_up, "row", -1)
    two_a = shift(two_dn, "row", 1)
    long_one = 2 * B + (rows + 4) * stride
    long_two = 2 * B + (rows + 2) * stride
    cache_frame, act_frame, send = call(
        second_kernel,
        [((long_one, ch), BF)] * 3,
        n_in=8,
        smem_first=True,
        flops=10**8,
        nbytes=4 * 10**6,
        name="frames",
    )(place, one, act, merged, row_a, row_b, cor_a, cor_b)
    middle = swap(send)
    (two_frame,) = call(
        functools.partial(second_cache_kernel, first=rows + crows),
        [((long_two, ch), BF)],
        n_in=6,
        flops=10**7,
        nbytes=2 * 10**6,
        name="frames_two",
    )(two, merged, two_a, two_b, cor_a, cor_b)
    conv_flops = 2 * 27 * ch * ch * rows * cols
    n_one = rows + 2
    act_two, send_two = call(
        functools.partial(conv_one_kernel, cols=cols, n_out=n_one),
        [((long_two, ch), BF)] * 2,
        scratch=[pltpu.VMEM((8 + B + n_one * stride + B + 8, 3 * ch), F32)],
        n_in=7,
        smem_first=True,
        flops=conv_flops,
        nbytes=6 * 10**6,
        name="conv_one",
    )(place, cache_frame, act_frame, middle, conv_one, bias_one.reshape(1, ch), two_frame)
    middle_two = swap(send_two)
    (decoded,) = call(
        conv_two_kernel,
        [((rows, cols, ch), BF)],
        scratch=[pltpu.VMEM((8 + B + rows * stride + 8, 3 * ch), F32)],
        n_in=6,
        flops=conv_flops,
        nbytes=6 * 10**6,
        name="conv_two",
    )(two_frame, act_two, middle_two, conv_two, bias_two.reshape(1, ch), proj)
    return decoded[None]


def solution(mesh):
    placed = (
        P(("grp", "frm"), "row", "col", None),
        P(),
        P(),
        P(("grp", "frm"), "row", "col", None),
        P(("grp", "frm"), "row", "col", None),
        P(),
        P(),
        P(),
        P(),
    )
    return jax.shard_map(
        per_device,
        mesh=mesh,
        in_specs=placed,
        out_specs=P(("grp", "frm"), "row", "col", None),
        check_vma=False,
    )
```

time: 108 us -> 94.7 us (0.88)
  matrix products: 13.4 us -> 0 us
  Pallas kernels: 0 us -> 11.3 us
  other arithmetic: 8.4 us -> 0 us
  local copies, waits for them, and re-layouts: 8.16 us -> 6.04 us
  starting transfers between devices: 66.8 us -> 64.7 us
  waiting for transfers between devices: 10.1 us -> 11.9 us
    dot_general x19 -> x0, matrix products: 13.4 us -> none  [the longest x18 12.3 us: causal_conv(): jnp.dot(stencil, folded[frame_step, row_step], preferred_element_type=jnp...]
    pallas_call x0 -> x6, Pallas kernels: none -> 11.3 us  [the longest x1 5.29 us: per_device(): call(functools.partial(conv_one_kernel, cols=cols, n_out=n_one), [((long_...]
    slice x5 -> x0, local copies, waits for them, and re-layouts: 5.26 us -> none  [causal_conv(): padded[frame_step, row_step:row_step + tile_rows, col_step:col_step + til...]
    concatenate x6 -> x0, other arithmetic: 5.23 us -> none  [padded_2(): jnp.concatenate([lax.ppermute(tail, axis, [(i, (i + 1) % count) for i in...]
    unnamed x18 -> x22, local copies, waits for them, and re-layouts: 2.4 us -> 5.95 us
    convert_element_type x4 -> x0, other arithmetic: 2.91 us -> none  [the longest x2 1.54 us: per_device(): act_one = jax.nn.silu(upsampled.astype(jnp.float32)).astype(jnp.bfloat16)]
    ppermute x10, starting transfers between devices: 66.8 us -> 64.7 us  [the longest x2 43.3 us: swap(): return lax.ppermute(x, 'frm', [(0, 1), (1, 0)])]
    ppermute x10, waiting for transfers between devices: 10.1 us -> 11.9 us  [the longest x8 9.93 us: shift(): lax.ppermute(x, axis, [(i, i + step) for i in range(n) if 0 <= i + step <...]
  transfers between devices with their start and end apart: 10 -> 10, of which waited for: 5 -> 5; matrix products, arithmetic and copies ran while one was open for 8% -> 0% of each run, Pallas kernels for 0% -> 0%
where the time goes in v1:
time: 94.7 us; the launch traced here: 94.2 us
  starting transfers between devices  64.7 us (68%)
  waiting for transfers between devices  11.9 us (13%)
  Pallas kernels  11.3 us (12%)
  local copies, waits for them, and re-layouts  6.04 us (6%)
    ppermute x2, starting transfers between devices, swap(): return lax.ppermute(x, 'frm', [(0, 1), (1, 0)])  43.3 us
    ppermute x8, starting transfers between devices, shift(): lax.ppermute(x, axis, [(i, i + step) for i in range(n) if 0 <= i + step <...  21.4 us
    ppermute x8, waiting for transfers between devices, shift(): lax.ppermute(x, axis, [(i, i + step) for i in range(n) if 0 <= i + step <...  9.93 us
    unnamed x22, local copies, waits for them, and re-layouts  5.95 us
    pallas_call x1, Pallas kernels, per_device(): call(functools.partial(conv_one_kernel, cols=cols, n_out=n_one), [((long_...  5.29 us
    pallas_call x1, Pallas kernels, per_device(): call(conv_two_kernel, [((rows, cols, ch), BF)], scratch=[pltpu.VMEM((8 +...  4.72 us
    ppermute x2, waiting for transfers between devices, swap(): return lax.ppermute(x, 'frm', [(0, 1), (1, 0)])  2.01 us
  transfers between devices with their start and end apart: 10, of which 5 were waited for; matrix products, arithmetic and copies ran while one was open for 0% of the time, Pallas kernels for 0%

profile of v1, /device:TPU:33, one launch (start us, length us, event | category | flops | bytes accessed | tf_op | source)
XLA Modules:
  0.0 94.2 jit_solution(9676481033901509206)
XLA Ops:
  0.0 0.7 copy-done.6
  0.7 1.1 %copy-done = bf16[1,8,320,128]{3,2,1,0:T(8,128)(2,1)S(1)} copy-done((bf16[1,8,320,128]{3,2,1,0:T(8,128)(2,1)S(1)}, bf16[1,8,320,128]{3,2,1,0:T(8,128)(2,1)}, u32[]{:S(2)}) %copy-start) | copy-done | bytes 655384
  1.7 1.1 %copy-done.2 = bf16[1,8,320,128]{3,2,1,0:T(8,128)(2,1)S(1)} copy-done((bf16[1,8,320,128]{3,2,1,0:T(8,128)(2,1)S(1)}, bf16[1,8,320,128]{3,2,1,0:T(8,128)(2,1)}, u32[]{:S(2)}) %copy-start.2) | copy-done | bytes 655384
  2.8 1.0 %copy-done.4 = bf16[1,4,160,256]{3,2,1,0:T(8,128)(2,1)S(1)} copy-done((bf16[1,4,160,256]{3,2,1,0:T(8,128)(2,1)S(1)}, bf16[1,4,160,256]{3,2,1,0:T(8,128)(2,1)}, u32[]{:S(2)}) %copy-start.4) | copy-done | bytes 327704
  3.8 0.8 copy-done.5
  4.6 0.3 first.1
  4.9 5.3 %collective-permute-start.6 = (bf16[800,128]{1,0:T(8,128)(2,1)S(1)}, bf16[800,128]{1,0:T(8,128)(2,1)S(1)}, u32[]{:S(2)}, u32[]{:S(2)}) collective-permute-start(bf16[800,128]{1,0:T(8,128)(2,1)S(1)} %get-tuple-element.29), channel_id=1, source_target_pairs={{0,8},{8,16},{16,24},{24,32},{32,40},{40,48},{48,56},{56,64},{64,7... | collective-permute-start | bytes 614408 | tf_op jit(solution)/shard_map/ppermute | solution.py:228
  10.2 1.3 %collective-permute-start.7 = (bf16[800,128]{1,0:T(8,128)(2,1)S(1)}, bf16[800,128]{1,0:T(8,128)(2,1)S(1)}, u32[]{:S(2)}, u32[]{:S(2)}) collective-permute-start(bf16[800,128]{1,0:T(8,128)(2,1)S(1)} %get-tuple-element.30), channel_id=1, source_target_pairs={{8,0},{16,8},{24,16},{32,24},{40,32},{48,40},{56,48},{64,56},{72,6... | collective-permute-start | bytes 614408 | tf_op jit(solution)/shard_map/ppermute | solution.py:228
  11.5 1.3 %collective-permute-start = (bf16[320,128]{1,0:T(8,128)(2,1)S(1)}, bf16[320,128]{1,0:T(8,128)(2,1)S(1)}, u32[]{:S(2)}, u32[]{:S(2)}) collective-permute-start(bf16[320,128]{1,0:T(8,128)(2,1)S(1)} %get-tuple-element.21), channel_id=1, source_target_pairs={{2,0},{4,2},{6,4},{3,1},{5,3},{7,5},{10,8},{12,10},{14,12},{11,9},... | collective-permute-start | bytes 245768 | tf_op jit(solution)/shard_map/ppermute | solution.py:228
  12.8 4.0 %collective-permute-start.1 = (bf16[320,128]{1,0:T(8,128)(2,1)S(1)}, bf16[320,128]{1,0:T(8,128)(2,1)S(1)}, u32[]{:S(2)}, u32[]{:S(2)}) collective-permute-start(bf16[320,128]{1,0:T(8,128)(2,1)S(1)} %get-tuple-element.22), channel_id=1, source_target_pairs={{0,2},{2,4},{4,6},{1,3},{3,5},{5,7},{8,10},{10,12},{12,14},{9,11},... | collective-permute-start | bytes 245768 | tf_op jit(solution)/shard_map/ppermute | solution.py:228
  16.9 0.0 collective-permute-done.from_right
  16.9 1.5 %collective-permute-done.1.from_left = bf16[320,128]{1,0:T(8,128)(2,1)S(1)} collective-permute-done((bf16[320,128]{1,0:T(8,128)(2,1)S(1)}, bf16[320,128]{1,0:T(8,128)(2,1)S(1)}, u32[]{:S(2)}, u32[]{:S(2)}) %collective-permute-start.1) | collective-permute-done | bytes 81952 | tf_op jit(solution)/shard_map/ppermute | solution.py:228
  18.4 5.1 %collective-permute-start.4 = (bf16[64,128]{1,0:T(8,128)(2,1)S(1)}, bf16[64,128]{1,0:T(8,128)(2,1)S(1)}, u32[]{:S(2)}, u32[]{:S(2)}) collective-permute-start(bf16[64,128]{1,0:T(8,128)(2,1)S(1)} %get-tuple-element.26), channel_id=1, source_target_pairs={{0,8},{8,16},{16,24},{24,32},{32,40},{40,48},{48,56},{56,64},{64,7... | collective-permute-start | bytes 49160 | tf_op jit(solution)/shard_map/ppermute | solution.py:228
  23.4 1.3 %collective-permute-start.5 = (bf16[64,128]{1,0:T(8,128)(2,1)S(1)}, bf16[64,128]{1,0:T(8,128)(2,1)S(1)}, u32[]{:S(2)}, u32[]{:S(2)}) collective-permute-start(bf16[64,128]{1,0:T(8,128)(2,1)S(1)} %get-tuple-element.27), channel_id=1, source_target_pairs={{8,0},{16,8},{24,16},{32,24},{40,32},{48,40},{56,48},{64,56},{72,6... | collective-permute-start | bytes 49160 | tf_op jit(solution)/shard_map/ppermute | solution.py:228
  24.8 0.1 stack.15.where_ref
  24.8 4.1 %collective-permute-done.5.cor_b = bf16[64,128]{1,0:T(8,128)(2,1)S(1)} collective-permute-done((bf16[64,128]{1,0:T(8,128)(2,1)S(1)}, bf16[64,128]{1,0:T(8,128)(2,1)S(1)}, u32[]{:S(2)}, u32[]{:S(2)}) %collective-permute-start.5) | collective-permute-done | bytes 16416 | tf_op jit(solution)/shard_map/ppermute | solution.py:228
  29.0 0.0 copy-start.1
  29.0 1.0 %frames.1 = (bf16[4064,128]{1,0:T(8,128)(2,1)S(1)}, bf16[4064,128]{1,0:T(8,128)(2,1)S(1)}, bf16[4064,128]{1,0:T(8,128)(2,1)S(1)}) custom-call(s32[5]{0:T(128)S(1)} %stack.15.where_ref, bf16[8,320,128]{2,1,0:T(8,128)(2,1)S(1)} %bitcast.13, bf16[4,160,128]{2,1,0:T(8,128)(2,1)S(1)} %get-tuple-element.28.act, bf16[320,128]{1,0:T(8,128)(2,1)S(1)} %get-tuple-element.23.merged, ...), custom_call_target="tpu_custom_call" | custom-call | flops 100000000 | bytes 4000000 | tf_op jit(solution)/shard_map/frames/pallas_call | solution.py:285
  30.0 40.2 %collective-permute-start.8 = (bf16[4064,128]{1,0:T(8,128)(2,1)S(1)}, bf16[4064,128]{1,0:T(8,128)(2,1)S(1)}, u32[]{:S(2)}, u32[]{:S(2)}) collective-permute-start(bf16[4064,128]{1,0:T(8,128)(2,1)S(1)} %get-tuple-element.33), channel_id=1, source_target_pairs={{0,1},{1,0},{2,3},{3,2},{4,5},{5,4},{6,7},{7,6},{8,9},{9,8},{10,11... | collective-permute-start | bytes 3121160 | tf_op jit(solution)/shard_map/ppermute | solution.py:232
  70.2 1.7 %collective-permute-start.2 = (bf16[320,128]{1,0:T(8,128)(2,1)S(1)}, bf16[320,128]{1,0:T(8,128)(2,1)S(1)}, u32[]{:S(2)}, u32[]{:S(2)}) collective-permute-start(bf16[320,128]{1,0:T(8,128)(2,1)S(1)} %get-tuple-element.24), channel_id=1, source_target_pairs={{0,8},{8,16},{16,24},{24,32},{32,40},{40,48},{48,56},{56,64},{64,7... | collective-permute-start | bytes 245768 | tf_op jit(solution)/shard_map/ppermute | solution.py:228
  71.9 0.0 copy-start.7
  71.9 1.4 %collective-permute-start.3 = (bf16[320,128]{1,0:T(8,128)(2,1)S(1)}, bf16[320,128]{1,0:T(8,128)(2,1)S(1)}, u32[]{:S(2)}, u32[]{:S(2)}) collective-permute-start(bf16[320,128]{1,0:T(8,128)(2,1)S(1)} %get-tuple-element.25), channel_id=1, source_target_pairs={{8,0},{16,8},{24,16},{32,24},{40,32},{48,40},{56,48},{64,56},{72,6... | collective-permute-start | bytes 245768 | tf_op jit(solution)/shard_map/ppermute | solution.py:228
  73.3 0.3 collective-permute-done.2.two_a
  73.6 4.0 %collective-permute-done.3.two_b = bf16[320,128]{1,0:T(8,128)(2,1)S(1)} collective-permute-done((bf16[320,128]{1,0:T(8,128)(2,1)S(1)}, bf16[320,128]{1,0:T(8,128)(2,1)S(1)}, u32[]{:S(2)}, u32[]{:S(2)}) %collective-permute-start.3) | collective-permute-done | bytes 81952 | tf_op jit(solution)/shard_map/ppermute | solution.py:228
  77.6 0.1 frames_two.1.two_frame.cache
  77.7 0.0 copy-start.9
  77.7 0.6 copy-done.9
  78.4 5.3 %conv_one.1 = (bf16[3392,128]{1,0:T(8,128)(2,1)S(1)}, bf16[3392,128]{1,0:T(8,128)(2,1)S(1)}) custom-call(s32[5]{0:T(128)S(1)} %stack.15.where_ref, bf16[4064,128]{1,0:T(8,128)(2,1)S(1)} %get-tuple-element.31.cache, bf16[4064,128]{1,0:T(8,128)(2,1)S(1)} %get-tuple-element.32.act, bf16[4064,128]{1,0:T(8,128)(2,1)S(1)} %collective-permute-done.8.middle, ...), custom_call_target="tpu_custom_call" | custom-call | flops 2264924160 | bytes 6000000 | tf_op jit(solution)/shard_map/conv_one/pallas_call | solution.py:305
  83.7 3.1 %collective-permute-start.9 = (bf16[3392,128]{1,0:T(8,128)(2,1)S(1)}, bf16[3392,128]{1,0:T(8,128)(2,1)S(1)}, u32[]{:S(2)}, u32[]{:S(2)}) collective-permute-start(bf16[3392,128]{1,0:T(8,128)(2,1)S(1)} %get-tuple-element.35), channel_id=1, source_target_pairs={{0,1},{1,0},{2,3},{3,2},{4,5},{5,4},{6,7},{7,6},{8,9},{9,8},{10,11... | collective-permute-start | bytes 2605064 | tf_op jit(solution)/shard_map/ppermute | solution.py:232
  86.8 2.0 %collective-permute-done.9.middle = bf16[3392,128]{1,0:T(8,128)(2,1)S(1)} collective-permute-done((bf16[3392,128]{1,0:T(8,128)(2,1)S(1)}, bf16[3392,128]{1,0:T(8,128)(2,1)S(1)}, u32[]{:S(2)}, u32[]{:S(2)}) %collective-permute-start.9) | collective-permute-done | bytes 868384 | tf_op jit(solution)/shard_map/ppermute | solution.py:232
  88.8 0.7 copy-done.10
  89.4 4.7 %conv_two.1 = bf16[8,320,128]{2,1,0:T(8,128)(2,1)} custom-call(bf16[3392,128]{1,0:T(8,128)(2,1)S(1)} %frames_two.1.two_frame.cache, bf16[3392,128]{1,0:T(8,128)(2,1)S(1)} %get-tuple-element.34.act, bf16[3392,128]{1,0:T(8,128)(2,1)S(1)} %collective-permute-done.9.middle, bf16[3,3,3,128,128]{4,3,2,1,0:T(8,128)(2,1)S(1)} %copy-done.8, f32[1,128]{1,0:T(1,128)S(1)} %bitcast.17, ...), custom_call_target="tpu_custom_call" | custom-call | flops 2264924160 | bytes 6000000 | tf_op jit(solution)/shard_map/conv_two/pallas_call | solution.py:316
  (17 shorter events, 0.0 us)
Async XLA Ops:
  0.0 0.7 copy-start.6
  0.7 1.1 %copy-start = (bf16[1,8,320,128]{3,2,1,0:T(8,128)(2,1)S(1)}, bf16[1,8,320,128]{3,2,1,0:T(8,128)(2,1)}, u32[]{:S(2)}) copy-start(bf16[1,8,320,128]{3,2,1,0:T(8,128)(2,1)} %param.13) | copy-start | bytes 1966084
  1.7 1.1 %copy-start.2 = (bf16[1,8,320,128]{3,2,1,0:T(8,128)(2,1)S(1)}, bf16[1,8,320,128]{3,2,1,0:T(8,128)(2,1)}, u32[]{:S(2)}) copy-start(bf16[1,8,320,128]{3,2,1,0:T(8,128)(2,1)} %param.12) | copy-start | bytes 1966084
  2.8 1.0 %copy-start.4 = (bf16[1,4,160,256]{3,2,1,0:T(8,128)(2,1)S(1)}, bf16[1,4,160,256]{3,2,1,0:T(8,128)(2,1)}, u32[]{:S(2)}) copy-start(bf16[1,4,160,256]{3,2,1,0:T(8,128)(2,1)} %param.9) | copy-start | bytes 983044
  3.8 0.8 copy-start.5
  4.6 24.4 %copy-start.3 = (bf16[1,8,320,128]{3,2,1,0:T(8,128)(2,1)S(1)}, bf16[1,8,320,128]{3,2,1,0:T(8,128)(2,1)}, u32[]{:S(2)}) copy-start(bf16[1,8,320,128]{3,2,1,0:T(8,128)(2,1)} %param.12) | copy-start | bytes 1966084
  4.9 24.1 %collective-permute-start.6 = (bf16[800,128]{1,0:T(8,128)(2,1)S(1)}, bf16[800,128]{1,0:T(8,128)(2,1)S(1)}, u32[]{:S(2)}, u32[]{:S(2)}) collective-permute-start(bf16[800,128]{1,0:T(8,128)(2,1)S(1)} %get-tuple-element.29), channel_id=1, source_target_pairs={{0,8},{8,16},{16,24},{24,32},{32,40},{40,48},{48,56},{56,64},{64,7... | collective-permute-start | bytes 614408 | tf_op jit(solution)/shard_map/ppermute | solution.py:228
  10.2 18.8 %collective-permute-start.7 = (bf16[800,128]{1,0:T(8,128)(2,1)S(1)}, bf16[800,128]{1,0:T(8,128)(2,1)S(1)}, u32[]{:S(2)}, u32[]{:S(2)}) collective-permute-start(bf16[800,128]{1,0:T(8,128)(2,1)S(1)} %get-tuple-element.30), channel_id=1, source_target_pairs={{8,0},{16,8},{24,16},{32,24},{40,32},{48,40},{56,48},{64,56},{72,6... | collective-permute-start | bytes 614408 | tf_op jit(solution)/shard_map/ppermute | solution.py:228
  11.5 5.4 %collective-permute-start = (bf16[320,128]{1,0:T(8,128)(2,1)S(1)}, bf16[320,128]{1,0:T(8,128)(2,1)S(1)}, u32[]{:S(2)}, u32[]{:S(2)}) collective-permute-start(bf16[320,128]{1,0:T(8,128)(2,1)S(1)} %get-tuple-element.21), channel_id=1, source_target_pairs={{2,0},{4,2},{6,4},{3,1},{5,3},{7,5},{10,8},{12,10},{14,12},{11,9},... | collective-permute-start | bytes 245768 | tf_op jit(solution)/shard_map/ppermute | solution.py:228
  12.8 5.5 %collective-permute-start.1 = (bf16[320,128]{1,0:T(8,128)(2,1)S(1)}, bf16[320,128]{1,0:T(8,128)(2,1)S(1)}, u32[]{:S(2)}, u32[]{:S(2)}) collective-permute-start(bf16[320,128]{1,0:T(8,128)(2,1)S(1)} %get-tuple-element.22), channel_id=1, source_target_pairs={{0,2},{2,4},{4,6},{1,3},{3,5},{5,7},{8,10},{10,12},{12,14},{9,11},... | collective-permute-start | bytes 245768 | tf_op jit(solution)/shard_map/ppermute | solution.py:228
  18.4 6.5 %collective-permute-start.4 = (bf16[64,128]{1,0:T(8,128)(2,1)S(1)}, bf16[64,128]{1,0:T(8,128)(2,1)S(1)}, u32[]{:S(2)}, u32[]{:S(2)}) collective-permute-start(bf16[64,128]{1,0:T(8,128)(2,1)S(1)} %get-tuple-element.26), channel_id=1, source_target_pairs={{0,8},{8,16},{16,24},{24,32},{32,40},{40,48},{48,56},{56,64},{64,7... | collective-permute-start | bytes 49160 | tf_op jit(solution)/shard_map/ppermute | solution.py:228
  23.4 5.6 %collective-permute-start.5 = (bf16[64,128]{1,0:T(8,128)(2,1)S(1)}, bf16[64,128]{1,0:T(8,128)(2,1)S(1)}, u32[]{:S(2)}, u32[]{:S(2)}) collective-permute-start(bf16[64,128]{1,0:T(8,128)(2,1)S(1)} %get-tuple-element.27), channel_id=1, source_target_pairs={{8,0},{16,8},{24,16},{32,24},{40,32},{48,40},{56,48},{64,56},{72,6... | collective-permute-start | bytes 49160 | tf_op jit(solution)/shard_map/ppermute | solution.py:228
  29.0 48.6 %copy-start.1 = (bf16[1,8,320,128]{3,2,1,0:T(8,128)(2,1)S(1)}, bf16[1,8,320,128]{3,2,1,0:T(8,128)(2,1)}, u32[]{:S(2)}) copy-start(bf16[1,8,320,128]{3,2,1,0:T(8,128)(2,1)} %param.13) | copy-start | bytes 1966084
  30.0 47.7 %collective-permute-start.8 = (bf16[4064,128]{1,0:T(8,128)(2,1)S(1)}, bf16[4064,128]{1,0:T(8,128)(2,1)S(1)}, u32[]{:S(2)}, u32[]{:S(2)}) collective-permute-start(bf16[4064,128]{1,0:T(8,128)(2,1)S(1)} %get-tuple-element.33), channel_id=1, source_target_pairs={{0,1},{1,0},{2,3},{3,2},{4,5},{5,4},{6,7},{7,6},{8,9},{9,8},{10,11... | collective-permute-start | bytes 3121160 | tf_op jit(solution)/shard_map/ppermute | solution.py:232
  70.2 3.5 %collective-permute-start.2 = (bf16[320,128]{1,0:T(8,128)(2,1)S(1)}, bf16[320,128]{1,0:T(8,128)(2,1)S(1)}, u32[]{:S(2)}, u32[]{:S(2)}) collective-permute-start(bf16[320,128]{1,0:T(8,128)(2,1)S(1)} %get-tuple-element.24), channel_id=1, source_target_pairs={{0,8},{8,16},{16,24},{24,32},{32,40},{40,48},{48,56},{56,64},{64,7... | collective-permute-start | bytes 245768 | tf_op jit(solution)/shard_map/ppermute | solution.py:228
  71.9 5.9 %copy-start.7 = (bf16[3,3,3,128,128]{4,3,2,1,0:T(8,128)(2,1)S(1)}, bf16[3,3,3,128,128]{4,3,2,1,0:T(8,128)(2,1)}, u32[]{:S(2)}) copy-start(bf16[3,3,3,128,128]{4,3,2,1,0:T(8,128)(2,1)} %weight.4) | copy-start | bytes 2654212
  71.9 5.8 %collective-permute-start.3 = (bf16[320,128]{1,0:T(8,128)(2,1)S(1)}, bf16[320,128]{1,0:T(8,128)(2,1)S(1)}, u32[]{:S(2)}, u32[]{:S(2)}) collective-permute-start(bf16[320,128]{1,0:T(8,128)(2,1)S(1)} %get-tuple-element.25), channel_id=1, source_target_pairs={{8,0},{16,8},{24,16},{32,24},{40,32},{48,40},{56,48},{64,56},{72,6... | collective-permute-start | bytes 245768 | tf_op jit(solution)/shard_map/ppermute | solution.py:228
  77.7 0.7 copy-start.9
  78.4 10.4 %copy-start.8 = (bf16[3,3,3,128,128]{4,3,2,1,0:T(8,128)(2,1)S(1)}, bf16[3,3,3,128,128]{4,3,2,1,0:T(8,128)(2,1)}, u32[]{:S(2)}) copy-start(bf16[3,3,3,128,128]{4,3,2,1,0:T(8,128)(2,1)} %weight.5) | copy-start | bytes 2654212
  83.7 5.1 %collective-permute-start.9 = (bf16[3392,128]{1,0:T(8,128)(2,1)S(1)}, bf16[3392,128]{1,0:T(8,128)(2,1)S(1)}, u32[]{:S(2)}, u32[]{:S(2)}) collective-permute-start(bf16[3392,128]{1,0:T(8,128)(2,1)S(1)} %get-tuple-element.35), channel_id=1, source_target_pairs={{0,1},{1,0},{2,3},{3,2},{4,5},{5,4},{6,7},{7,6},{8,9},{9,8},{10,11... | collective-permute-start | bytes 2605064 | tf_op jit(solution)/shard_map/ppermute | solution.py:232
  88.8 0.7 copy-start.10

commit v2 on v0

v2 whole, which is shorter than its diff:
```python
import functools

import jax
import jax.numpy as jnp
from jax import lax
from jax.experimental import pallas as pl
from jax.experimental.pallas import tpu as pltpu
from jax.sharding import PartitionSpec as P

B = 16
BF = jnp.bfloat16
F32 = jnp.float32
VMEM = pl.BlockSpec(memory_space=pltpu.VMEM)
SMEM = pl.BlockSpec(memory_space=pltpu.SMEM)
HBM = pl.BlockSpec(memory_space=pltpu.HBM)


def call(body, outs, specs, scratch=(), flops=0, nbytes=0, limit=24):
    run = pl.pallas_call(
        body,
        out_shape=[jax.ShapeDtypeStruct(s, d) for s, d in outs],
        in_specs=specs,
        out_specs=[VMEM] * len(outs),
        scratch_shapes=list(scratch),
        cost_estimate=pl.CostEstimate(flops=flops, bytes_accessed=nbytes, transcendentals=0),
        compiler_params=pltpu.CompilerParams(vmem_limit_bytes=int(limit * 1024 * 1024)),
    )
    held = lambda v, spec: pltpu.with_memory_space_constraint(v, pltpu.HBM) if spec is HBM else v
    return lambda *args: run(*(held(v, spec) for v, spec in zip(args, specs, strict=True)))


def silu(v):
    return v / (1.0 + jnp.exp(-v))


def low_half():
    return lax.broadcasted_iota(jnp.int32, (B, 128), 0) < B // 2


def spread_matrix(cols, ccols):
    fine = lax.broadcasted_iota(jnp.int32, (cols, ccols), 0)
    return (fine // 2 == lax.broadcasted_iota(jnp.int32, (cols, ccols), 1)).astype(F32).astype(BF)


def first_kernel(
    latent, weight, bias, one, two, bias_one, bias_two,
    proj, act, row_up, row_dn, col_lf, col_rt, b_one, b_two,
    latent_v, weight_v, bias_v, sems,
):
    rows, cols, _ = one.shape
    crows, ccols, _ = latent.shape
    copies = [(latent, latent_v), (weight, weight_v), (bias, bias_v)]
    n_first = len(copies)
    n_c1 = rows * B
    n_c2 = (rows + crows) * B
    for i in range(rows):
        copies.append((one.at[i, 0:B], col_lf.at[i * B : (i + 1) * B]))
        copies.append((one.at[i, cols - B : cols], col_rt.at[i * B : (i + 1) * B]))
        copies.append((two.at[i, 0:B], col_lf.at[n_c2 + i * B : n_c2 + (i + 1) * B]))
        copies.append((two.at[i, cols - B : cols], col_rt.at[n_c2 + i * B : n_c2 + (i + 1) * B]))
    t0 = 2 * cols + ccols
    for k in range(2):
        copies.append((one.at[k], row_up.at[k * cols : (k + 1) * cols]))
        copies.append((one.at[rows - 2 + k], row_dn.at[k * cols : (k + 1) * cols]))
    copies.append((two.at[0], row_up.at[t0 : t0 + cols]))
    copies.append((two.at[rows - 1], row_dn.at[t0 : t0 + cols]))
    copies.append((bias_one, b_one))
    copies.append((bias_two, b_two))
    started = [pltpu.make_async_copy(s, d, sems.at[i]) for i, (s, d) in enumerate(copies)]
    for c in started:
        c.start()
    for c in started[:n_first]:
        c.wait()
    for i in range(crows):
        p = (jnp.dot(latent_v[i], weight_v[...], preferred_element_type=F32) + bias_v[...]).astype(BF)
        proj[i] = p
        a = silu(p.astype(F32)).astype(BF)
        act[i] = a
        if i == 0:
            row_up[2 * cols : t0, :] = a
        if i == crows - 1:
            row_dn[2 * cols : t0, :] = a
        o = n_c1 + i * B
        col_lf[o : o + B, :] = a[:B]
        col_rt[o : o + B, :] = a[ccols - B :]
    for c in started[n_first:]:
        c.wait()


def corner_kernel(rows, crows, from_right, from_left, merged, up, dn):
    low = low_half()
    picks_up = (0, 1, rows, rows + crows)
    picks_dn = (rows - 2, rows - 1, rows + crows - 1, 2 * rows + crows - 1)
    for i in range(2 * rows + crows):
        s = slice(i * B, (i + 1) * B)
        b = jnp.where(low, from_right[s, :].astype(F32), from_left[s, :].astype(F32)).astype(BF)
        merged[s, :] = b
        for dst, picks in ((up, picks_up), (dn, picks_dn)):
            if i in picks:
                k = picks.index(i)
                dst[k * B : (k + 1) * B, :] = b


def block(ref, i):
    return ref[i * B : (i + 1) * B, :].astype(F32)


def spread_edge(m):
    return jnp.where(
        low_half(), jnp.broadcast_to(m[0:1], (B, 128)), jnp.broadcast_to(m[B - 1 : B], (B, 128))
    ).astype(BF)


def put_row(dst, i, inside, edges):
    cols = dst.shape[1] - 2 * B
    dst[i, 0:B, :] = edges
    dst[i, B : B + cols, :] = inside
    dst[i, B + cols :, :] = edges


def conv_rows(frames, steps, weight, k, sums, slot):
    span = sums.shape[1] - 16
    w01, w2 = [], []
    zero = jnp.zeros(weight.shape[3:], BF)
    for a in steps:
        for p in range(4):
            if p < 3:
                w01.append(jnp.concatenate([weight[a, p, 0], weight[a, p, 1]], axis=1))
            w2.append(jnp.concatenate([weight[a, p, 2] if p < 3 else zero, weight[a, p - 1, 2] if p else zero], axis=1))
    w01, w2 = jnp.concatenate(w01, axis=0), jnp.concatenate(w2, axis=0)
    lhs = jnp.concatenate([f(k + p) for f in frames for p in range(4)], axis=1)
    y2 = jnp.dot(lhs, w2, preferred_element_type=F32)
    results = []
    for h in range(2):
        lhs = jnp.concatenate([f(k + h + p) for f in frames for p in range(3)], axis=1)
        y01 = jnp.dot(lhs, w01, preferred_element_type=F32)
        s = 2 * slot + h
        sums[s, 8 : 8 + span, 0:128] = y01[:, 0:128]
        sums[s, 8 : 8 + span, 128:256] = y2[:, h * 128 : (h + 1) * 128]
        results.append(sums[s, 7 : 7 + span, 0:128] + y01[:, 128:256] + sums[s, 9 : 9 + span, 128:256])
    return results


def joined(core, border):
    n = core.shape[0]
    return lambda i: border[i] if i < 2 else core[i - 2] if i < n + 2 else border[i - n]


def inner_kernel(one, act, merged, weight, cache_core, act_core, part, sums):
    rows, cols, _ = one.shape
    crows, ccols, _ = act.shape
    for i in range(rows):
        put_row(cache_core, i, one[i], merged[i * B : (i + 1) * B, :])
    spread = spread_matrix(cols, ccols)
    for m in range(0, crows, 2):
        wide = jnp.dot(spread, jnp.concatenate([act[m], act[m + 1]], axis=1), preferred_element_type=F32).astype(BF)
        for h in range(2):
            edges = spread_edge(block(merged, rows + m + h))
            for i in range(2):
                put_row(act_core, 2 * (m + h) + i, wide[:, h * 128 : (h + 1) * 128], edges)
    frames = (lambda i: cache_core[i - 2], lambda i: act_core[i - 2])
    for n, k in enumerate(range(2, rows, 2)):
        for h, v in enumerate(conv_rows(frames, (0, 2), weight, k, sums, n % 2)):
            part[k - 2 + h] = v


def border_kernel(where_ref, row_a, row_b, cor_a, cor_b, cache_core, act_core, cache_border, act_border, send):
    rows, span, _ = cache_core.shape
    cols = span - 2 * B
    ccols = row_a.shape[0] - 3 * cols
    coarse = jnp.concatenate([row_a[2 * cols : 2 * cols + ccols, :], row_b[2 * cols : 2 * cols + ccols, :]], axis=1)
    wide = jnp.dot(spread_matrix(cols, ccols), coarse, preferred_element_type=F32).astype(BF)
    for h, (row, cor) in enumerate(((row_a, cor_a), (row_b, cor_b))):
        edges = spread_edge(block(cor, 2))
        for k in range(2):
            put_row(cache_border, 2 * h + k, row[k * cols : (k + 1) * cols, :], cor[k * B : (k + 1) * B, :])
            put_row(act_border, 2 * h + k, wide[:, h * 128 : (h + 1) * 128], edges)
    for lead, core, border in ((True, act_core, act_border), (False, cache_core, cache_border)):

        @pl.when((where_ref[0] == 0) == lead)
        def _(core=core, border=border):
            send[0:2] = border[0:2]
            send[2 : rows + 2] = core[...]
            send[rows + 2 :] = border[2:4]


def outer_kernel(cache_core, act_core, cache_border, act_border, weight, two, merged, row_a, row_b, cor_a, cor_b, part, two_frame, sums, *, first):
    rows, cols, _ = two.shape
    frames = (joined(cache_core, cache_border), joined(act_core, act_border))
    for n, k in enumerate((0, rows)):
        for h, v in enumerate(conv_rows(frames, (0, 2), weight, k, sums, n)):
            part[2 * n + h] = v
    t0 = row_a.shape[0] - cols
    put_row(two_frame, 0, row_a[t0:, :], cor_a[3 * B :, :])
    for i in range(rows):
        put_row(two_frame, i + 1, two[i], merged[(first + i) * B : (first + i + 1) * B, :])
    put_row(two_frame, rows + 1, row_b[t0:, :], cor_b[3 * B :, :])


def middle_kernel(where_ref, middle, part_in, part_out, weight, bias, two_frame, out, send, sums):
    n_out, span, _ = out.shape
    frm, row, rows_n, col, cols_n = (where_ref[i] for i in range(5))
    t = lax.broadcasted_iota(jnp.int32, (B, 128), 0)
    keep_left = (t != B - 1) | (col != 0)
    keep_right = (t != 0) | (col != cols_n - 1)
    part = joined(part_in, part_out)
    for k in range(0, n_out, 2):
        for h, v in enumerate(conv_rows((lambda i: middle[i],), (1,), weight, k, sums, k // 2 % 2)):
            i = k + h
            v = silu(v + part(i) + bias[...])
            if i == 0:
                v = jnp.where(row != 0, v, 0.0)
            if i == n_out - 1:
                v = jnp.where(row != rows_n - 1, v, 0.0)
            out[i, 0:B, :] = jnp.where(keep_left, v[0:B], 0.0).astype(BF)
            out[i, B : span - B, :] = v[B : span - B].astype(BF)
            out[i, span - B :, :] = jnp.where(keep_right, v[span - B :], 0.0).astype(BF)

    @pl.when(frm == 0)
    def _():
        send[...] = out[...]

    @pl.when(frm != 0)
    def _():
        send[...] = two_frame[...]


def own_two_kernel(two_frame, act_two, weight, proj, bias, part, sums):
    n_out, cols, _ = part.shape
    spread = spread_matrix(cols, proj.shape[1])
    frames = (lambda i: two_frame[i], lambda i: act_two[i])
    for k in range(0, n_out, 2):
        if k % 4 == 0:
            wide = jnp.dot(spread, jnp.concatenate([proj[k // 2], proj[k // 2 + 1]], axis=1), preferred_element_type=F32)
        base = wide[:, k % 4 * 64 : k % 4 * 64 + 128] + bias[...]
        for h, v in enumerate(conv_rows(frames, (0, 2), weight, k, sums, k // 2 % 2)):
            part[k + h] = v[B : B + cols] + base


def middle_two_kernel(middle, part, weight, out, sums):
    n_out, cols, _ = out.shape
    for k in range(0, n_out, 2):
        for h, v in enumerate(conv_rows((lambda i: middle[i],), (1,), weight, k, sums, k // 2 % 2)):
            out[k + h] = (part[k + h] + v[B : B + cols]).astype(BF)


def shift(x, axis, step):
    n = lax.axis_size(axis)
    return lax.ppermute(x, axis, [(i, i + step) for i in range(n) if 0 <= i + step < n])


def swap(x):
    return lax.ppermute(x, "frm", [(0, 1), (1, 0)])


def program(latent, proj_weight, proj_bias, cache_one, cache_two, conv_one, bias_one, conv_two, bias_two):
    latent, one, two = latent[0], cache_one[0], cache_two[0]
    rows, cols, ch = one.shape
    crows, ccols, lch = latent.shape
    span = cols + 2 * B
    place = jnp.stack(
        [
            lax.axis_index("frm"),
            lax.axis_index("row"),
            jnp.int32(lax.axis_size("row")),
            lax.axis_index("col"),
            jnp.int32(lax.axis_size("col")),
        ]
    ).astype(jnp.int32)
    n_edge = (2 * rows + crows) * B
    n_row = 3 * cols + ccols
    sums = pltpu.VMEM((4, span + 16, 2 * ch), F32)
    proj, act, row_up, row_dn, col_lf, col_rt, b_one, b_two = call(
        first_kernel,
        [
            ((crows, ccols, ch), BF),
            ((crows, ccols, ch), BF),
            ((n_row, ch), BF),
            ((n_row, ch), BF),
            ((n_edge, ch), BF),
            ((n_edge, ch), BF),
            ((1, ch), F32),
            ((1, ch), F32),
        ],
        [HBM] * 7,
        scratch=[
            pltpu.VMEM((crows, ccols, lch), BF),
            pltpu.VMEM((lch, ch), BF),
            pltpu.VMEM((1, ch), F32),
            pltpu.SemaphoreType.DMA((3 + 4 * rows + 8,)),
        ],
        flops=10**8,
        nbytes=2 * 10**6,
        limit=24,
    )(latent, proj_weight, proj_bias.reshape(1, ch), one, two, bias_one.reshape(1, ch), bias_two.reshape(1, ch))
    from_left = shift(col_rt, "col", 1)
    from_right = shift(col_lf, "col", -1)
    row_a = shift(row_dn, "row", 1)
    row_b = shift(row_up, "row", -1)
    merged, cor_up, cor_dn = call(
        functools.partial(corner_kernel, rows, crows),
        [((n_edge, ch), BF), ((4 * B, ch), BF), ((4 * B, ch), BF)],
        [VMEM] * 2,
        flops=10**6,
        nbytes=2 * 10**5,
    )(from_right, from_left)
    cor_a = shift(cor_dn, "row", 1)
    cor_b = shift(cor_up, "row", -1)
    third = 2 * 9 * ch * ch * rows * cols
    cache_core, act_core, part_in = call(
        inner_kernel,
        [((rows, span, ch), BF), ((rows, span, ch), BF), ((rows - 2, span, ch), F32)],
        [VMEM] * 4,
        scratch=[sums],
        flops=2 * third,
        nbytes=4 * 10**6,
    )(one, act, merged, conv_one)
    cache_border, act_border, send = call(
        border_kernel,
        [((4, span, ch), BF), ((4, span, ch), BF), ((rows + 4, span, ch), BF)],
        [SMEM] + [VMEM] * 6,
        flops=10**8,
        nbytes=4 * 10**6,
    )(place, row_a, row_b, cor_a, cor_b, cache_core, act_core)
    middle = swap(send)
    part_out, two_frame = call(
        functools.partial(outer_kernel, first=rows + crows),
        [((4, span, ch), F32), ((rows + 2, span, ch), BF)],
        [VMEM] * 11,
        scratch=[sums],
        flops=third,
        nbytes=4 * 10**6,
    )(cache_core, act_core, cache_border, act_border, conv_one, two, merged, row_a, row_b, cor_a, cor_b)
    act_two, send_two = call(
        middle_kernel,
        [((rows + 2, span, ch), BF)] * 2,
        [SMEM] + [VMEM] * 6,
        scratch=[sums],
        flops=third,
        nbytes=6 * 10**6,
    )(place, middle, part_in, part_out, conv_one, b_one, two_frame)
    middle_two = swap(send_two)
    (part_two,) = call(
        own_two_kernel, [((rows, cols, ch), F32)], [VMEM] * 5, scratch=[sums], flops=2 * third, nbytes=6 * 10**6
    )(two_frame, act_two, conv_two, proj, b_two)
    (decoded,) = call(
        middle_two_kernel, [((rows, cols, ch), BF)], [VMEM] * 3, scratch=[sums], flops=third, nbytes=6 * 10**6
    )(middle_two, part_two, conv_two)
    return decoded[None]


def solution(mesh):
    placed = (
        P(("grp", "frm"), "row", "col", None),
        P(),
        P(),
        P(("grp", "frm"), "row", "col", None),
        P(("grp", "frm"), "row", "col", None),
        P(),
        P(),
        P(),
        P(),
    )
    return jax.shard_map(
        program,
        mesh=mesh,
        in_specs=placed,
        out_specs=P(("grp", "frm"), "row", "col", None),
        check_vma=False,
    )
```

time: 108 us -> 79 us (0.73)
  matrix products: 13.4 us -> 0 us
  Pallas kernels: 0 us -> 12.6 us
  other arithmetic: 8.4 us -> 0 us
  local copies, waits for them, and re-layouts: 8.16 us -> 0.1 us
  starting transfers between devices: 66.8 us -> 60.8 us
  waiting for transfers between devices: 10.1 us -> 5.01 us
    dot_general x19 -> x0, matrix products: 13.4 us -> none  [the longest x18 12.3 us: causal_conv(): jnp.dot(stencil, folded[frame_step, row_step], preferred_element_type=jnp...]
    pallas_call x0 -> x8, Pallas kernels: none -> 12.6 us  [call(): run(*(held(v, spec) for v, spec in zip(args, specs, strict=True)))]
    ppermute x10 -> x8, starting transfers between devices: 66.8 us -> 60.8 us  [the longest x2 42.5 us: swap(): return lax.ppermute(x, 'frm', [(0, 1), (1, 0)])]
    slice x5 -> x0, local copies, waits for them, and re-layouts: 5.26 us -> none  [causal_conv(): padded[frame_step, row_step:row_step + tile_rows, col_step:col_step + til...]
    concatenate x6 -> x0, other arithmetic: 5.23 us -> none  [padded_2(): jnp.concatenate([lax.ppermute(tail, axis, [(i, (i + 1) % count) for i in...]
    ppermute x10 -> x8, waiting for transfers between devices: 10.1 us -> 5.01 us  [the longest x6 3.84 us: shift(): lax.ppermute(x, axis, [(i, i + step) for i in range(n) if 0 <= i + step <...]
    convert_element_type x4 -> x0, other arithmetic: 2.91 us -> none  [the longest x2 1.54 us: per_device(): act_one = jax.nn.silu(upsampled.astype(jnp.float32)).astype(jnp.bfloat16)]
    unnamed x18 -> x8, local copies, waits for them, and re-layouts: 2.4 us -> 0.02 us
  transfers between devices with their start and end apart: 10 -> 8, of which waited for: 5 -> 3; matrix products, arithmetic and copies ran while one was open for 8% -> 0% of each run, Pallas kernels for 0% -> 6%
where the time goes in v2:
time: 79 us; the launch traced here: 78.7 us
  starting transfers between devices  60.8 us (77%)
  Pallas kernels  12.6 us (16%)
  waiting for transfers between devices  5.01 us (6%)
    ppermute x2, starting transfers between devices, swap(): return lax.ppermute(x, 'frm', [(0, 1), (1, 0)])  42.5 us
    ppermute x6, starting transfers between devices, shift(): lax.ppermute(x, axis, [(i, i + step) for i in range(n) if 0 <= i + step <...  18.3 us
    pallas_call x8, Pallas kernels, call(): run(*(held(v, spec) for v, spec in zip(args, specs, strict=True)))  12.6 us
    ppermute x6, waiting for transfers between devices, shift(): lax.ppermute(x, axis, [(i, i + step) for i in range(n) if 0 <= i + step <...  3.84 us
  transfers between devices with their start and end apart: 8, of which 3 were waited for; matrix products, arithmetic and copies ran while one was open for 0% of the time, Pallas kernels for 6%

profile of v2, /device:TPU:33, one launch (start us, length us, event | category | flops | bytes accessed | tf_op | source)
XLA Modules:
  0.0 78.7 jit_solution(12858520690520485087)
XLA Ops:
  0.0 0.0 copy-start.3
  0.0 0.0 copy-start
  0.0 1.8 %shard_map.91 = (bf16[4,160,128]{2,1,0:T(8,128)(2,1)S(1)}, bf16[4,160,128]{2,1,0:T(8,128)(2,1)S(1)}, bf16[1120,128]{1,0:T(8,128)(2,1)S(1)}, bf16[1120,128]{1,0:T...) custom-call(bf16[4,160,256]{2,1,0:T(8,128)(2,1)} %bitcast.14, ...), custom_call_target="tpu_custom_call" | custom-call | flops 100000000 | bytes 2000000 | tf_op jit(solution)/shard_map/pallas_call | solution.py:29
  1.8 5.3 %collective-permute-start = (bf16[1120,128]{1,0:T(8,128)(2,1)S(1)}, bf16[1120,128]{1,0:T(8,128)(2,1)S(1)}, u32[]{:S(2)}, u32[]{:S(2)}) collective-permute-start(bf16[1120,128]{1,0:T(8,128)(2,1)S(1)} %get-tuple-element.26), channel_id=1, source_target_pairs={{0,8},{8,16},{16,24},{24,32},{32,40},{40,48},{48,56},{56,64},{64,7... | collective-permute-start | bytes 860168 | tf_op jit(solution)/shard_map/ppermute | solution.py:249
  7.1 1.3 %collective-permute-start.1 = (bf16[1120,128]{1,0:T(8,128)(2,1)S(1)}, bf16[1120,128]{1,0:T(8,128)(2,1)S(1)}, u32[]{:S(2)}, u32[]{:S(2)}) collective-permute-start(bf16[1120,128]{1,0:T(8,128)(2,1)S(1)} %get-tuple-element.27), channel_id=1, source_target_pairs={{8,0},{16,8},{24,16},{32,24},{40,32},{48,40},{56,48},{64,56},{72,6... | collective-permute-start | bytes 860168 | tf_op jit(solution)/shard_map/ppermute | solution.py:249
  8.4 1.3 %collective-permute-start.2 = (bf16[320,128]{1,0:T(8,128)(2,1)S(1)}, bf16[320,128]{1,0:T(8,128)(2,1)S(1)}, u32[]{:S(2)}, u32[]{:S(2)}) collective-permute-start(bf16[320,128]{1,0:T(8,128)(2,1)S(1)} %get-tuple-element.28), channel_id=1, source_target_pairs={{2,0},{4,2},{6,4},{3,1},{5,3},{7,5},{10,8},{12,10},{14,12},{11,9},... | collective-permute-start | bytes 245768 | tf_op jit(solution)/shard_map/ppermute | solution.py:249
  9.7 4.0 %collective-permute-start.3 = (bf16[320,128]{1,0:T(8,128)(2,1)S(1)}, bf16[320,128]{1,0:T(8,128)(2,1)S(1)}, u32[]{:S(2)}, u32[]{:S(2)}) collective-permute-start(bf16[320,128]{1,0:T(8,128)(2,1)S(1)} %get-tuple-element.29), channel_id=1, source_target_pairs={{0,2},{2,4},{4,6},{1,3},{3,5},{5,7},{8,10},{10,12},{12,14},{9,11},... | collective-permute-start | bytes 245768 | tf_op jit(solution)/shard_map/ppermute | solution.py:249
  13.8 0.1 stack.15.where_ref
  13.9 0.0 collective-permute-done.2.from_right
  13.9 1.4 %collective-permute-done.3.from_left = bf16[320,128]{1,0:T(8,128)(2,1)S(1)} collective-permute-done((bf16[320,128]{1,0:T(8,128)(2,1)S(1)}, bf16[320,128]{1,0:T(8,128)(2,1)S(1)}, u32[]{:S(2)}, u32[]{:S(2)}) %collective-permute-start.3) | collective-permute-done | bytes 81952 | tf_op jit(solution)/shard_map/ppermute | solution.py:249
  15.3 5.1 %collective-permute-start.4 = (bf16[64,128]{1,0:T(8,128)(2,1)S(1)}, bf16[64,128]{1,0:T(8,128)(2,1)S(1)}, u32[]{:S(2)}, u32[]{:S(2)}) collective-permute-start(bf16[64,128]{1,0:T(8,128)(2,1)S(1)} %get-tuple-element.30), channel_id=1, source_target_pairs={{0,8},{8,16},{16,24},{24,32},{32,40},{40,48},{48,56},{56,64},{64,7... | collective-permute-start | bytes 49160 | tf_op jit(solution)/shard_map/ppermute | solution.py:249
  20.3 1.3 %collective-permute-start.5 = (bf16[64,128]{1,0:T(8,128)(2,1)S(1)}, bf16[64,128]{1,0:T(8,128)(2,1)S(1)}, u32[]{:S(2)}, u32[]{:S(2)}) collective-permute-start(bf16[64,128]{1,0:T(8,128)(2,1)S(1)} %get-tuple-element.31), channel_id=1, source_target_pairs={{8,0},{16,8},{24,16},{32,24},{40,32},{48,40},{56,48},{64,56},{72,6... | collective-permute-start | bytes 49160 | tf_op jit(solution)/shard_map/ppermute | solution.py:249
  21.6 0.0 copy-done.3
  21.7 0.0 copy-done
  21.7 1.7 %shard_map.93 = (bf16[8,352,128]{2,1,0:T(8,128)(2,1)S(1)}, bf16[8,352,128]{2,1,0:T(8,128)(2,1)S(1)}, f32[6,352,128]{2,1,0:T(8,128)S(1)}) custom-call(bf16[8,320,128]{2,1,0:T(8,128)(2,1)S(1)} %bitcast.13, bf16[4,160,128]{2,1,0:T(8,128)(2,1)S(1)} %get-tuple-element.32.act, bf16[320,128]{1,0:T(8,128)(2,1)S(1)} %get-tuple-element.33.merged, ...), custom_call_target="tpu_custom_call" | custom-call | flops 1509949440 | bytes 4000000 | tf_op jit(solution)/shard_map/pallas_call | solution.py:29
  23.4 0.0 copy-start.1
  23.4 0.0 collective-permute-done.4.cor_a
  23.4 2.5 %collective-permute-done.5.cor_b = bf16[64,128]{1,0:T(8,128)(2,1)S(1)} collective-permute-done((bf16[64,128]{1,0:T(8,128)(2,1)S(1)}, bf16[64,128]{1,0:T(8,128)(2,1)S(1)}, u32[]{:S(2)}, u32[]{:S(2)}) %collective-permute-start.5) | collective-permute-done | bytes 16416 | tf_op jit(solution)/shard_map/ppermute | solution.py:249
  25.9 0.0 collective-permute-done.row_a
  25.9 0.0 collective-permute-done.1.row_b
  25.9 0.8 %shard_map.94 = (bf16[4,352,128]{2,1,0:T(8,128)(2,1)S(1)}, bf16[4,352,128]{2,1,0:T(8,128)(2,1)S(1)}, bf16[12,352,128]{2,1,0:T(8,128)(2,1)S(1)}) custom-call(s32[5]{0:T(128)S(1)} %stack.15.where_ref, bf16[1120,128]{1,0:T(8,128)(2,1)S(1)} %collective-permute-done.row_a, bf16[1120,128]{1,0:T(8,128)(2,1)S(1)} %collective-permute-done.1.row_b, ...), custom_call_target="tpu_custom_call" | custom-call | flops 100000000 | bytes 4000000 | tf_op jit(solution)/shard_map/pallas_call | solution.py:29
  26.7 40.2 %collective-permute-start.6 = (bf16[12,352,128]{2,1,0:T(8,128)(2,1)S(1)}, bf16[12,352,128]{2,1,0:T(8,128)(2,1)S(1)}, u32[]{:S(2)}, u32[]{:S(2)}) collective-permute-start(bf16[12,352,128]{2,1,0:T(8,128)(2,1)S(1)} %get-tuple-element.36), channel_id=1, source_target_pairs={{0,1},{1,0},{2,3},{3,2},{4,5},{5,4},{6,7},{7,6},{8,9},{9,8},{10,11... | collective-permute-start | bytes 3244040 | tf_op jit(solution)/shard_map/ppermute | solution.py:253
  66.9 0.0 copy-done.1
  66.9 1.1 %shard_map.95 = (f32[4,352,128]{2,1,0:T(8,128)S(1)}, bf16[10,352,128]{2,1,0:T(8,128)(2,1)S(1)}) custom-call(bf16[8,352,128]{2,1,0:T(8,128)(2,1)S(1)} %get-tuple-element.34.cache_core, bf16[8,352,128]{2,1,0:T(8,128)(2,1)S(1)} %get-tuple-element.35.act_core, bf16[4,352,128]{2,1,0:T(8,128)(2,1)S(1)} %get-tuple-element.38.cache_border, ...), custom_call_target="tpu_custom_call" | custom-call | flops 754974720 | bytes 4000000 | tf_op jit(solution)/shard_map/pallas_call | solution.py:29
  68.1 1.2 %collective-permute-done.6.middle = bf16[12,352,128]{2,1,0:T(8,128)(2,1)S(1)} collective-permute-done((bf16[12,352,128]{2,1,0:T(8,128)(2,1)S(1)}, bf16[12,352,128]{2,1,0:T(8,128)(2,1)S(1)}, u32[]{:S(2)}, u32[]{:S(2)}) %collective-permute-start.6) | collective-permute-done | bytes 1081376 | tf_op jit(solution)/shard_map/ppermute | solution.py:253
  69.2 0.0 copy-start.2
  69.2 2.8 %shard_map.96 = (bf16[10,352,128]{2,1,0:T(8,128)(2,1)S(1)}, bf16[10,352,128]{2,1,0:T(8,128)(2,1)S(1)}) custom-call(s32[5]{0:T(128)S(1)} %stack.15.where_ref, bf16[12,352,128]{2,1,0:T(8,128)(2,1)S(1)} %collective-permute-done.6.middle, f32[6,352,128]{2,1,0:T(8,128)S(1)} %get-tuple-element.37.part_in, f32[4,352,128]{2,1,0:T(8,128)S(1)} %get-tuple-element.40.part_out, ...), custom_call_target="tpu_custom_call" | custom-call | flops 754974720 | bytes 6000000 | tf_op jit(solution)/shard_map/pallas_call | solution.py:29
  72.0 2.3 %collective-permute-start.7 = (bf16[10,352,128]{2,1,0:T(8,128)(2,1)S(1)}, bf16[10,352,128]{2,1,0:T(8,128)(2,1)S(1)}, u32[]{:S(2)}, u32[]{:S(2)}) collective-permute-start(bf16[10,352,128]{2,1,0:T(8,128)(2,1)S(1)} %get-tuple-element.43), channel_id=1, source_target_pairs={{0,1},{1,0},{2,3},{3,2},{4,5},{5,4},{6,7},{7,6},{8,9},{9,8},{10,11... | collective-permute-start | bytes 2703368 | tf_op jit(solution)/shard_map/ppermute | solution.py:253
  74.3 0.0 copy-done.2
  74.4 2.2 %shard_map.97.part = f32[8,320,128]{2,1,0:T(8,128)S(1)} custom-call(bf16[10,352,128]{2,1,0:T(8,128)(2,1)S(1)} %get-tuple-element.42.two_frame, bf16[10,352,128]{2,1,0:T(8,128)(2,1)S(1)} %get-tuple-element.44.act_two, bf16[3,3,3,128,128]{4,3,2,1,0:T(8,128)(2,1)S(1)} %copy-done.2, bf16[4,160,128]{2,1,0:T(8,128)(2,1)S(1)} %get-tuple-element.45.proj, ...), custom_call_target="tpu_custom_call" | custom-call | flops 1509949440 | bytes 6000000 | tf_op jit(solution)/shard_map/pallas_call | solution.py:29
  76.5 0.0 collective-permute-done.7.middle
  76.5 2.2 %shard_map.98 = bf16[8,320,128]{2,1,0:T(8,128)(2,1)} custom-call(bf16[10,352,128]{2,1,0:T(8,128)(2,1)S(1)} %collective-permute-done.7.middle, f32[8,320,128]{2,1,0:T(8,128)S(1)} %shard_map.97.part, bf16[3,3,3,128,128]{4,3,2,1,0:T(8,128)(2,1)S(1)} %copy-done.2), custom_call_target="tpu_custom_call" | custom-call | flops 754974720 | bytes 6000000 | tf_op jit(solution)/shard_map/pallas_call | solution.py:29
  (1 shorter events, 0.0 us)
Async XLA Ops:
  0.0 21.7 %copy-start.3 = (bf16[1,8,320,128]{3,2,1,0:T(8,128)(2,1)S(1)}, bf16[1,8,320,128]{3,2,1,0:T(8,128)(2,1)}, u32[]{:S(2)}) copy-start(bf16[1,8,320,128]{3,2,1,0:T(8,128)(2,1)} %param.12) | copy-start | bytes 1966084
  0.0 21.7 %copy-start = (bf16[3,3,3,128,128]{4,3,2,1,0:T(8,128)(2,1)S(1)}, bf16[3,3,3,128,128]{4,3,2,1,0:T(8,128)(2,1)}, u32[]{:S(2)}) copy-start(bf16[3,3,3,128,128]{4,3,2,1,0:T(8,128)(2,1)} %weight.9) | copy-start | bytes 2654212
  1.8 24.1 %collective-permute-start = (bf16[1120,128]{1,0:T(8,128)(2,1)S(1)}, bf16[1120,128]{1,0:T(8,128)(2,1)S(1)}, u32[]{:S(2)}, u32[]{:S(2)}) collective-permute-start(bf16[1120,128]{1,0:T(8,128)(2,1)S(1)} %get-tuple-element.26), channel_id=1, source_target_pairs={{0,8},{8,16},{16,24},{24,32},{32,40},{40,48},{48,56},{56,64},{64,7... | collective-permute-start | bytes 860168 | tf_op jit(solution)/shard_map/ppermute | solution.py:249
  7.1 18.8 %collective-permute-start.1 = (bf16[1120,128]{1,0:T(8,128)(2,1)S(1)}, bf16[1120,128]{1,0:T(8,128)(2,1)S(1)}, u32[]{:S(2)}, u32[]{:S(2)}) collective-permute-start(bf16[1120,128]{1,0:T(8,128)(2,1)S(1)} %get-tuple-element.27), channel_id=1, source_target_pairs={{8,0},{16,8},{24,16},{32,24},{40,32},{48,40},{56,48},{64,56},{72,6... | collective-permute-start | bytes 860168 | tf_op jit(solution)/shard_map/ppermute | solution.py:249
  8.4 5.5 %collective-permute-start.2 = (bf16[320,128]{1,0:T(8,128)(2,1)S(1)}, bf16[320,128]{1,0:T(8,128)(2,1)S(1)}, u32[]{:S(2)}, u32[]{:S(2)}) collective-permute-start(bf16[320,128]{1,0:T(8,128)(2,1)S(1)} %get-tuple-element.28), channel_id=1, source_target_pairs={{2,0},{4,2},{6,4},{3,1},{5,3},{7,5},{10,8},{12,10},{14,12},{11,9},... | collective-permute-start | bytes 245768 | tf_op jit(solution)/shard_map/ppermute | solution.py:249
  9.7 5.5 %collective-permute-start.3 = (bf16[320,128]{1,0:T(8,128)(2,1)S(1)}, bf16[320,128]{1,0:T(8,128)(2,1)S(1)}, u32[]{:S(2)}, u32[]{:S(2)}) collective-permute-start(bf16[320,128]{1,0:T(8,128)(2,1)S(1)} %get-tuple-element.29), channel_id=1, source_target_pairs={{0,2},{2,4},{4,6},{1,3},{3,5},{5,7},{8,10},{10,12},{12,14},{9,11},... | collective-permute-start | bytes 245768 | tf_op jit(solution)/shard_map/ppermute | solution.py:249
  15.3 8.2 %collective-permute-start.4 = (bf16[64,128]{1,0:T(8,128)(2,1)S(1)}, bf16[64,128]{1,0:T(8,128)(2,1)S(1)}, u32[]{:S(2)}, u32[]{:S(2)}) collective-permute-start(bf16[64,128]{1,0:T(8,128)(2,1)S(1)} %get-tuple-element.30), channel_id=1, source_target_pairs={{0,8},{8,16},{16,24},{24,32},{32,40},{40,48},{48,56},{56,64},{64,7... | collective-permute-start | bytes 49160 | tf_op jit(solution)/shard_map/ppermute | solution.py:249
  20.3 5.6 %collective-permute-start.5 = (bf16[64,128]{1,0:T(8,128)(2,1)S(1)}, bf16[64,128]{1,0:T(8,128)(2,1)S(1)}, u32[]{:S(2)}, u32[]{:S(2)}) collective-permute-start(bf16[64,128]{1,0:T(8,128)(2,1)S(1)} %get-tuple-element.31), channel_id=1, source_target_pairs={{8,0},{16,8},{24,16},{32,24},{40,32},{48,40},{56,48},{64,56},{72,6... | collective-permute-start | bytes 49160 | tf_op jit(solution)/shard_map/ppermute | solution.py:249
  23.4 43.5 %copy-start.1 = (bf16[1,8,320,128]{3,2,1,0:T(8,128)(2,1)S(1)}, bf16[1,8,320,128]{3,2,1,0:T(8,128)(2,1)}, u32[]{:S(2)}) copy-start(bf16[1,8,320,128]{3,2,1,0:T(8,128)(2,1)} %param.13) | copy-start | bytes 1966084
  26.7 42.5 %collective-permute-start.6 = (bf16[12,352,128]{2,1,0:T(8,128)(2,1)S(1)}, bf16[12,352,128]{2,1,0:T(8,128)(2,1)S(1)}, u32[]{:S(2)}, u32[]{:S(2)}) collective-permute-start(bf16[12,352,128]{2,1,0:T(8,128)(2,1)S(1)} %get-tuple-element.36), channel_id=1, source_target_pairs={{0,1},{1,0},{2,3},{3,2},{4,5},{5,4},{6,7},{7,6},{8,9},{9,8},{10,11... | collective-permute-start | bytes 3244040 | tf_op jit(solution)/shard_map/ppermute | solution.py:253
  69.2 5.1 %copy-start.2 = (bf16[3,3,3,128,128]{4,3,2,1,0:T(8,128)(2,1)S(1)}, bf16[3,3,3,128,128]{4,3,2,1,0:T(8,128)(2,1)}, u32[]{:S(2)}) copy-start(bf16[3,3,3,128,128]{4,3,2,1,0:T(8,128)(2,1)} %weight.11) | copy-start | bytes 2654212
  72.0 4.5 %collective-permute-start.7 = (bf16[10,352,128]{2,1,0:T(8,128)(2,1)S(1)}, bf16[10,352,128]{2,1,0:T(8,128)(2,1)S(1)}, u32[]{:S(2)}, u32[]{:S(2)}) collective-permute-start(bf16[10,352,128]{2,1,0:T(8,128)(2,1)S(1)} %get-tuple-element.43), channel_id=1, source_target_pairs={{0,1},{1,0},{2,3},{3,2},{4,5},{5,4},{6,7},{7,6},{8,9},{9,8},{10,11... | collective-permute-start | bytes 2703368 | tf_op jit(solution)/shard_map/ppermute | solution.py:253

commit v3 on v2

v3 whole, which is shorter than its diff:
```python
import functools

import jax
import jax.numpy as jnp
from jax import lax
from jax.experimental import pallas as pl
from jax.experimental.pallas import tpu as pltpu
from jax.sharding import PartitionSpec as P

B = 16
BF = jnp.bfloat16
F32 = jnp.float32
VMEM = pl.BlockSpec(memory_space=pltpu.VMEM)
HBM = pl.BlockSpec(memory_space=pltpu.HBM)


def call(body, outs, specs, scratch=(), flops=0, nbytes=0, limit=24):
    run = pl.pallas_call(
        body,
        out_shape=[jax.ShapeDtypeStruct(s, d) for s, d in outs],
        in_specs=specs,
        out_specs=[VMEM] * len(outs),
        scratch_shapes=list(scratch),
        cost_estimate=pl.CostEstimate(flops=flops, bytes_accessed=nbytes, transcendentals=0),
        compiler_params=pltpu.CompilerParams(vmem_limit_bytes=int(limit * 1024 * 1024)),
    )
    held = lambda v, spec: pltpu.with_memory_space_constraint(v, pltpu.HBM) if spec is HBM else v
    return lambda *args: run(*(held(v, spec) for v, spec in zip(args, specs, strict=True)))


def silu(v):
    return v / (1.0 + jnp.exp(-v))


def low_half():
    return lax.broadcasted_iota(jnp.int32, (B, 128), 0) < B // 2


def spread_matrix(cols, ccols):
    fine = lax.broadcasted_iota(jnp.int32, (cols, ccols), 0)
    return (fine // 2 == lax.broadcasted_iota(jnp.int32, (cols, ccols), 1)).astype(F32).astype(BF)


def even(axis):
    return lax.rem(lax.axis_index(axis), 2) == 0


def pick(axis, high, low, step=1):
    start = jnp.where(even(axis), high, low)
    return pl.multiple_of(start, step) if step > 1 else start


def first_kernel(
    latent, weight, bias, one, two, bias_one, bias_two,
    proj, act, row_0, row_1, col_0, col_1, b_one, b_two,
    latent_v, weight_v, bias_v, sems,
):
    rows, cols, _ = one.shape
    crows, ccols, _ = latent.shape
    copies = [(latent, latent_v), (weight, weight_v), (bias, bias_v)]
    n_first = len(copies)
    n_c1 = rows * B
    n_c2 = (rows + crows) * B
    t0 = 2 * cols + ccols
    sends = ((row_0, col_0, False), (row_1, col_1, True))
    for row_s, col_s, flip in sends:
        lo, hi = (cols - B, 0) if flip else (0, cols - B)
        c = pl.ds(pick("col", hi, lo, B), B)
        for i in range(rows):
            copies.append((one.at[i, c], col_s.at[i * B : (i + 1) * B]))
            copies.append((two.at[i, c], col_s.at[n_c2 + i * B : n_c2 + (i + 1) * B]))
        lo, hi = (rows - 2, 0) if flip else (0, rows - 2)
        r = pick("row", hi, lo)
        for k in range(2):
            copies.append((one.at[r + k], row_s.at[k * cols : (k + 1) * cols]))
        lo, hi = (rows - 1, 0) if flip else (0, rows - 1)
        copies.append((two.at[pick("row", hi, lo)], row_s.at[t0 : t0 + cols]))
    copies.append((bias_one, b_one))
    copies.append((bias_two, b_two))
    started = [pltpu.make_async_copy(s, d, sems.at[i]) for i, (s, d) in enumerate(copies)]
    for c in started:
        c.start()
    for c in started[:n_first]:
        c.wait()
    for i in range(crows):
        p = (jnp.dot(latent_v[i], weight_v[...], preferred_element_type=F32) + bias_v[...]).astype(BF)
        proj[i] = p
        act[i] = silu(p.astype(F32)).astype(BF)
    for row_s, col_s, flip in sends:
        lo, hi = (crows - 1, 0) if flip else (0, crows - 1)
        row_s[2 * cols : t0, :] = act[pick("row", hi, lo)]
        lo, hi = (ccols - B, 0) if flip else (0, ccols - B)
        c = pl.ds(pick("col", hi, lo, B), B)
        for i in range(crows):
            col_s[n_c1 + i * B : n_c1 + (i + 1) * B, :] = act[i, c, :]
    for c in started[n_first:]:
        c.wait()


def corner_kernel(rows, crows, got_0, got_1, merged, cor_0, cor_1):
    take_0 = low_half() == even("col")
    for i in range(2 * rows + crows):
        s = slice(i * B, (i + 1) * B)
        merged[s, :] = jnp.where(take_0, got_0[s, :].astype(F32), got_1[s, :].astype(F32)).astype(BF)
    lows = (0, 1, rows, rows + crows)
    highs = (rows - 2, rows - 1, rows + crows - 1, 2 * rows + crows - 1)
    for k, (lo, hi) in enumerate(zip(lows, highs)):
        s = slice(k * B, (k + 1) * B)
        cor_0[s, :] = merged[pl.ds(pick("row", hi * B, lo * B, B), B), :]
        cor_1[s, :] = merged[pl.ds(pick("row", lo * B, hi * B, B), B), :]


def block(ref, i):
    return ref[i * B : (i + 1) * B, :].astype(F32)


def spread_edge(m):
    return jnp.where(
        low_half(), jnp.broadcast_to(m[0:1], (B, 128)), jnp.broadcast_to(m[B - 1 : B], (B, 128))
    ).astype(BF)


def put_row(dst, i, inside, edges):
    cols = dst.shape[1] - 2 * B
    dst[i, 0:B, :] = edges
    dst[i, B : B + cols, :] = inside
    dst[i, B + cols :, :] = edges


def conv_rows(frames, steps, weight, k, sums, slot):
    span = sums.shape[1] - 16
    w01, w2 = [], []
    zero = jnp.zeros(weight.shape[3:], BF)
    for a in steps:
        for p in range(4):
            if p < 3:
                w01.append(jnp.concatenate([weight[a, p, 0], weight[a, p, 1]], axis=1))
            w2.append(jnp.concatenate([weight[a, p, 2] if p < 3 else zero, weight[a, p - 1, 2] if p else zero], axis=1))
    w01, w2 = jnp.concatenate(w01, axis=0), jnp.concatenate(w2, axis=0)
    lhs = jnp.concatenate([f(k + p) for f in frames for p in range(4)], axis=1)
    y2 = jnp.dot(lhs, w2, preferred_element_type=F32)
    results = []
    for h in range(2):
        lhs = jnp.concatenate([f(k + h + p) for f in frames for p in range(3)], axis=1)
        y01 = jnp.dot(lhs, w01, preferred_element_type=F32)
        s = 2 * slot + h
        sums[s, 8 : 8 + span, 0:128] = y01[:, 0:128]
        sums[s, 8 : 8 + span, 128:256] = y2[:, h * 128 : (h + 1) * 128]
        results.append(sums[s, 7 : 7 + span, 0:128] + y01[:, 128:256] + sums[s, 9 : 9 + span, 128:256])
    return results


def joined(core, border):
    n = core.shape[0]
    return lambda i: border[i] if i < 2 else core[i - 2] if i < n + 2 else border[i - n]


def fill_kernel(one, act, merged, cache_core, act_core, send):
    rows, cols, _ = one.shape
    crows, ccols, _ = act.shape
    for i in range(rows):
        put_row(cache_core, i, one[i], merged[i * B : (i + 1) * B, :])
    spread = spread_matrix(cols, ccols)
    for m in range(0, crows, 2):
        wide = jnp.dot(spread, jnp.concatenate([act[m], act[m + 1]], axis=1), preferred_element_type=F32).astype(BF)
        for h in range(2):
            edges = spread_edge(block(merged, rows + m + h))
            for i in range(2):
                put_row(act_core, 2 * (m + h) + i, wide[:, h * 128 : (h + 1) * 128], edges)
    choose(send, act_core, cache_core)


def choose(send, leading, other):
    for first, src in ((True, leading), (False, other)):

        @pl.when((lax.axis_index("frm") == 0) == first)
        def _(src=src):
            send[...] = src[...]


def inner_kernel(cache_core, act_core, weight, part, sums):
    frames = (lambda i: cache_core[i - 2], lambda i: act_core[i - 2])
    for n, k in enumerate(range(2, 2 + part.shape[0], 2)):
        for h, v in enumerate(conv_rows(frames, (0, 2), weight, k, sums, n % 2)):
            part[k - 2 + h] = v


def border_kernel(row_0, row_1, cor_0, cor_1, cache_border, act_border, send):
    _, span, _ = cache_border.shape
    cols = span - 2 * B
    ccols = row_0.shape[0] - 3 * cols
    for lead in (True, False):

        @pl.when(even("row") == lead)
        def _(lead=lead):
            pairs = ((row_1, cor_1), (row_0, cor_0)) if lead else ((row_0, cor_0), (row_1, cor_1))
            coarse = jnp.concatenate([row[2 * cols : 2 * cols + ccols, :] for row, _ in pairs], axis=1)
            wide = jnp.dot(spread_matrix(cols, ccols), coarse, preferred_element_type=F32).astype(BF)
            for h, (row, cor) in enumerate(pairs):
                edges = spread_edge(block(cor, 2))
                for k in range(2):
                    put_row(cache_border, 2 * h + k, row[k * cols : (k + 1) * cols, :], cor[k * B : (k + 1) * B, :])
                    put_row(act_border, 2 * h + k, wide[:, h * 128 : (h + 1) * 128], edges)

    choose(send, act_border, cache_border)


def outer_kernel(cache_core, act_core, cache_border, act_border, weight, two, merged, row_0, row_1, cor_0, cor_1, part, two_frame, sums, *, first):
    rows, cols, _ = two.shape
    frames = (joined(cache_core, cache_border), joined(act_core, act_border))
    for n, k in enumerate((0, rows)):
        for h, v in enumerate(conv_rows(frames, (0, 2), weight, k, sums, n)):
            part[2 * n + h] = v
    t0 = row_0.shape[0] - cols
    for i in range(rows):
        put_row(two_frame, i + 1, two[i], merged[(first + i) * B : (first + i + 1) * B, :])
    for lead in (True, False):

        @pl.when(even("row") == lead)
        def _(lead=lead):
            put_row(two_frame, rows + 1 if lead else 0, row_0[t0:, :], cor_0[3 * B :, :])
            put_row(two_frame, 0 if lead else rows + 1, row_1[t0:, :], cor_1[3 * B :, :])


def finish_row(out, i, v, row, n_out):
    span = v.shape[0]
    t = lax.broadcasted_iota(jnp.int32, (B, 128), 0)
    keep_left = (t != B - 1) | (lax.axis_index("col") != 0)
    keep_right = (t != 0) | (lax.axis_index("col") != lax.axis_size("col") - 1)
    v = silu(v)
    if row == 0:
        v = jnp.where(lax.axis_index("row") != 0, v, 0.0)
    if row == n_out - 1:
        v = jnp.where(lax.axis_index("row") != lax.axis_size("row") - 1, v, 0.0)
    out[i, 0:B, :] = jnp.where(keep_left, v[0:B], 0.0).astype(BF)
    out[i, B : span - B, :] = v[B : span - B].astype(BF)
    out[i, span - B :, :] = jnp.where(keep_right, v[span - B :], 0.0).astype(BF)


def middle_inner_kernel(core, part, weight, bias, out, sums):
    n = out.shape[0]
    for m in range(0, n, 2):
        for h, v in enumerate(conv_rows((lambda i: core[i - 2],), (1,), weight, m + 2, sums, m // 2 % 2)):
            finish_row(out, m + h, v + part[m + h] + bias[...], m + h + 2, n + 4)


def middle_outer_kernel(core, border, part, weight, bias, inner, two_frame, out, send, sums):
    n_out = out.shape[0]
    frame = joined(core, border)
    for n, k in enumerate((0, n_out - 2)):
        for h, v in enumerate(conv_rows((frame,), (1,), weight, k, sums, n)):
            finish_row(out, k + h, v + part[2 * n + h] + bias[...], k + h, n_out)
    out[2 : n_out - 2] = inner[...]
    choose(send, out, two_frame)


def own_two_kernel(two_frame, act_two, weight, proj, bias, part, sums):
    n_out, cols, _ = part.shape
    spread = spread_matrix(cols, proj.shape[1])
    frames = (lambda i: two_frame[i], lambda i: act_two[i])
    for k in range(0, n_out, 2):
        if k % 4 == 0:
            wide = jnp.dot(spread, jnp.concatenate([proj[k // 2], proj[k // 2 + 1]], axis=1), preferred_element_type=F32)
        base = wide[:, k % 4 * 64 : k % 4 * 64 + 128] + bias[...]
        for h, v in enumerate(conv_rows(frames, (0, 2), weight, k, sums, k // 2 % 2)):
            part[k + h] = v[B : B + cols] + base


def middle_two_kernel(middle, part, weight, out, sums):
    n_out, cols, _ = out.shape
    for k in range(0, n_out, 2):
        for h, v in enumerate(conv_rows((lambda i: middle[i],), (1,), weight, k, sums, k // 2 % 2)):
            out[k + h] = (part[k + h] + v[B : B + cols]).astype(BF)


def exchange(x, axis, first):
    pairs = [(i, i + 1) for i in range(first, lax.axis_size(axis) - 1, 2)]
    return lax.ppermute(x, axis, pairs + [(j, i) for i, j in pairs])


def swap(x):
    return lax.ppermute(x, "frm", [(0, 1), (1, 0)])


def program(latent, proj_weight, proj_bias, cache_one, cache_two, conv_one, bias_one, conv_two, bias_two):
    latent, one, two = latent[0], cache_one[0], cache_two[0]
    rows, cols, ch = one.shape
    crows, ccols, lch = latent.shape
    span = cols + 2 * B
    n_edge = (2 * rows + crows) * B
    n_row = 3 * cols + ccols
    sums = pltpu.VMEM((4, span + 16, 2 * ch), F32)
    proj, act, row_0, row_1, col_0, col_1, b_one, b_two = call(
        first_kernel,
        [
            ((crows, ccols, ch), BF),
            ((crows, ccols, ch), BF),
            ((n_row, ch), BF),
            ((n_row, ch), BF),
            ((n_edge, ch), BF),
            ((n_edge, ch), BF),
            ((1, ch), F32),
            ((1, ch), F32),
        ],
        [HBM] * 7,
        scratch=[
            pltpu.VMEM((crows, ccols, lch), BF),
            pltpu.VMEM((lch, ch), BF),
            pltpu.VMEM((1, ch), F32),
            pltpu.SemaphoreType.DMA((3 + 4 * rows + 8,)),
        ],
        flops=10**8,
        nbytes=2 * 10**6,
        limit=24,
    )(latent, proj_weight, proj_bias.reshape(1, ch), one, two, bias_one.reshape(1, ch), bias_two.reshape(1, ch))
    got_1 = exchange(col_1, "col", 1)
    got_0 = exchange(col_0, "col", 0)
    row_1 = exchange(row_1, "row", 1)
    row_0 = exchange(row_0, "row", 0)
    merged, cor_0, cor_1 = call(
        functools.partial(corner_kernel, rows, crows),
        [((n_edge, ch), BF), ((4 * B, ch), BF), ((4 * B, ch), BF)],
        [VMEM] * 2,
        flops=10**6,
        nbytes=2 * 10**5,
    )(got_0, got_1)
    cor_1 = exchange(cor_1, "row", 1)
    cor_0 = exchange(cor_0, "row", 0)
    third = 2 * 9 * ch * ch * rows * cols
    core_shape, border_shape = ((rows, span, ch), BF), ((4, span, ch), BF)
    cache_core, act_core, send_core = call(
        fill_kernel, [core_shape] * 3, [VMEM] * 3, flops=10**8, nbytes=4 * 10**6
    )(one, act, merged)
    middle_core = swap(send_core)
    (part_in,) = call(
        inner_kernel, [((rows - 2, span, ch), F32)], [VMEM] * 3, scratch=[sums], flops=2 * third, nbytes=4 * 10**6
    )(cache_core, act_core, conv_one)
    cache_border, act_border, send_border = call(
        border_kernel, [border_shape] * 3, [VMEM] * 4, flops=10**8, nbytes=4 * 10**6
    )(row_0, row_1, cor_0, cor_1)
    middle_border = swap(send_border)
    part_out, two_frame = call(
        functools.partial(outer_kernel, first=rows + crows),
        [((4, span, ch), F32), ((rows + 2, span, ch), BF)],
        [VMEM] * 11,
        scratch=[sums],
        flops=third,
        nbytes=4 * 10**6,
    )(cache_core, act_core, cache_border, act_border, conv_one, two, merged, row_0, row_1, cor_0, cor_1)
    (act_inner,) = call(
        middle_inner_kernel, [((rows - 2, span, ch), BF)], [VMEM] * 4, scratch=[sums], flops=third, nbytes=6 * 10**6
    )(middle_core, part_in, conv_one, b_one)
    act_two, send_two = call(
        middle_outer_kernel,
        [((rows + 2, span, ch), BF)] * 2,
        [VMEM] * 7,
        scratch=[sums],
        flops=third // 2,
        nbytes=6 * 10**6,
    )(middle_core, middle_border, part_out, conv_one, b_one, act_inner, two_frame)
    middle_two = swap(send_two)
    (part_two,) = call(
        own_two_kernel, [((rows, cols, ch), F32)], [VMEM] * 5, scratch=[sums], flops=2 * third, nbytes=6 * 10**6
    )(two_frame, act_two, conv_two, proj, b_two)
    (decoded,) = call(
        middle_two_kernel, [((rows, cols, ch), BF)], [VMEM] * 3, scratch=[sums], flops=third, nbytes=6 * 10**6
    )(middle_two, part_two, conv_two)
    return decoded[None]


def solution(mesh):
    placed = (
        P(("grp", "frm"), "row", "col", None),
        P(),
        P(),
        P(("grp", "frm"), "row", "col", None),
        P(("grp", "frm"), "row", "col", None),
        P(),
        P(),
        P(),
        P(),
    )
    return jax.shard_map(
        program,
        mesh=mesh,
        in_specs=placed,
        out_specs=P(("grp", "frm"), "row", "col", None),
        check_vma=False,
    )
```

time: 79 us -> 80.1 us (1.014)
  the two profiles are of different devices: /device:TPU:33 before, /device:TPU:99 now
where the time goes in v3:
time: 80.1 us; the launch traced here: 79.8 us
  starting transfers between devices  62.7 us (78%)
  Pallas kernels  11.7 us (15%)
  waiting for transfers between devices  5.11 us (6%)
    ppermute x6, starting transfers between devices, exchange(): return lax.ppermute(x, axis, pairs + [(j, i) for i, j in pairs])  53.9 us
    pallas_call x10, Pallas kernels, call(): run(*(held(v, spec) for v, spec in zip(args, specs, strict=True)))  11.7 us
    ppermute x3, starting transfers between devices, swap(): return lax.ppermute(x, 'frm', [(0, 1), (1, 0)])  8.74 us
    ppermute x6, waiting for transfers between devices, exchange(): return lax.ppermute(x, axis, pairs + [(j, i) for i, j in pairs])  4.86 us
  transfers between devices with their start and end apart: 9, of which 4 were waited for; matrix products, arithmetic and copies ran while one was open for 0% of the time, Pallas kernels for 8%

profile of v3, /device:TPU:99, one launch (start us, length us, event | category | flops | bytes accessed | tf_op | source)
XLA Modules:
  0.0 79.8 jit_solution(2896902778796638064)
XLA Ops:
  0.0 1.8 %shard_map.91 = (bf16[4,160,128]{2,1,0:T(8,128)(2,1)S(1)}, bf16[4,160,128]{2,1,0:T(8,128)(2,1)S(1)}, bf16[1120,128]{1,0:T(8,128)(2,1)S(1)}, bf16[1120,128]{1,0:T...) custom-call(bf16[4,160,256]{2,1,0:T(8,128)(2,1)} %bitcast.11, ...), custom_call_target="tpu_custom_call" | custom-call | flops 100000000 | bytes 2000000 | tf_op jit(solution)/shard_map/pallas_call | solution.py:28
  1.8 2.1 %collective-permute-start = (bf16[320,128]{1,0:T(8,128)(2,1)S(1)}, bf16[320,128]{1,0:T(8,128)(2,1)S(1)}, u32[]{:S(2)}, u32[]{:S(2)}) collective-permute-start(bf16[320,128]{1,0:T(8,128)(2,1)S(1)} %get-tuple-element.27), channel_id=1, source_target_pairs={{0,2},{4,6},{2,0},{6,4},{1,3},{5,7},{3,1},{7,5},{8,10},{12,14},{10... | collective-permute-start | bytes 245768 | tf_op jit(solution)/shard_map/ppermute | solution.py:278
  3.9 4.2 %collective-permute-start.1 = (bf16[320,128]{1,0:T(8,128)(2,1)S(1)}, bf16[320,128]{1,0:T(8,128)(2,1)S(1)}, u32[]{:S(2)}, u32[]{:S(2)}) collective-permute-start(bf16[320,128]{1,0:T(8,128)(2,1)S(1)} %get-tuple-element.28), channel_id=1, source_target_pairs={{2,4},{4,2},{3,5},{5,3},{10,12},{12,10},{11,13},{13,11},{18,20},{2... | collective-permute-start | bytes 245768 | tf_op jit(solution)/shard_map/ppermute | solution.py:278
  8.1 0.0 collective-permute-done.got_0
  8.1 1.8 %collective-permute-done.1.got_1 = bf16[320,128]{1,0:T(8,128)(2,1)S(1)} collective-permute-done((bf16[320,128]{1,0:T(8,128)(2,1)S(1)}, bf16[320,128]{1,0:T(8,128)(2,1)S(1)}, u32[]{:S(2)}, u32[]{:S(2)}) %collective-permute-start.1) | collective-permute-done | bytes 81952 | tf_op jit(solution)/shard_map/ppermute | solution.py:278
  10.0 0.0 copy-done.1
  10.0 0.3 shard_map.93
  10.3 3.7 %collective-permute-start.2 = (bf16[8,352,128]{2,1,0:T(8,128)(2,1)S(1)}, bf16[8,352,128]{2,1,0:T(8,128)(2,1)S(1)}, u32[]{:S(2)}, u32[]{:S(2)}) collective-permute-start(bf16[8,352,128]{2,1,0:T(8,128)(2,1)S(1)} %get-tuple-element.30), channel_id=1, source_target_pairs={{0,1},{1,0},{2,3},{3,2},{4,5},{5,4},{6,7},{7,6},{8,9},{9,8},{10,11... | collective-permute-start | bytes 2162696 | tf_op jit(solution)/shard_map/ppermute | solution.py:282
  14.0 40.4 %collective-permute-start.3 = (bf16[1120,128]{1,0:T(8,128)(2,1)S(1)}, bf16[1120,128]{1,0:T(8,128)(2,1)S(1)}, u32[]{:S(2)}, u32[]{:S(2)}) collective-permute-start(bf16[1120,128]{1,0:T(8,128)(2,1)S(1)} %get-tuple-element.31), channel_id=1, source_target_pairs={{0,8},{16,24},{32,40},{48,56},{64,72},{80,88},{96,104},{112,120},{... | collective-permute-start | bytes 860168 | tf_op jit(solution)/shard_map/ppermute | solution.py:278
  54.4 2.0 %collective-permute-start.4 = (bf16[1120,128]{1,0:T(8,128)(2,1)S(1)}, bf16[1120,128]{1,0:T(8,128)(2,1)S(1)}, u32[]{:S(2)}, u32[]{:S(2)}) collective-permute-start(bf16[1120,128]{1,0:T(8,128)(2,1)S(1)} %get-tuple-element.32), channel_id=1, source_target_pairs={{8,16},{24,32},{40,48},{56,64},{72,80},{88,96},{104,112},{120,128}... | collective-permute-start | bytes 860168 | tf_op jit(solution)/shard_map/ppermute | solution.py:278
  56.4 2.0 %collective-permute-start.5 = (bf16[64,128]{1,0:T(8,128)(2,1)S(1)}, bf16[64,128]{1,0:T(8,128)(2,1)S(1)}, u32[]{:S(2)}, u32[]{:S(2)}) collective-permute-start(bf16[64,128]{1,0:T(8,128)(2,1)S(1)} %get-tuple-element.33), channel_id=1, source_target_pairs={{0,8},{16,24},{32,40},{48,56},{64,72},{80,88},{96,104},{112,120},{... | collective-permute-start | bytes 49160 | tf_op jit(solution)/shard_map/ppermute | solution.py:278
  58.3 3.4 %collective-permute-start.6 = (bf16[64,128]{1,0:T(8,128)(2,1)S(1)}, bf16[64,128]{1,0:T(8,128)(2,1)S(1)}, u32[]{:S(2)}, u32[]{:S(2)}) collective-permute-start(bf16[64,128]{1,0:T(8,128)(2,1)S(1)} %get-tuple-element.34), channel_id=1, source_target_pairs={{8,16},{24,32},{40,48},{56,64},{72,80},{88,96},{104,112},{120,128}... | collective-permute-start | bytes 49160 | tf_op jit(solution)/shard_map/ppermute | solution.py:278
  61.7 0.2 collective-permute-done.5.cor_0
  62.0 2.8 %collective-permute-done.6.cor_1 = bf16[64,128]{1,0:T(8,128)(2,1)S(1)} collective-permute-done((bf16[64,128]{1,0:T(8,128)(2,1)S(1)}, bf16[64,128]{1,0:T(8,128)(2,1)S(1)}, u32[]{:S(2)}, u32[]{:S(2)}) %collective-permute-start.6) | collective-permute-done | bytes 16416 | tf_op jit(solution)/shard_map/ppermute | solution.py:278
  64.8 0.0 collective-permute-done.3.row_0
  64.8 0.0 collective-permute-done.4.row_1
  64.8 0.2 shard_map.94
  65.0 3.1 %collective-permute-start.7 = (bf16[4,352,128]{2,1,0:T(8,128)(2,1)S(1)}, bf16[4,352,128]{2,1,0:T(8,128)(2,1)S(1)}, u32[]{:S(2)}, u32[]{:S(2)}) collective-permute-start(bf16[4,352,128]{2,1,0:T(8,128)(2,1)S(1)} %get-tuple-element.35), channel_id=1, source_target_pairs={{0,1},{1,0},{2,3},{3,2},{4,5},{5,4},{6,7},{7,6},{8,9},{9,8},{10,11... | collective-permute-start | bytes 1081352 | tf_op jit(solution)/shard_map/ppermute | solution.py:282
  68.1 0.0 copy-done
  68.1 0.0 copy-start.2
  68.2 1.6 %shard_map.96.part = f32[6,352,128]{2,1,0:T(8,128)S(1)} custom-call(bf16[8,352,128]{2,1,0:T(8,128)(2,1)S(1)} %get-tuple-element.36.cache_core, bf16[8,352,128]{2,1,0:T(8,128)(2,1)S(1)} %get-tuple-element.37.act_core, bf16[3,3,3,128,128]{4,3,2,1,0:T(8,128)(2,1)S(1)} %copy-done), custom_call_target="tpu_custom_call" | custom-call | flops 1509949440 | bytes 4000000 | tf_op jit(solution)/shard_map/pallas_call | solution.py:28
  69.7 0.0 copy-done.2
  69.8 1.1 %shard_map.95 = (f32[4,352,128]{2,1,0:T(8,128)S(1)}, bf16[10,352,128]{2,1,0:T(8,128)(2,1)S(1)}) custom-call(bf16[8,352,128]{2,1,0:T(8,128)(2,1)S(1)} %get-tuple-element.36.cache_core, bf16[8,352,128]{2,1,0:T(8,128)(2,1)S(1)} %get-tuple-element.37.act_core, bf16[4,352,128]{2,1,0:T(8,128)(2,1)S(1)} %get-tuple-element.38.cache_border, ...), custom_call_target="tpu_custom_call" | custom-call | flops 754974720 | bytes 4000000 | tf_op jit(solution)/shard_map/pallas_call | solution.py:28
  70.9 0.0 collective-permute-done.2.core
  70.9 1.3 %shard_map.97.inner = bf16[6,352,128]{2,1,0:T(8,128)(2,1)S(1)} custom-call(bf16[8,352,128]{2,1,0:T(8,128)(2,1)S(1)} %collective-permute-done.2.core, f32[6,352,128]{2,1,0:T(8,128)S(1)} %shard_map.96.part, bf16[3,3,3,128,128]{4,3,2,1,0:T(8,128)(2,1)S(1)} %copy-done, f32[1,128]{1,0:T(1,128)S(1)} %get-tuple-element.41.bias), custom_call_target="tpu_custom_call" | custom-call | flops 754974720 | bytes 6000000 | tf_op jit(solution)/shard_map/pallas_call | solution.py:28
  72.2 0.0 collective-permute-done.7.border
  72.2 0.0 copy-start.3
  72.2 1.0 %shard_map.98 = (bf16[10,352,128]{2,1,0:T(8,128)(2,1)S(1)}, bf16[10,352,128]{2,1,0:T(8,128)(2,1)S(1)}) custom-call(bf16[8,352,128]{2,1,0:T(8,128)(2,1)S(1)} %collective-permute-done.2.core, bf16[4,352,128]{2,1,0:T(8,128)(2,1)S(1)} %collective-permute-done.7.border, f32[4,352,128]{2,1,0:T(8,128)S(1)} %get-tuple-element.40.part, ...), custom_call_target="tpu_custom_call" | custom-call | flops 377487360 | bytes 6000000 | tf_op jit(solution)/shard_map/pallas_call | solution.py:28
  73.2 2.0 %collective-permute-start.8 = (bf16[10,352,128]{2,1,0:T(8,128)(2,1)S(1)}, bf16[10,352,128]{2,1,0:T(8,128)(2,1)S(1)}, u32[]{:S(2)}, u32[]{:S(2)}) collective-permute-start(bf16[10,352,128]{2,1,0:T(8,128)(2,1)S(1)} %get-tuple-element.43), channel_id=1, source_target_pairs={{0,1},{1,0},{2,3},{3,2},{4,5},{5,4},{6,7},{7,6},{8,9},{9,8},{10,11... | collective-permute-start | bytes 2703368 | tf_op jit(solution)/shard_map/ppermute | solution.py:282
  75.2 2.2 %shard_map.99.part = f32[8,320,128]{2,1,0:T(8,128)S(1)} custom-call(bf16[10,352,128]{2,1,0:T(8,128)(2,1)S(1)} %get-tuple-element.42.two_frame, bf16[10,352,128]{2,1,0:T(8,128)(2,1)S(1)} %get-tuple-element.44.act_two, bf16[3,3,3,128,128]{4,3,2,1,0:T(8,128)(2,1)S(1)} %copy-done.3, bf16[4,160,128]{2,1,0:T(8,128)(2,1)S(1)} %get-tuple-element.45.proj, ...), custom_call_target="tpu_custom_call" | custom-call | flops 1509949440 | bytes 6000000 | tf_op jit(solution)/shard_map/pallas_call | solution.py:28
  77.4 0.2 collective-permute-done.8.middle
  77.6 2.2 %shard_map.100 = bf16[8,320,128]{2,1,0:T(8,128)(2,1)} custom-call(bf16[10,352,128]{2,1,0:T(8,128)(2,1)S(1)} %collective-permute-done.8.middle, f32[8,320,128]{2,1,0:T(8,128)S(1)} %shard_map.99.part, bf16[3,3,3,128,128]{4,3,2,1,0:T(8,128)(2,1)S(1)} %copy-done.3), custom_call_target="tpu_custom_call" | custom-call | flops 754974720 | bytes 6000000 | tf_op jit(solution)/shard_map/pallas_call | solution.py:28
  (4 shorter events, 0.0 us)
Async XLA Ops:
  0.0 10.0 %copy-start.1 = (bf16[1,8,320,128]{3,2,1,0:T(8,128)(2,1)S(1)}, bf16[1,8,320,128]{3,2,1,0:T(8,128)(2,1)}, u32[]{:S(2)}) copy-start(bf16[1,8,320,128]{3,2,1,0:T(8,128)(2,1)} %param.12) | copy-start | bytes 1966084
  0.0 68.1 %copy-start = (bf16[3,3,3,128,128]{4,3,2,1,0:T(8,128)(2,1)S(1)}, bf16[3,3,3,128,128]{4,3,2,1,0:T(8,128)(2,1)}, u32[]{:S(2)}) copy-start(bf16[3,3,3,128,128]{4,3,2,1,0:T(8,128)(2,1)} %weight.11) | copy-start | bytes 2654212
  1.8 6.3 %collective-permute-start = (bf16[320,128]{1,0:T(8,128)(2,1)S(1)}, bf16[320,128]{1,0:T(8,128)(2,1)S(1)}, u32[]{:S(2)}, u32[]{:S(2)}) collective-permute-start(bf16[320,128]{1,0:T(8,128)(2,1)S(1)} %get-tuple-element.27), channel_id=1, source_target_pairs={{0,2},{4,6},{2,0},{6,4},{1,3},{5,7},{3,1},{7,5},{8,10},{12,14},{10... | collective-permute-start | bytes 245768 | tf_op jit(solution)/shard_map/ppermute | solution.py:278
  3.9 6.0 %collective-permute-start.1 = (bf16[320,128]{1,0:T(8,128)(2,1)S(1)}, bf16[320,128]{1,0:T(8,128)(2,1)S(1)}, u32[]{:S(2)}, u32[]{:S(2)}) collective-permute-start(bf16[320,128]{1,0:T(8,128)(2,1)S(1)} %get-tuple-element.28), channel_id=1, source_target_pairs={{2,4},{4,2},{3,5},{5,3},{10,12},{12,10},{11,13},{13,11},{18,20},{2... | collective-permute-start | bytes 245768 | tf_op jit(solution)/shard_map/ppermute | solution.py:278
  10.3 60.6 %collective-permute-start.2 = (bf16[8,352,128]{2,1,0:T(8,128)(2,1)S(1)}, bf16[8,352,128]{2,1,0:T(8,128)(2,1)S(1)}, u32[]{:S(2)}, u32[]{:S(2)}) collective-permute-start(bf16[8,352,128]{2,1,0:T(8,128)(2,1)S(1)} %get-tuple-element.30), channel_id=1, source_target_pairs={{0,1},{1,0},{2,3},{3,2},{4,5},{5,4},{6,7},{7,6},{8,9},{9,8},{10,11... | collective-permute-start | bytes 2162696 | tf_op jit(solution)/shard_map/ppermute | solution.py:282
  14.0 50.7 %collective-permute-start.3 = (bf16[1120,128]{1,0:T(8,128)(2,1)S(1)}, bf16[1120,128]{1,0:T(8,128)(2,1)S(1)}, u32[]{:S(2)}, u32[]{:S(2)}) collective-permute-start(bf16[1120,128]{1,0:T(8,128)(2,1)S(1)} %get-tuple-element.31), channel_id=1, source_target_pairs={{0,8},{16,24},{32,40},{48,56},{64,72},{80,88},{96,104},{112,120},{... | collective-permute-start | bytes 860168 | tf_op jit(solution)/shard_map/ppermute | solution.py:278
  54.4 10.4 %collective-permute-start.4 = (bf16[1120,128]{1,0:T(8,128)(2,1)S(1)}, bf16[1120,128]{1,0:T(8,128)(2,1)S(1)}, u32[]{:S(2)}, u32[]{:S(2)}) collective-permute-start(bf16[1120,128]{1,0:T(8,128)(2,1)S(1)} %get-tuple-element.32), channel_id=1, source_target_pairs={{8,16},{24,32},{40,48},{56,64},{72,80},{88,96},{104,112},{120,128}... | collective-permute-start | bytes 860168 | tf_op jit(solution)/shard_map/ppermute | solution.py:278
  56.4 5.6 %collective-permute-start.5 = (bf16[64,128]{1,0:T(8,128)(2,1)S(1)}, bf16[64,128]{1,0:T(8,128)(2,1)S(1)}, u32[]{:S(2)}, u32[]{:S(2)}) collective-permute-start(bf16[64,128]{1,0:T(8,128)(2,1)S(1)} %get-tuple-element.33), channel_id=1, source_target_pairs={{0,8},{16,24},{32,40},{48,56},{64,72},{80,88},{96,104},{112,120},{... | collective-permute-start | bytes 49160 | tf_op jit(solution)/shard_map/ppermute | solution.py:278
  58.3 6.5 %collective-permute-start.6 = (bf16[64,128]{1,0:T(8,128)(2,1)S(1)}, bf16[64,128]{1,0:T(8,128)(2,1)S(1)}, u32[]{:S(2)}, u32[]{:S(2)}) collective-permute-start(bf16[64,128]{1,0:T(8,128)(2,1)S(1)} %get-tuple-element.34), channel_id=1, source_target_pairs={{8,16},{24,32},{40,48},{56,64},{72,80},{88,96},{104,112},{120,128}... | collective-permute-start | bytes 49160 | tf_op jit(solution)/shard_map/ppermute | solution.py:278
  65.0 7.2 %collective-permute-start.7 = (bf16[4,352,128]{2,1,0:T(8,128)(2,1)S(1)}, bf16[4,352,128]{2,1,0:T(8,128)(2,1)S(1)}, u32[]{:S(2)}, u32[]{:S(2)}) collective-permute-start(bf16[4,352,128]{2,1,0:T(8,128)(2,1)S(1)} %get-tuple-element.35), channel_id=1, source_target_pairs={{0,1},{1,0},{2,3},{3,2},{4,5},{5,4},{6,7},{7,6},{8,9},{9,8},{10,11... | collective-permute-start | bytes 1081352 | tf_op jit(solution)/shard_map/ppermute | solution.py:282
  68.1 1.6 %copy-start.2 = (bf16[1,8,320,128]{3,2,1,0:T(8,128)(2,1)S(1)}, bf16[1,8,320,128]{3,2,1,0:T(8,128)(2,1)}, u32[]{:S(2)}) copy-start(bf16[1,8,320,128]{3,2,1,0:T(8,128)(2,1)} %param.13) | copy-start | bytes 1966084
  72.2 3.0 %copy-start.3 = (bf16[3,3,3,128,128]{4,3,2,1,0:T(8,128)(2,1)S(1)}, bf16[3,3,3,128,128]{4,3,2,1,0:T(8,128)(2,1)}, u32[]{:S(2)}) copy-start(bf16[3,3,3,128,128]{4,3,2,1,0:T(8,128)(2,1)} %weight.13) | copy-start | bytes 2654212
  73.2 4.4 %collective-permute-start.8 = (bf16[10,352,128]{2,1,0:T(8,128)(2,1)S(1)}, bf16[10,352,128]{2,1,0:T(8,128)(2,1)S(1)}, u32[]{:S(2)}, u32[]{:S(2)}) collective-permute-start(bf16[10,352,128]{2,1,0:T(8,128)(2,1)S(1)} %get-tuple-element.43), channel_id=1, source_target_pairs={{0,1},{1,0},{2,3},{3,2},{4,5},{5,4},{6,7},{7,6},{8,9},{9,8},{10,11... | collective-permute-start | bytes 2703368 | tf_op jit(solution)/shard_map/ppermute | solution.py:282

commit v4 on v3

--- a/solution.py
+++ b/solution.py
@@ -8,18 +8,19 @@
 from jax.sharding import PartitionSpec as P
 
 B = 16
+E = B // 2
 BF = jnp.bfloat16
 F32 = jnp.float32
 VMEM = pl.BlockSpec(memory_space=pltpu.VMEM)
 HBM = pl.BlockSpec(memory_space=pltpu.HBM)
 
 
-def call(body, outs, specs, scratch=(), flops=0, nbytes=0, limit=24):
+def call(body, outs, specs, scratch=(), flops=0, nbytes=0, limit=24, out_specs=None):
     run = pl.pallas_call(
         body,
         out_shape=[jax.ShapeDtypeStruct(s, d) for s, d in outs],
         in_specs=specs,
-        out_specs=[VMEM] * len(outs),
+        out_specs=out_specs or [VMEM] * len(outs),
         scratch_shapes=list(scratch),
         cost_estimate=pl.CostEstimate(flops=flops, bytes_accessed=nbytes, transcendentals=0),
         compiler_params=pltpu.CompilerParams(vmem_limit_bytes=int(limit * 1024 * 1024)),
@@ -59,16 +60,16 @@
     crows, ccols, _ = latent.shape
     copies = [(latent, latent_v), (weight, weight_v), (bias, bias_v)]
     n_first = len(copies)
-    n_c1 = rows * B
-    n_c2 = (rows + crows) * B
+    n_c1 = rows * E
+    n_c2 = (rows + crows) * E
     t0 = 2 * cols + ccols
     sends = ((row_0, col_0, False), (row_1, col_1, True))
     for row_s, col_s, flip in sends:
-        lo, hi = (cols - B, 0) if flip else (0, cols - B)
-        c = pl.ds(pick("col", hi, lo, B), B)
+        lo, hi = (cols - E, 0) if flip else (0, cols - E)
+        c = pl.ds(pick("col", hi, lo, E), E)
         for i in range(rows):
-            copies.append((one.at[i, c], col_s.at[i * B : (i + 1) * B]))
-            copies.append((two.at[i, c], col_s.at[n_c2 + i * B : n_c2 + (i + 1) * B]))
+            copies.append((one.at[i, c], col_s.at[i * E : (i + 1) * E]))
+            copies.append((two.at[i, c], col_s.at[n_c2 + i * E : n_c2 + (i + 1) * E]))
         lo, hi = (rows - 2, 0) if flip else (0, rows - 2)
         r = pick("row", hi, lo)
         for k in range(2):
@@ -89,19 +90,22 @@
     for row_s, col_s, flip in sends:
         lo, hi = (crows - 1, 0) if flip else (0, crows - 1)
         row_s[2 * cols : t0, :] = act[pick("row", hi, lo)]
-        lo, hi = (ccols - B, 0) if flip else (0, ccols - B)
-        c = pl.ds(pick("col", hi, lo, B), B)
+        lo, hi = (ccols - E, 0) if flip else (0, ccols - E)
+        c = pl.ds(pick("col", hi, lo, E), E)
         for i in range(crows):
-            col_s[n_c1 + i * B : n_c1 + (i + 1) * B, :] = act[i, c, :]
+            col_s[n_c1 + i * E : n_c1 + (i + 1) * E, :] = act[i, c, :]
     for c in started[n_first:]:
         c.wait()
 
 
-def corner_kernel(rows, crows, got_0, got_1, merged, cor_0, cor_1):
-    take_0 = low_half() == even("col")
+def corner_kernel(rows, crows, got_0, got_1, merged, act_edge, cor_0, cor_1):
+    is_even = even("col")
     for i in range(2 * rows + crows):
-        s = slice(i * B, (i + 1) * B)
-        merged[s, :] = jnp.where(take_0, got_0[s, :].astype(F32), got_1[s, :].astype(F32)).astype(BF)
+        x, y = (g[i * E : (i + 1) * E, :].astype(F32) for g in (got_0, got_1))
+        both = jnp.concatenate([jnp.where(is_even, x, y), jnp.where(is_even, y, x)], axis=0)
+        merged[i * B : (i + 1) * B, :] = both.astype(BF)
+        if rows <= i < rows + crows:
+            act_edge[(i - rows) * B : (i - rows + 1) * B, :] = spread_edge(both)
     lows = (0, 1, rows, rows + crows)
     highs = (rows - 2, rows - 1, rows + crows - 1, 2 * rows + crows - 1)
     for k, (lo, hi) in enumerate(zip(lows, highs)):
@@ -151,41 +155,47 @@
 
 
 def joined(core, border):
-    n = core.shape[0]
-    return lambda i: border[i] if i < 2 else core[i - 2] if i < n + 2 else border[i - n]
-
-
-def fill_kernel(one, act, merged, cache_core, act_core, send):
+    core, n = core
+    return lambda i: border(i) if i < 2 else core(i - 2) if i < n + 2 else border(i - n)
+
+
+def framed(tile, edges, first=0, each=1):
+    def row(i):
+        i = i // each
+        e = edges[first + i * B : first + (i + 1) * B, :]
+        return jnp.concatenate([e, tile[i], e], axis=0)
+
+    return row, tile.shape[0] * each
+
+
+def fill_kernel(one, act, act_up, send):
     rows, cols, _ = one.shape
     crows, ccols, _ = act.shape
-    for i in range(rows):
-        put_row(cache_core, i, one[i], merged[i * B : (i + 1) * B, :])
     spread = spread_matrix(cols, ccols)
     for m in range(0, crows, 2):
         wide = jnp.dot(spread, jnp.concatenate([act[m], act[m + 1]], axis=1), preferred_element_type=F32).astype(BF)
         for h in range(2):
-            edges = spread_edge(block(merged, rows + m + h))
-            for i in range(2):
-                put_row(act_core, 2 * (m + h) + i, wide[:, h * 128 : (h + 1) * 128], edges)
-    choose(send, act_core, cache_core)
-
-
-def choose(send, leading, other):
-    for first, src in ((True, leading), (False, other)):
-
-        @pl.when((lax.axis_index("frm") == 0) == first)
-        def _(src=src):
-            send[...] = src[...]
-
-
-def inner_kernel(cache_core, act_core, weight, part, sums):
-    frames = (lambda i: cache_core[i - 2], lambda i: act_core[i - 2])
+            act_up[m + h] = wide[:, h * 128 : (h + 1) * 128]
+    lead = lax.axis_index("frm") == 0
+
+    @pl.when(lead)
+    def _():
+        for i in range(rows):
+            send[i] = act_up[i // 2]
+
+    @pl.when(jnp.logical_not(lead))
+    def _():
+        send[...] = one[...]
+
+
+def inner_kernel(one, act_up, merged, act_edge, weight, part, sums):
+    frames = [joined(f, None) for f in (framed(one, merged), framed(act_up, act_edge, each=2))]
     for n, k in enumerate(range(2, 2 + part.shape[0], 2)):
         for h, v in enumerate(conv_rows(frames, (0, 2), weight, k, sums, n % 2)):
             part[k - 2 + h] = v
 
 
-def border_kernel(row_0, row_1, cor_0, cor_1, cache_border, act_border, send):
+def border_kernel(row_0, row_1, cor_0, cor_1, merged, act_edge, cache_border, act_border, send):
     _, span, _ = cache_border.shape
     cols = span - 2 * B
     ccols = row_0.shape[0] - 3 * cols
@@ -197,17 +207,36 @@
             coarse = jnp.concatenate([row[2 * cols : 2 * cols + ccols, :] for row, _ in pairs], axis=1)
             wide = jnp.dot(spread_matrix(cols, ccols), coarse, preferred_element_type=F32).astype(BF)
             for h, (row, cor) in enumerate(pairs):
-                edges = spread_edge(block(cor, 2))
                 for k in range(2):
                     put_row(cache_border, 2 * h + k, row[k * cols : (k + 1) * cols, :], cor[k * B : (k + 1) * B, :])
-                    put_row(act_border, 2 * h + k, wide[:, h * 128 : (h + 1) * 128], edges)
-
-    choose(send, act_border, cache_border)
-
-
-def outer_kernel(cache_core, act_core, cache_border, act_border, weight, two, merged, row_0, row_1, cor_0, cor_1, part, two_frame, sums, *, first):
+                put_row(act_border, h, wide[:, h * 128 : (h + 1) * 128], spread_edge(block(cor, 2)))
+
+    lead = lax.axis_index("frm") == 0
+    n_edge = send.shape[0] - 4 * span
+
+    @pl.when(lead)
+    def _():
+        for i in range(4):
+            send[i * span : (i + 1) * span, :] = act_border[i // 2]
+        for i in range(n_edge // B):
+            send[4 * span + i * B : 4 * span + (i + 1) * B, :] = act_edge[i // 2 * B : (i // 2 + 1) * B, :]
+
+    @pl.when(jnp.logical_not(lead))
+    def _():
+        for i in range(4):
+            send[i * span : (i + 1) * span, :] = cache_border[i]
+        send[4 * span :, :] = merged[0:n_edge, :]
+
+
+def outer_kernel(
+    one, act_up, merged, act_edge, cache_border, act_border, weight, two, row_0, row_1, cor_0, cor_1,
+    part, two_frame, sums, *, first,
+):
     rows, cols, _ = two.shape
-    frames = (joined(cache_core, cache_border), joined(act_core, act_border))
+    frames = (
+        joined(framed(one, merged), lambda i: cache_border[i]),
+        joined(framed(act_up, act_edge, each=2), lambda i: act_border[i // 2]),
+    )
     for n, k in enumerate((0, rows)):
         for h, v in enumerate(conv_rows(frames, (0, 2), weight, k, sums, n)):
             part[2 * n + h] = v
@@ -237,21 +266,19 @@
     out[i, span - B :, :] = jnp.where(keep_right, v[span - B :], 0.0).astype(BF)
 
 
-def middle_inner_kernel(core, part, weight, bias, out, sums):
-    n = out.shape[0]
-    for m in range(0, n, 2):
-        for h, v in enumerate(conv_rows((lambda i: core[i - 2],), (1,), weight, m + 2, sums, m // 2 % 2)):
-            finish_row(out, m + h, v + part[m + h] + bias[...], m + h + 2, n + 4)
-
-
-def middle_outer_kernel(core, border, part, weight, bias, inner, two_frame, out, send, sums):
-    n_out = out.shape[0]
-    frame = joined(core, border)
-    for n, k in enumerate((0, n_out - 2)):
-        for h, v in enumerate(conv_rows((frame,), (1,), weight, k, sums, n)):
-            finish_row(out, k + h, v + part[2 * n + h] + bias[...], k + h, n_out)
-    out[2 : n_out - 2] = inner[...]
-    choose(send, out, two_frame)
+def middle_kernel(core, border, part_in, part_out, weight, bias, two_frame, out, send, sums):
+    n_out, span, _ = out.shape
+    frame = joined(framed(core, border, 4 * span), lambda i: border[i * span : (i + 1) * span, :])
+    for k in range(0, n_out, 2):
+        for h, v in enumerate(conv_rows((frame,), (1,), weight, k, sums, k // 2 % 2)):
+            i = k + h
+            part = part_in[i - 2] if 2 <= i < n_out - 2 else part_out[i if i < 2 else i - n_out + 4]
+            finish_row(out, i, v + part + bias[...], i, n_out)
+    for first, src in ((True, out), (False, two_frame)):
+
+        @pl.when((lax.axis_index("frm") == 0) == first)
+        def _(src=src):
+            send[...] = src[...]
 
 
 def own_two_kernel(two_frame, act_two, weight, proj, bias, part, sums):
@@ -266,11 +293,16 @@
             part[k + h] = v[B : B + cols] + base
 
 
-def middle_two_kernel(middle, part, weight, out, sums):
-    n_out, cols, _ = out.shape
+def middle_two_kernel(middle, part, weight, out, sums, done, sems):
+    n_out, cols, _ = done.shape
+    copies = []
     for k in range(0, n_out, 2):
         for h, v in enumerate(conv_rows((lambda i: middle[i],), (1,), weight, k, sums, k // 2 % 2)):
-            out[k + h] = (part[k + h] + v[B : B + cols]).astype(BF)
+            done[k + h] = (part[k + h] + v[B : B + cols]).astype(BF)
+        copies.append(pltpu.make_async_copy(done.at[k : k + 2], out.at[k : k + 2], sems.at[k // 2]))
+        copies[-1].start()
+    for c in copies:
+        c.wait()
 
 
 def exchange(x, axis, first):
@@ -288,6 +320,7 @@
     crows, ccols, lch = latent.shape
     span = cols + 2 * B
     n_edge = (2 * rows + crows) * B
+    n_send = (2 * rows + crows) * E
     n_row = 3 * cols + ccols
     sums = pltpu.VMEM((4, span + 16, 2 * ch), F32)
     proj, act, row_0, row_1, col_0, col_1, b_one, b_two = call(
@@ -297,8 +330,8 @@
             ((crows, ccols, ch), BF),
             ((n_row, ch), BF),
             ((n_row, ch), BF),
-            ((n_edge, ch), BF),
-            ((n_edge, ch), BF),
+            ((n_send, ch), BF),
+            ((n_send, ch), BF),
             ((1, ch), F32),
             ((1, ch), F32),
         ],
@@ -317,53 +350,54 @@
     got_0 = exchange(col_0, "col", 0)
     row_1 = exchange(row_1, "row", 1)
     row_0 = exchange(row_0, "row", 0)
-    merged, cor_0, cor_1 = call(
+    third = 2 * 9 * ch * ch * rows * cols
+    act_up, send_core = call(
+        fill_kernel, [((crows, cols, ch), BF), ((rows, cols, ch), BF)], [VMEM] * 2, flops=10**8, nbytes=4 * 10**6
+    )(one, act)
+    middle_core = swap(send_core)
+    merged, act_edge, cor_0, cor_1 = call(
         functools.partial(corner_kernel, rows, crows),
-        [((n_edge, ch), BF), ((4 * B, ch), BF), ((4 * B, ch), BF)],
+        [((n_edge, ch), BF), ((crows * B, ch), BF), ((4 * B, ch), BF), ((4 * B, ch), BF)],
         [VMEM] * 2,
         flops=10**6,
         nbytes=2 * 10**5,
     )(got_0, got_1)
+    cor_0 = exchange(cor_0, "row", 0)
     cor_1 = exchange(cor_1, "row", 1)
-    cor_0 = exchange(cor_0, "row", 0)
-    third = 2 * 9 * ch * ch * rows * cols
-    core_shape, border_shape = ((rows, span, ch), BF), ((4, span, ch), BF)
-    cache_core, act_core, send_core = call(
-        fill_kernel, [core_shape] * 3, [VMEM] * 3, flops=10**8, nbytes=4 * 10**6
-    )(one, act, merged)
-    middle_core = swap(send_core)
     (part_in,) = call(
-        inner_kernel, [((rows - 2, span, ch), F32)], [VMEM] * 3, scratch=[sums], flops=2 * third, nbytes=4 * 10**6
-    )(cache_core, act_core, conv_one)
+        inner_kernel, [((rows - 2, span, ch), F32)], [VMEM] * 5, scratch=[sums], flops=2 * third, nbytes=4 * 10**6
+    )(one, act_up, merged, act_edge, conv_one)
     cache_border, act_border, send_border = call(
-        border_kernel, [border_shape] * 3, [VMEM] * 4, flops=10**8, nbytes=4 * 10**6
-    )(row_0, row_1, cor_0, cor_1)
+        border_kernel,
+        [((4, span, ch), BF), ((2, span, ch), BF), ((4 * span + rows * B, ch), BF)],
+        [VMEM] * 6,
+        flops=10**8,
+        nbytes=4 * 10**6,
+    )(row_0, row_1, cor_0, cor_1, merged, act_edge)
     middle_border = swap(send_border)
     part_out, two_frame = call(
         functools.partial(outer_kernel, first=rows + crows),
         [((4, span, ch), F32), ((rows + 2, span, ch), BF)],
-        [VMEM] * 11,
+        [VMEM] * 12,
         scratch=[sums],
         flops=third,
         nbytes=4 * 10**6,
-    )(cache_core, act_core, cache_border, act_border, conv_one, two, merged, row_0, row_1, cor_0, cor_1)
-    (act_inner,) = call(
-        middle_inner_kernel, [((rows - 2, span, ch), BF)], [VMEM] * 4, scratch=[sums], flops=third, nbytes=6 * 10**6
-    )(middle_core, part_in, conv_one, b_one)
+    )(one, act_up, merged, act_edge, cache_border, act_border, conv_one, two, row_0, row_1, cor_0, cor_1)
     act_two, send_two = call(
-        middle_outer_kernel,
-        [((rows + 2, span, ch), BF)] * 2,
-        [VMEM] * 7,
-        scratch=[sums],
-        flops=third // 2,
-        nbytes=6 * 10**6,
-    )(middle_core, middle_border, part_out, conv_one, b_one, act_inner, two_frame)
+        middle_kernel, [((rows + 2, span, ch), BF)] * 2, [VMEM] * 7, scratch=[sums], flops=third, nbytes=6 * 10**6
+    )(middle_core, middle_border, part_in, part_out, conv_one, b_one, two_frame)
     middle_two = swap(send_two)
     (part_two,) = call(
         own_two_kernel, [((rows, cols, ch), F32)], [VMEM] * 5, scratch=[sums], flops=2 * third, nbytes=6 * 10**6
     )(two_frame, act_two, conv_two, proj, b_two)
     (decoded,) = call(
-        middle_two_kernel, [((rows, cols, ch), BF)], [VMEM] * 3, scratch=[sums], flops=third, nbytes=6 * 10**6
+        middle_two_kernel,
+        [((rows, cols, ch), BF)],
+        [VMEM] * 3,
+        scratch=[sums, pltpu.VMEM((rows, cols, ch), BF), pltpu.SemaphoreType.DMA((rows // 2,))],
+        out_specs=[HBM],
+        flops=third,
+        nbytes=6 * 10**6,
     )(middle_two, part_two, conv_two)
     return decoded[None]
 

time: 80.1 us -> 77.9 us (0.973)
  starting transfers between devices: 62.7 us -> 61.6 us
  waiting for transfers between devices: 5.11 us -> 4.17 us
    ppermute x6, starting transfers between devices: 53.9 us -> 52.2 us  [exchange(): return lax.ppermute(x, axis, pairs + [(j, i) for i, j in pairs])]
    ppermute x6, waiting for transfers between devices: 4.86 us -> 3.92 us  [exchange(): return lax.ppermute(x, axis, pairs + [(j, i) for i, j in pairs])]
    pallas_call x10 -> x9, Pallas kernels: 11.7 us -> 11.6 us  [call(): run(*(held(v, spec) for v, spec in zip(args, specs, strict=True)))]
  transfers between devices with their start and end apart: 9 -> 9, of which waited for: 4 -> 3; matrix products, arithmetic and copies ran while one was open for 0% -> 0% of each run, Pallas kernels for 8% -> 7%
where the time goes in v4:
time: 77.9 us; the launch traced here: 77.6 us
  starting transfers between devices  61.6 us (79%)
  Pallas kernels  11.6 us (15%)
  waiting for transfers between devices  4.17 us (5%)
    ppermute x6, starting transfers between devices, exchange(): return lax.ppermute(x, axis, pairs + [(j, i) for i, j in pairs])  52.2 us
    pallas_call x9, Pallas kernels, call(): run(*(held(v, spec) for v, spec in zip(args, specs, strict=True)))  11.6 us
    ppermute x3, starting transfers between devices, swap(): return lax.ppermute(x, 'frm', [(0, 1), (1, 0)])  9.37 us
    ppermute x6, waiting for transfers between devices, exchange(): return lax.ppermute(x, axis, pairs + [(j, i) for i, j in pairs])  3.92 us
  transfers between devices with their start and end apart: 9, of which 3 were waited for; matrix products, arithmetic and copies ran while one was open for 0% of the time, Pallas kernels for 7%

profile of v4, /device:TPU:99, one launch (start us, length us, event | category | flops | bytes accessed | tf_op | source)
XLA Modules:
  0.0 77.6 jit_solution(4899136547817316664)
XLA Ops:
  0.0 1.8 %shard_map.91 = (bf16[4,160,128]{2,1,0:T(8,128)(2,1)S(1)}, bf16[4,160,128]{2,1,0:T(8,128)(2,1)S(1)}, bf16[1120,128]{1,0:T(8,128)(2,1)S(1)}, bf16[1120,128]{1,0:T...) custom-call(bf16[4,160,256]{2,1,0:T(8,128)(2,1)} %bitcast.13, ...), custom_call_target="tpu_custom_call" | custom-call | flops 100000000 | bytes 2000000 | tf_op jit(solution)/shard_map/pallas_call | solution.py:29
  1.9 2.0 %collective-permute-start.1 = (bf16[1120,128]{1,0:T(8,128)(2,1)S(1)}, bf16[1120,128]{1,0:T(8,128)(2,1)S(1)}, u32[]{:S(2)}, u32[]{:S(2)}) collective-permute-start(bf16[1120,128]{1,0:T(8,128)(2,1)S(1)} %get-tuple-element.28), channel_id=1, source_target_pairs={{0,8},{16,24},{32,40},{48,56},{64,72},{80,88},{96,104},{112,120},{... | collective-permute-start | bytes 860168 | tf_op jit(solution)/shard_map/ppermute | solution.py:310
  3.8 6.9 %collective-permute-start.2 = (bf16[1120,128]{1,0:T(8,128)(2,1)S(1)}, bf16[1120,128]{1,0:T(8,128)(2,1)S(1)}, u32[]{:S(2)}, u32[]{:S(2)}) collective-permute-start(bf16[1120,128]{1,0:T(8,128)(2,1)S(1)} %get-tuple-element.29), channel_id=1, source_target_pairs={{8,16},{24,32},{40,48},{56,64},{72,80},{88,96},{104,112},{120,128}... | collective-permute-start | bytes 860168 | tf_op jit(solution)/shard_map/ppermute | solution.py:310
  10.7 0.0 copy-done
  10.8 0.3 shard_map.92
  11.0 3.1 %collective-permute-start = (bf16[8,320,128]{2,1,0:T(8,128)(2,1)S(1)}, bf16[8,320,128]{2,1,0:T(8,128)(2,1)S(1)}, u32[]{:S(2)}, u32[]{:S(2)}) collective-permute-start(bf16[8,320,128]{2,1,0:T(8,128)(2,1)S(1)} %get-tuple-element.27), channel_id=1, source_target_pairs={{0,1},{1,0},{2,3},{3,2},{4,5},{5,4},{6,7},{7,6},{8,9},{9,8},{10,11... | collective-permute-start | bytes 1966088 | tf_op jit(solution)/shard_map/ppermute | solution.py:314
  14.2 35.8 %collective-permute-start.3 = (bf16[160,128]{1,0:T(8,128)(2,1)S(1)}, bf16[160,128]{1,0:T(8,128)(2,1)S(1)}, u32[]{:S(2)}, u32[]{:S(2)}) collective-permute-start(bf16[160,128]{1,0:T(8,128)(2,1)S(1)} %get-tuple-element.30), channel_id=1, source_target_pairs={{0,2},{4,6},{2,0},{6,4},{1,3},{5,7},{3,1},{7,5},{8,10},{12,14},{10... | collective-permute-start | bytes 122888 | tf_op jit(solution)/shard_map/ppermute | solution.py:310
  50.0 2.0 %collective-permute-start.4 = (bf16[160,128]{1,0:T(8,128)(2,1)S(1)}, bf16[160,128]{1,0:T(8,128)(2,1)S(1)}, u32[]{:S(2)}, u32[]{:S(2)}) collective-permute-start(bf16[160,128]{1,0:T(8,128)(2,1)S(1)} %get-tuple-element.31), channel_id=1, source_target_pairs={{2,4},{4,2},{3,5},{5,3},{10,12},{12,10},{11,13},{13,11},{18,20},{2... | collective-permute-start | bytes 122888 | tf_op jit(solution)/shard_map/ppermute | solution.py:310
  51.9 0.0 collective-permute-done.3.got_0
  51.9 2.8 %collective-permute-done.4.got_1 = bf16[160,128]{1,0:T(8,128)(2,1)S(1)} collective-permute-done((bf16[160,128]{1,0:T(8,128)(2,1)S(1)}, bf16[160,128]{1,0:T(8,128)(2,1)S(1)}, u32[]{:S(2)}, u32[]{:S(2)}) %collective-permute-start.4) | collective-permute-done | bytes 40992 | tf_op jit(solution)/shard_map/ppermute | solution.py:310
  54.8 2.0 %collective-permute-start.5 = (bf16[64,128]{1,0:T(8,128)(2,1)S(1)}, bf16[64,128]{1,0:T(8,128)(2,1)S(1)}, u32[]{:S(2)}, u32[]{:S(2)}) collective-permute-start(bf16[64,128]{1,0:T(8,128)(2,1)S(1)} %get-tuple-element.32), channel_id=1, source_target_pairs={{0,8},{16,24},{32,40},{48,56},{64,72},{80,88},{96,104},{112,120},{... | collective-permute-start | bytes 49160 | tf_op jit(solution)/shard_map/ppermute | solution.py:310
  56.7 3.7 %collective-permute-start.6 = (bf16[64,128]{1,0:T(8,128)(2,1)S(1)}, bf16[64,128]{1,0:T(8,128)(2,1)S(1)}, u32[]{:S(2)}, u32[]{:S(2)}) collective-permute-start(bf16[64,128]{1,0:T(8,128)(2,1)S(1)} %get-tuple-element.33), channel_id=1, source_target_pairs={{8,16},{24,32},{40,48},{56,64},{72,80},{88,96},{104,112},{120,128}... | collective-permute-start | bytes 49160 | tf_op jit(solution)/shard_map/ppermute | solution.py:310
  60.4 0.0 collective-permute-done.5.cor_0
  60.4 1.1 %collective-permute-done.6.cor_1 = bf16[64,128]{1,0:T(8,128)(2,1)S(1)} collective-permute-done((bf16[64,128]{1,0:T(8,128)(2,1)S(1)}, bf16[64,128]{1,0:T(8,128)(2,1)S(1)}, u32[]{:S(2)}, u32[]{:S(2)}) %collective-permute-start.6) | collective-permute-done | bytes 16416 | tf_op jit(solution)/shard_map/ppermute | solution.py:310
  61.5 0.0 collective-permute-done.1.row_0
  61.5 0.0 collective-permute-done.2.row_1
  61.5 0.2 shard_map.94
  61.8 4.3 %collective-permute-start.7 = (bf16[1536,128]{1,0:T(8,128)(2,1)S(1)}, bf16[1536,128]{1,0:T(8,128)(2,1)S(1)}, u32[]{:S(2)}, u32[]{:S(2)}) collective-permute-start(bf16[1536,128]{1,0:T(8,128)(2,1)S(1)} %get-tuple-element.36), channel_id=1, source_target_pairs={{0,1},{1,0},{2,3},{3,2},{4,5},{5,4},{6,7},{7,6},{8,9},{9,8},{10,11... | collective-permute-start | bytes 1179656 | tf_op jit(solution)/shard_map/ppermute | solution.py:314
  66.0 0.0 copy-done.1
  66.1 0.0 copy-start.2
  66.1 1.6 %shard_map.95.part_in = f32[6,352,128]{2,1,0:T(8,128)S(1)} custom-call(bf16[8,320,128]{2,1,0:T(8,128)(2,1)S(1)} %bitcast.9, bf16[4,320,128]{2,1,0:T(8,128)(2,1)S(1)} %get-tuple-element.37.act_up, bf16[320,128]{1,0:T(8,128)(2,1)S(1)} %get-tuple-element.34.merged, bf16[64,128]{1,0:T(8,128)(2,1)S(1)} %get-tuple-element.35.act_edge, ...), custom_call_target="tpu_custom_call" | custom-call | flops 1509949440 | bytes 4000000 | tf_op jit(solution)/shard_map/pallas_call | solution.py:29
  67.7 0.0 copy-done.2
  67.7 1.2 %shard_map.96 = (f32[4,352,128]{2,1,0:T(8,128)S(1)}, bf16[10,352,128]{2,1,0:T(8,128)(2,1)S(1)}) custom-call(bf16[8,320,128]{2,1,0:T(8,128)(2,1)S(1)} %bitcast.10, bf16[4,320,128]{2,1,0:T(8,128)(2,1)S(1)} %get-tuple-element.37.act_up, bf16[320,128]{1,0:T(8,128)(2,1)S(1)} %get-tuple-element.34.merged, bf16[64,128]{1,0:T(8,128)(2,1)S(1)} %get-tuple-element.35.act_edge, ...), custom_call_target="tpu_custom_call" | custom-call | flops 754974720 | bytes 4000000 | tf_op jit(solution)/shard_map/pallas_call | solution.py:29
  68.9 0.0 collective-permute-done.core
  68.9 0.0 collective-permute-done.7.border
  68.9 0.0 copy-start.3
  68.9 2.3 %shard_map.97 = (bf16[10,352,128]{2,1,0:T(8,128)(2,1)S(1)}, bf16[10,352,128]{2,1,0:T(8,128)(2,1)S(1)}) custom-call(bf16[8,320,128]{2,1,0:T(8,128)(2,1)S(1)} %collective-permute-done.core, bf16[1536,128]{1,0:T(8,128)(2,1)S(1)} %collective-permute-done.7.border, f32[6,352,128]{2,1,0:T(8,128)S(1)} %shard_map.95.part_in, ...), custom_call_target="tpu_custom_call" | custom-call | flops 754974720 | bytes 6000000 | tf_op jit(solution)/shard_map/pallas_call | solution.py:29
  71.2 2.0 %collective-permute-start.8 = (bf16[10,352,128]{2,1,0:T(8,128)(2,1)S(1)}, bf16[10,352,128]{2,1,0:T(8,128)(2,1)S(1)}, u32[]{:S(2)}, u32[]{:S(2)}) collective-permute-start(bf16[10,352,128]{2,1,0:T(8,128)(2,1)S(1)} %get-tuple-element.43), channel_id=1, source_target_pairs={{0,1},{1,0},{2,3},{3,2},{4,5},{5,4},{6,7},{7,6},{8,9},{9,8},{10,11... | collective-permute-start | bytes 2703368 | tf_op jit(solution)/shard_map/ppermute | solution.py:314
  73.2 0.0 copy-done.3
  73.2 2.2 %shard_map.98.part = f32[8,320,128]{2,1,0:T(8,128)S(1)} custom-call(bf16[10,352,128]{2,1,0:T(8,128)(2,1)S(1)} %get-tuple-element.42.two_frame, bf16[10,352,128]{2,1,0:T(8,128)(2,1)S(1)} %get-tuple-element.44.act_two, bf16[3,3,3,128,128]{4,3,2,1,0:T(8,128)(2,1)S(1)} %copy-done.3, bf16[4,160,128]{2,1,0:T(8,128)(2,1)S(1)} %get-tuple-element.45.proj, ...), custom_call_target="tpu_custom_call" | custom-call | flops 1509949440 | bytes 6000000 | tf_op jit(solution)/shard_map/pallas_call | solution.py:29
  75.3 0.2 collective-permute-done.8.middle
  75.6 2.0 %shard_map.99 = bf16[8,320,128]{2,1,0:T(8,128)(2,1)} custom-call(bf16[10,352,128]{2,1,0:T(8,128)(2,1)S(1)} %collective-permute-done.8.middle, f32[8,320,128]{2,1,0:T(8,128)S(1)} %shard_map.98.part, bf16[3,3,3,128,128]{4,3,2,1,0:T(8,128)(2,1)S(1)} %copy-done.3), custom_call_target="tpu_custom_call" | custom-call | flops 754974720 | bytes 6000000 | tf_op jit(solution)/shard_map/pallas_call | solution.py:29
  (3 shorter events, 0.0 us)
Async XLA Ops:
  0.0 10.7 %copy-start = (bf16[1,8,320,128]{3,2,1,0:T(8,128)(2,1)S(1)}, bf16[1,8,320,128]{3,2,1,0:T(8,128)(2,1)}, u32[]{:S(2)}) copy-start(bf16[1,8,320,128]{3,2,1,0:T(8,128)(2,1)} %param.12) | copy-start | bytes 1966084
  0.0 66.0 %copy-start.1 = (bf16[3,3,3,128,128]{4,3,2,1,0:T(8,128)(2,1)S(1)}, bf16[3,3,3,128,128]{4,3,2,1,0:T(8,128)(2,1)}, u32[]{:S(2)}) copy-start(bf16[3,3,3,128,128]{4,3,2,1,0:T(8,128)(2,1)} %weight.9) | copy-start | bytes 2654212
  1.9 59.7 %collective-permute-start.1 = (bf16[1120,128]{1,0:T(8,128)(2,1)S(1)}, bf16[1120,128]{1,0:T(8,128)(2,1)S(1)}, u32[]{:S(2)}, u32[]{:S(2)}) collective-permute-start(bf16[1120,128]{1,0:T(8,128)(2,1)S(1)} %get-tuple-element.28), channel_id=1, source_target_pairs={{0,8},{16,24},{32,40},{48,56},{64,72},{80,88},{96,104},{112,120},{... | collective-permute-start | bytes 860168 | tf_op jit(solution)/shard_map/ppermute | solution.py:310
  3.8 57.7 %collective-permute-start.2 = (bf16[1120,128]{1,0:T(8,128)(2,1)S(1)}, bf16[1120,128]{1,0:T(8,128)(2,1)S(1)}, u32[]{:S(2)}, u32[]{:S(2)}) collective-permute-start(bf16[1120,128]{1,0:T(8,128)(2,1)S(1)} %get-tuple-element.29), channel_id=1, source_target_pairs={{8,16},{24,32},{40,48},{56,64},{72,80},{88,96},{104,112},{120,128}... | collective-permute-start | bytes 860168 | tf_op jit(solution)/shard_map/ppermute | solution.py:310
  11.0 57.9 %collective-permute-start = (bf16[8,320,128]{2,1,0:T(8,128)(2,1)S(1)}, bf16[8,320,128]{2,1,0:T(8,128)(2,1)S(1)}, u32[]{:S(2)}, u32[]{:S(2)}) collective-permute-start(bf16[8,320,128]{2,1,0:T(8,128)(2,1)S(1)} %get-tuple-element.27), channel_id=1, source_target_pairs={{0,1},{1,0},{2,3},{3,2},{4,5},{5,4},{6,7},{7,6},{8,9},{9,8},{10,11... | collective-permute-start | bytes 1966088 | tf_op jit(solution)/shard_map/ppermute | solution.py:314
  14.2 37.7 %collective-permute-start.3 = (bf16[160,128]{1,0:T(8,128)(2,1)S(1)}, bf16[160,128]{1,0:T(8,128)(2,1)S(1)}, u32[]{:S(2)}, u32[]{:S(2)}) collective-permute-start(bf16[160,128]{1,0:T(8,128)(2,1)S(1)} %get-tuple-element.30), channel_id=1, source_target_pairs={{0,2},{4,6},{2,0},{6,4},{1,3},{5,7},{3,1},{7,5},{8,10},{12,14},{10... | collective-permute-start | bytes 122888 | tf_op jit(solution)/shard_map/ppermute | solution.py:310
  50.0 4.8 %collective-permute-start.4 = (bf16[160,128]{1,0:T(8,128)(2,1)S(1)}, bf16[160,128]{1,0:T(8,128)(2,1)S(1)}, u32[]{:S(2)}, u32[]{:S(2)}) collective-permute-start(bf16[160,128]{1,0:T(8,128)(2,1)S(1)} %get-tuple-element.31), channel_id=1, source_target_pairs={{2,4},{4,2},{3,5},{5,3},{10,12},{12,10},{11,13},{13,11},{18,20},{2... | collective-permute-start | bytes 122888 | tf_op jit(solution)/shard_map/ppermute | solution.py:310
  54.8 5.6 %collective-permute-start.5 = (bf16[64,128]{1,0:T(8,128)(2,1)S(1)}, bf16[64,128]{1,0:T(8,128)(2,1)S(1)}, u32[]{:S(2)}, u32[]{:S(2)}) collective-permute-start(bf16[64,128]{1,0:T(8,128)(2,1)S(1)} %get-tuple-element.32), channel_id=1, source_target_pairs={{0,8},{16,24},{32,40},{48,56},{64,72},{80,88},{96,104},{112,120},{... | collective-permute-start | bytes 49160 | tf_op jit(solution)/shard_map/ppermute | solution.py:310
  56.7 4.8 %collective-permute-start.6 = (bf16[64,128]{1,0:T(8,128)(2,1)S(1)}, bf16[64,128]{1,0:T(8,128)(2,1)S(1)}, u32[]{:S(2)}, u32[]{:S(2)}) collective-permute-start(bf16[64,128]{1,0:T(8,128)(2,1)S(1)} %get-tuple-element.33), channel_id=1, source_target_pairs={{8,16},{24,32},{40,48},{56,64},{72,80},{88,96},{104,112},{120,128}... | collective-permute-start | bytes 49160 | tf_op jit(solution)/shard_map/ppermute | solution.py:310
  61.8 7.1 %collective-permute-start.7 = (bf16[1536,128]{1,0:T(8,128)(2,1)S(1)}, bf16[1536,128]{1,0:T(8,128)(2,1)S(1)}, u32[]{:S(2)}, u32[]{:S(2)}) collective-permute-start(bf16[1536,128]{1,0:T(8,128)(2,1)S(1)} %get-tuple-element.36), channel_id=1, source_target_pairs={{0,1},{1,0},{2,3},{3,2},{4,5},{5,4},{6,7},{7,6},{8,9},{9,8},{10,11... | collective-permute-start | bytes 1179656 | tf_op jit(solution)/shard_map/ppermute | solution.py:314
  66.1 1.7 %copy-start.2 = (bf16[1,8,320,128]{3,2,1,0:T(8,128)(2,1)S(1)}, bf16[1,8,320,128]{3,2,1,0:T(8,128)(2,1)}, u32[]{:S(2)}) copy-start(bf16[1,8,320,128]{3,2,1,0:T(8,128)(2,1)} %param.13) | copy-start | bytes 1966084
  68.9 4.2 %copy-start.3 = (bf16[3,3,3,128,128]{4,3,2,1,0:T(8,128)(2,1)S(1)}, bf16[3,3,3,128,128]{4,3,2,1,0:T(8,128)(2,1)}, u32[]{:S(2)}) copy-start(bf16[3,3,3,128,128]{4,3,2,1,0:T(8,128)(2,1)} %weight.11) | copy-start | bytes 2654212
  71.2 4.4 %collective-permute-start.8 = (bf16[10,352,128]{2,1,0:T(8,128)(2,1)S(1)}, bf16[10,352,128]{2,1,0:T(8,128)(2,1)S(1)}, u32[]{:S(2)}, u32[]{:S(2)}) collective-permute-start(bf16[10,352,128]{2,1,0:T(8,128)(2,1)S(1)} %get-tuple-element.43), channel_id=1, source_target_pairs={{0,1},{1,0},{2,3},{3,2},{4,5},{5,4},{6,7},{7,6},{8,9},{9,8},{10,11... | collective-permute-start | bytes 2703368 | tf_op jit(solution)/shard_map/ppermute | solution.py:314

commit v5 on v4

--- a/solution.py
+++ b/solution.py
@@ -60,16 +60,13 @@
     crows, ccols, _ = latent.shape
     copies = [(latent, latent_v), (weight, weight_v), (bias, bias_v)]
     n_first = len(copies)
-    n_c1 = rows * E
-    n_c2 = (rows + crows) * E
     t0 = 2 * cols + ccols
     sends = ((row_0, col_0, False), (row_1, col_1, True))
     for row_s, col_s, flip in sends:
         lo, hi = (cols - E, 0) if flip else (0, cols - E)
         c = pl.ds(pick("col", hi, lo, E), E)
-        for i in range(rows):
-            copies.append((one.at[i, c], col_s.at[i * E : (i + 1) * E]))
-            copies.append((two.at[i, c], col_s.at[n_c2 + i * E : n_c2 + (i + 1) * E]))
+        copies.append((one.at[:, c], col_s.at[0:rows]))
+        copies.append((two.at[:, c], col_s.at[rows + crows :]))
         lo, hi = (rows - 2, 0) if flip else (0, rows - 2)
         r = pick("row", hi, lo)
         for k in range(2):
@@ -93,7 +90,7 @@
         lo, hi = (ccols - E, 0) if flip else (0, ccols - E)
         c = pl.ds(pick("col", hi, lo, E), E)
         for i in range(crows):
-            col_s[n_c1 + i * E : n_c1 + (i + 1) * E, :] = act[i, c, :]
+            col_s[rows + i] = act[i, c, :]
     for c in started[n_first:]:
         c.wait()
 
@@ -101,7 +98,7 @@
 def corner_kernel(rows, crows, got_0, got_1, merged, act_edge, cor_0, cor_1):
     is_even = even("col")
     for i in range(2 * rows + crows):
-        x, y = (g[i * E : (i + 1) * E, :].astype(F32) for g in (got_0, got_1))
+        x, y = (g[i].astype(F32) for g in (got_0, got_1))
         both = jnp.concatenate([jnp.where(is_even, x, y), jnp.where(is_even, y, x)], axis=0)
         merged[i * B : (i + 1) * B, :] = both.astype(BF)
         if rows <= i < rows + crows:
@@ -168,24 +165,14 @@
     return row, tile.shape[0] * each
 
 
-def fill_kernel(one, act, act_up, send):
-    rows, cols, _ = one.shape
-    crows, ccols, _ = act.shape
+def fill_kernel(act, act_up):
+    crows, cols, _ = act_up.shape
+    ccols = act.shape[1]
     spread = spread_matrix(cols, ccols)
     for m in range(0, crows, 2):
         wide = jnp.dot(spread, jnp.concatenate([act[m], act[m + 1]], axis=1), preferred_element_type=F32).astype(BF)
         for h in range(2):
             act_up[m + h] = wide[:, h * 128 : (h + 1) * 128]
-    lead = lax.axis_index("frm") == 0
-
-    @pl.when(lead)
-    def _():
-        for i in range(rows):
-            send[i] = act_up[i // 2]
-
-    @pl.when(jnp.logical_not(lead))
-    def _():
-        send[...] = one[...]
 
 
 def inner_kernel(one, act_up, merged, act_edge, weight, part, sums):
@@ -195,15 +182,14 @@
             part[k - 2 + h] = v
 
 
-def border_kernel(row_0, row_1, cor_0, cor_1, merged, act_edge, cache_border, act_border, send):
-    _, span, _ = cache_border.shape
-    cols = span - 2 * B
+def border_kernel(one, act_up, merged, act_edge, row_0, row_1, cor_0, cor_1, cache_border, act_border, send):
+    rows, cols, _ = one.shape
     ccols = row_0.shape[0] - 3 * cols
-    for lead in (True, False):
-
-        @pl.when(even("row") == lead)
-        def _(lead=lead):
-            pairs = ((row_1, cor_1), (row_0, cor_0)) if lead else ((row_0, cor_0), (row_1, cor_1))
+    for even_row in (True, False):
+
+        @pl.when(even("row") == even_row)
+        def _(even_row=even_row):
+            pairs = ((row_1, cor_1), (row_0, cor_0)) if even_row else ((row_0, cor_0), (row_1, cor_1))
             coarse = jnp.concatenate([row[2 * cols : 2 * cols + ccols, :] for row, _ in pairs], axis=1)
             wide = jnp.dot(spread_matrix(cols, ccols), coarse, preferred_element_type=F32).astype(BF)
             for h, (row, cor) in enumerate(pairs):
@@ -212,20 +198,21 @@
                 put_row(act_border, h, wide[:, h * 128 : (h + 1) * 128], spread_edge(block(cor, 2)))
 
     lead = lax.axis_index("frm") == 0
-    n_edge = send.shape[0] - 4 * span
 
     @pl.when(lead)
     def _():
         for i in range(4):
-            send[i * span : (i + 1) * span, :] = act_border[i // 2]
-        for i in range(n_edge // B):
-            send[4 * span + i * B : 4 * span + (i + 1) * B, :] = act_edge[i // 2 * B : (i // 2 + 1) * B, :]
+            send[i if i < 2 else rows + i] = act_border[i // 2]
+        for i in range(rows):
+            m = i // 2
+            put_row(send, i + 2, act_up[m], act_edge[m * B : (m + 1) * B, :])
 
     @pl.when(jnp.logical_not(lead))
     def _():
         for i in range(4):
-            send[i * span : (i + 1) * span, :] = cache_border[i]
-        send[4 * span :, :] = merged[0:n_edge, :]
+            send[i if i < 2 else rows + i] = cache_border[i]
+        for i in range(rows):
+            put_row(send, i + 2, one[i], merged[i * B : (i + 1) * B, :])
 
 
 def outer_kernel(
@@ -266,11 +253,10 @@
     out[i, span - B :, :] = jnp.where(keep_right, v[span - B :], 0.0).astype(BF)
 
 
-def middle_kernel(core, border, part_in, part_out, weight, bias, two_frame, out, send, sums):
-    n_out, span, _ = out.shape
-    frame = joined(framed(core, border, 4 * span), lambda i: border[i * span : (i + 1) * span, :])
+def middle_kernel(middle, part_in, part_out, weight, bias, two_frame, out, send, sums):
+    n_out, _, _ = out.shape
     for k in range(0, n_out, 2):
-        for h, v in enumerate(conv_rows((frame,), (1,), weight, k, sums, k // 2 % 2)):
+        for h, v in enumerate(conv_rows((lambda i: middle[i],), (1,), weight, k, sums, k // 2 % 2)):
             i = k + h
             part = part_in[i - 2] if 2 <= i < n_out - 2 else part_out[i if i < 2 else i - n_out + 4]
             finish_row(out, i, v + part + bias[...], i, n_out)
@@ -320,7 +306,7 @@
     crows, ccols, lch = latent.shape
     span = cols + 2 * B
     n_edge = (2 * rows + crows) * B
-    n_send = (2 * rows + crows) * E
+    col_shape = (2 * rows + crows, E, ch)
     n_row = 3 * cols + ccols
     sums = pltpu.VMEM((4, span + 16, 2 * ch), F32)
     proj, act, row_0, row_1, col_0, col_1, b_one, b_two = call(
@@ -330,8 +316,8 @@
             ((crows, ccols, ch), BF),
             ((n_row, ch), BF),
             ((n_row, ch), BF),
-            ((n_send, ch), BF),
-            ((n_send, ch), BF),
+            (col_shape, BF),
+            (col_shape, BF),
             ((1, ch), F32),
             ((1, ch), F32),
         ],
@@ -340,7 +326,7 @@
             pltpu.VMEM((crows, ccols, lch), BF),
             pltpu.VMEM((lch, ch), BF),
             pltpu.VMEM((1, ch), F32),
-            pltpu.SemaphoreType.DMA((3 + 4 * rows + 8,)),
+            pltpu.SemaphoreType.DMA((15,)),
         ],
         flops=10**8,
         nbytes=2 * 10**6,
@@ -351,10 +337,7 @@
     row_1 = exchange(row_1, "row", 1)
     row_0 = exchange(row_0, "row", 0)
     third = 2 * 9 * ch * ch * rows * cols
-    act_up, send_core = call(
-        fill_kernel, [((crows, cols, ch), BF), ((rows, cols, ch), BF)], [VMEM] * 2, flops=10**8, nbytes=4 * 10**6
-    )(one, act)
-    middle_core = swap(send_core)
+    (act_up,) = call(fill_kernel, [((crows, cols, ch), BF)], [VMEM], flops=10**8, nbytes=10**6)(act)
     merged, act_edge, cor_0, cor_1 = call(
         functools.partial(corner_kernel, rows, crows),
         [((n_edge, ch), BF), ((crows * B, ch), BF), ((4 * B, ch), BF), ((4 * B, ch), BF)],
@@ -367,14 +350,14 @@
     (part_in,) = call(
         inner_kernel, [((rows - 2, span, ch), F32)], [VMEM] * 5, scratch=[sums], flops=2 * third, nbytes=4 * 10**6
     )(one, act_up, merged, act_edge, conv_one)
-    cache_border, act_border, send_border = call(
+    cache_border, act_border, send = call(
         border_kernel,
-        [((4, span, ch), BF), ((2, span, ch), BF), ((4 * span + rows * B, ch), BF)],
-        [VMEM] * 6,
+        [((4, span, ch), BF), ((2, span, ch), BF), ((rows + 4, span, ch), BF)],
+        [VMEM] * 8,
         flops=10**8,
         nbytes=4 * 10**6,
-    )(row_0, row_1, cor_0, cor_1, merged, act_edge)
-    middle_border = swap(send_border)
+    )(one, act_up, merged, act_edge, row_0, row_1, cor_0, cor_1)
+    middle = swap(send)
     part_out, two_frame = call(
         functools.partial(outer_kernel, first=rows + crows),
         [((4, span, ch), F32), ((rows + 2, span, ch), BF)],
@@ -384,8 +367,8 @@
         nbytes=4 * 10**6,
     )(one, act_up, merged, act_edge, cache_border, act_border, conv_one, two, row_0, row_1, cor_0, cor_1)
     act_two, send_two = call(
-        middle_kernel, [((rows + 2, span, ch), BF)] * 2, [VMEM] * 7, scratch=[sums], flops=third, nbytes=6 * 10**6
-    )(middle_core, middle_border, part_in, part_out, conv_one, b_one, two_frame)
+        middle_kernel, [((rows + 2, span, ch), BF)] * 2, [VMEM] * 6, scratch=[sums], flops=third, nbytes=6 * 10**6
+    )(middle, part_in, part_out, conv_one, b_one, two_frame)
     middle_two = swap(send_two)
     (part_two,) = call(
         own_two_kernel, [((rows, cols, ch), F32)], [VMEM] * 5, scratch=[sums], flops=2 * third, nbytes=6 * 10**6

time: 77.9 us -> 75.5 us (0.969)
  waiting for transfers between devices: 4.17 us -> 2.48 us
    ppermute x6, starting transfers between devices: 52.2 us -> 25.2 us  [exchange(): return lax.ppermute(x, axis, pairs + [(j, i) for i, j in pairs])]
    ppermute x3 -> x2, starting transfers between devices: 9.37 us -> 36 us  [swap(): return lax.ppermute(x, 'frm', [(0, 1), (1, 0)])]
    ppermute x6, waiting for transfers between devices: 3.92 us -> 2.23 us  [exchange(): return lax.ppermute(x, axis, pairs + [(j, i) for i, j in pairs])]
  transfers between devices with their start and end apart: 9 -> 8, of which waited for: 3 -> 3; matrix products, arithmetic and copies ran while one was open for 0% -> 0% of each run, Pallas kernels for 7% -> 7%
where the time goes in v5:
time: 75.5 us; the launch traced here: 75.2 us
  starting transfers between devices  61.2 us (81%)
  Pallas kernels  11.3 us (15%)
  waiting for transfers between devices  2.48 us (3%)
    ppermute x2, starting transfers between devices, swap(): return lax.ppermute(x, 'frm', [(0, 1), (1, 0)])  36 us
    ppermute x6, starting transfers between devices, exchange(): return lax.ppermute(x, axis, pairs + [(j, i) for i, j in pairs])  25.2 us
    pallas_call x9, Pallas kernels, call(): run(*(held(v, spec) for v, spec in zip(args, specs, strict=True)))  11.3 us
    ppermute x6, waiting for transfers between devices, exchange(): return lax.ppermute(x, axis, pairs + [(j, i) for i, j in pairs])  2.23 us
  transfers between devices with their start and end apart: 8, of which 3 were waited for; matrix products, arithmetic and copies ran while one was open for 0% of the time, Pallas kernels for 7%

profile of v5, /device:TPU:99, one launch (start us, length us, event | category | flops | bytes accessed | tf_op | source)
XLA Modules:
  0.0 75.2 jit_solution(12007258756766048131)
XLA Ops:
  0.0 0.0 copy-start
  0.0 1.5 %shard_map.91 = (bf16[4,160,128]{2,1,0:T(8,128)(2,1)S(1)}, bf16[4,160,128]{2,1,0:T(8,128)(2,1)S(1)}, bf16[1120,128]{1,0:T(8,128)(2,1)S(1)}, bf16[1120,128]{1,0:T...) custom-call(bf16[4,160,256]{2,1,0:T(8,128)(2,1)} %bitcast.13, ...), custom_call_target="tpu_custom_call" | custom-call | flops 100000000 | bytes 2000000 | tf_op jit(solution)/shard_map/pallas_call | solution.py:29
  1.5 2.0 %collective-permute-start.2 = (bf16[1120,128]{1,0:T(8,128)(2,1)S(1)}, bf16[1120,128]{1,0:T(8,128)(2,1)S(1)}, u32[]{:S(2)}, u32[]{:S(2)}) collective-permute-start(bf16[1120,128]{1,0:T(8,128)(2,1)S(1)} %get-tuple-element.29), channel_id=1, source_target_pairs={{0,8},{16,24},{32,40},{48,56},{64,72},{80,88},{96,104},{112,120},{... | collective-permute-start | bytes 860168 | tf_op jit(solution)/shard_map/ppermute | solution.py:296
  3.5 6.9 %collective-permute-start.3 = (bf16[1120,128]{1,0:T(8,128)(2,1)S(1)}, bf16[1120,128]{1,0:T(8,128)(2,1)S(1)}, u32[]{:S(2)}, u32[]{:S(2)}) collective-permute-start(bf16[1120,128]{1,0:T(8,128)(2,1)S(1)} %get-tuple-element.30), channel_id=1, source_target_pairs={{8,16},{24,32},{40,48},{56,64},{72,80},{88,96},{104,112},{120,128}... | collective-permute-start | bytes 860168 | tf_op jit(solution)/shard_map/ppermute | solution.py:296
  10.4 2.1 %collective-permute-start = (bf16[20,8,128]{2,1,0:T(8,128)(2,1)S(1)}, bf16[20,8,128]{2,1,0:T(8,128)(2,1)S(1)}, u32[]{:S(2)}, u32[]{:S(2)}) collective-permute-start(bf16[20,8,128]{2,1,0:T(8,128)(2,1)S(1)} %get-tuple-element.25), channel_id=1, source_target_pairs={{0,2},{4,6},{2,0},{6,4},{1,3},{5,7},{3,1},{7,5},{8,10},{12,14},{10... | collective-permute-start | bytes 122888 | tf_op jit(solution)/shard_map/ppermute | solution.py:296
  12.5 4.2 %collective-permute-start.1 = (bf16[20,8,128]{2,1,0:T(8,128)(2,1)S(1)}, bf16[20,8,128]{2,1,0:T(8,128)(2,1)S(1)}, u32[]{:S(2)}, u32[]{:S(2)}) collective-permute-start(bf16[20,8,128]{2,1,0:T(8,128)(2,1)S(1)} %get-tuple-element.26), channel_id=1, source_target_pairs={{2,4},{4,2},{3,5},{5,3},{10,12},{12,10},{11,13},{13,11},{18,20},{2... | collective-permute-start | bytes 122888 | tf_op jit(solution)/shard_map/ppermute | solution.py:296
  16.7 0.0 collective-permute-done.got_0
  16.7 1.4 %collective-permute-done.1.got_1 = bf16[20,8,128]{2,1,0:T(8,128)(2,1)S(1)} collective-permute-done((bf16[20,8,128]{2,1,0:T(8,128)(2,1)S(1)}, bf16[20,8,128]{2,1,0:T(8,128)(2,1)S(1)}, u32[]{:S(2)}, u32[]{:S(2)}) %collective-permute-start.1) | collective-permute-done | bytes 40992 | tf_op jit(solution)/shard_map/ppermute | solution.py:296
  18.1 2.0 %collective-permute-start.4 = (bf16[64,128]{1,0:T(8,128)(2,1)S(1)}, bf16[64,128]{1,0:T(8,128)(2,1)S(1)}, u32[]{:S(2)}, u32[]{:S(2)}) collective-permute-start(bf16[64,128]{1,0:T(8,128)(2,1)S(1)} %get-tuple-element.31), channel_id=1, source_target_pairs={{0,8},{16,24},{32,40},{48,56},{64,72},{80,88},{96,104},{112,120},{... | collective-permute-start | bytes 49160 | tf_op jit(solution)/shard_map/ppermute | solution.py:296
  20.0 8.1 %collective-permute-start.5 = (bf16[64,128]{1,0:T(8,128)(2,1)S(1)}, bf16[64,128]{1,0:T(8,128)(2,1)S(1)}, u32[]{:S(2)}, u32[]{:S(2)}) collective-permute-start(bf16[64,128]{1,0:T(8,128)(2,1)S(1)} %get-tuple-element.32), channel_id=1, source_target_pairs={{8,16},{24,32},{40,48},{56,64},{72,80},{88,96},{104,112},{120,128}... | collective-permute-start | bytes 49160 | tf_op jit(solution)/shard_map/ppermute | solution.py:296
  28.2 0.0 copy-start.1
  28.2 0.2 shard_map.92.act_up
  28.4 0.0 collective-permute-done.4.cor_0
  28.4 0.8 %collective-permute-done.5.cor_1 = bf16[64,128]{1,0:T(8,128)(2,1)S(1)} collective-permute-done((bf16[64,128]{1,0:T(8,128)(2,1)S(1)}, bf16[64,128]{1,0:T(8,128)(2,1)S(1)}, u32[]{:S(2)}, u32[]{:S(2)}) %collective-permute-start.5) | collective-permute-done | bytes 16416 | tf_op jit(solution)/shard_map/ppermute | solution.py:296
  29.3 0.0 collective-permute-done.2.row_0
  29.3 0.0 collective-permute-done.3.row_1
  29.3 0.0 copy-done
  29.3 0.3 shard_map.94
  29.6 0.0 copy-start.2
  29.6 34.0 %collective-permute-start.6 = (bf16[12,352,128]{2,1,0:T(8,128)(2,1)S(1)}, bf16[12,352,128]{2,1,0:T(8,128)(2,1)S(1)}, u32[]{:S(2)}, u32[]{:S(2)}) collective-permute-start(bf16[12,352,128]{2,1,0:T(8,128)(2,1)S(1)} %get-tuple-element.33), channel_id=1, source_target_pairs={{0,1},{1,0},{2,3},{3,2},{4,5},{5,4},{6,7},{7,6},{8,9},{9,8},{10,11... | collective-permute-start | bytes 3244040 | tf_op jit(solution)/shard_map/ppermute | solution.py:300
  63.7 0.0 copy-done.1
  63.7 1.6 %shard_map.95.part_in = f32[6,352,128]{2,1,0:T(8,128)S(1)} custom-call(bf16[8,320,128]{2,1,0:T(8,128)(2,1)S(1)} %bitcast.9, bf16[4,320,128]{2,1,0:T(8,128)(2,1)S(1)} %shard_map.92.act_up, bf16[320,128]{1,0:T(8,128)(2,1)S(1)} %get-tuple-element.27.merged, bf16[64,128]{1,0:T(8,128)(2,1)S(1)} %get-tuple-element.28.act_edge, ...), custom_call_target="tpu_custom_call" | custom-call | flops 1509949440 | bytes 4000000 | tf_op jit(solution)/shard_map/pallas_call | solution.py:29
  65.3 0.0 copy-done.2
  65.3 1.2 %shard_map.96 = (f32[4,352,128]{2,1,0:T(8,128)S(1)}, bf16[10,352,128]{2,1,0:T(8,128)(2,1)S(1)}) custom-call(bf16[8,320,128]{2,1,0:T(8,128)(2,1)S(1)} %bitcast.10, bf16[4,320,128]{2,1,0:T(8,128)(2,1)S(1)} %shard_map.92.act_up, bf16[320,128]{1,0:T(8,128)(2,1)S(1)} %get-tuple-element.27.merged, bf16[64,128]{1,0:T(8,128)(2,1)S(1)} %get-tuple-element.28.act_edge, ...), custom_call_target="tpu_custom_call" | custom-call | flops 754974720 | bytes 4000000 | tf_op jit(solution)/shard_map/pallas_call | solution.py:29
  66.5 0.0 collective-permute-done.6.middle
  66.5 0.0 copy-start.3
  66.5 2.3 %shard_map.97 = (bf16[10,352,128]{2,1,0:T(8,128)(2,1)S(1)}, bf16[10,352,128]{2,1,0:T(8,128)(2,1)S(1)}) custom-call(bf16[12,352,128]{2,1,0:T(8,128)(2,1)S(1)} %collective-permute-done.6.middle, f32[6,352,128]{2,1,0:T(8,128)S(1)} %shard_map.95.part_in, f32[4,352,128]{2,1,0:T(8,128)S(1)} %get-tuple-element.36.part_out, ...), custom_call_target="tpu_custom_call" | custom-call | flops 754974720 | bytes 6000000 | tf_op jit(solution)/shard_map/pallas_call | solution.py:29
  68.8 2.0 %collective-permute-start.7 = (bf16[10,352,128]{2,1,0:T(8,128)(2,1)S(1)}, bf16[10,352,128]{2,1,0:T(8,128)(2,1)S(1)}, u32[]{:S(2)}, u32[]{:S(2)}) collective-permute-start(bf16[10,352,128]{2,1,0:T(8,128)(2,1)S(1)} %get-tuple-element.39), channel_id=1, source_target_pairs={{0,1},{1,0},{2,3},{3,2},{4,5},{5,4},{6,7},{7,6},{8,9},{9,8},{10,11... | collective-permute-start | bytes 2703368 | tf_op jit(solution)/shard_map/ppermute | solution.py:300
  70.8 0.0 copy-done.3
  70.8 2.1 %shard_map.98.part = f32[8,320,128]{2,1,0:T(8,128)S(1)} custom-call(bf16[10,352,128]{2,1,0:T(8,128)(2,1)S(1)} %get-tuple-element.38.two_frame, bf16[10,352,128]{2,1,0:T(8,128)(2,1)S(1)} %get-tuple-element.40.act_two, bf16[3,3,3,128,128]{4,3,2,1,0:T(8,128)(2,1)S(1)} %copy-done.3, bf16[4,160,128]{2,1,0:T(8,128)(2,1)S(1)} %get-tuple-element.41.proj, ...), custom_call_target="tpu_custom_call" | custom-call | flops 1509949440 | bytes 6000000 | tf_op jit(solution)/shard_map/pallas_call | solution.py:29
  72.9 0.3 collective-permute-done.7.middle
  73.2 2.0 %shard_map.99 = bf16[8,320,128]{2,1,0:T(8,128)(2,1)} custom-call(bf16[10,352,128]{2,1,0:T(8,128)(2,1)S(1)} %collective-permute-done.7.middle, f32[8,320,128]{2,1,0:T(8,128)S(1)} %shard_map.98.part, bf16[3,3,3,128,128]{4,3,2,1,0:T(8,128)(2,1)S(1)} %copy-done.3), custom_call_target="tpu_custom_call" | custom-call | flops 754974720 | bytes 6000000 | tf_op jit(solution)/shard_map/pallas_call | solution.py:29
  (1 shorter events, 0.0 us)
Async XLA Ops:
  0.0 29.3 %copy-start = (bf16[1,8,320,128]{3,2,1,0:T(8,128)(2,1)S(1)}, bf16[1,8,320,128]{3,2,1,0:T(8,128)(2,1)}, u32[]{:S(2)}) copy-start(bf16[1,8,320,128]{3,2,1,0:T(8,128)(2,1)} %param.12) | copy-start | bytes 1966084
  1.5 27.8 %collective-permute-start.2 = (bf16[1120,128]{1,0:T(8,128)(2,1)S(1)}, bf16[1120,128]{1,0:T(8,128)(2,1)S(1)}, u32[]{:S(2)}, u32[]{:S(2)}) collective-permute-start(bf16[1120,128]{1,0:T(8,128)(2,1)S(1)} %get-tuple-element.29), channel_id=1, source_target_pairs={{0,8},{16,24},{32,40},{48,56},{64,72},{80,88},{96,104},{112,120},{... | collective-permute-start | bytes 860168 | tf_op jit(solution)/shard_map/ppermute | solution.py:296
  3.5 25.8 %collective-permute-start.3 = (bf16[1120,128]{1,0:T(8,128)(2,1)S(1)}, bf16[1120,128]{1,0:T(8,128)(2,1)S(1)}, u32[]{:S(2)}, u32[]{:S(2)}) collective-permute-start(bf16[1120,128]{1,0:T(8,128)(2,1)S(1)} %get-tuple-element.30), channel_id=1, source_target_pairs={{8,16},{24,32},{40,48},{56,64},{72,80},{88,96},{104,112},{120,128}... | collective-permute-start | bytes 860168 | tf_op jit(solution)/shard_map/ppermute | solution.py:296
  10.4 6.3 %collective-permute-start = (bf16[20,8,128]{2,1,0:T(8,128)(2,1)S(1)}, bf16[20,8,128]{2,1,0:T(8,128)(2,1)S(1)}, u32[]{:S(2)}, u32[]{:S(2)}) collective-permute-start(bf16[20,8,128]{2,1,0:T(8,128)(2,1)S(1)} %get-tuple-element.25), channel_id=1, source_target_pairs={{0,2},{4,6},{2,0},{6,4},{1,3},{5,7},{3,1},{7,5},{8,10},{12,14},{10... | collective-permute-start | bytes 122888 | tf_op jit(solution)/shard_map/ppermute | solution.py:296
  12.5 5.6 %collective-permute-start.1 = (bf16[20,8,128]{2,1,0:T(8,128)(2,1)S(1)}, bf16[20,8,128]{2,1,0:T(8,128)(2,1)S(1)}, u32[]{:S(2)}, u32[]{:S(2)}) collective-permute-start(bf16[20,8,128]{2,1,0:T(8,128)(2,1)S(1)} %get-tuple-element.26), channel_id=1, source_target_pairs={{2,4},{4,2},{3,5},{5,3},{10,12},{12,10},{11,13},{13,11},{18,20},{2... | collective-permute-start | bytes 122888 | tf_op jit(solution)/shard_map/ppermute | solution.py:296
  18.1 10.3 %collective-permute-start.4 = (bf16[64,128]{1,0:T(8,128)(2,1)S(1)}, bf16[64,128]{1,0:T(8,128)(2,1)S(1)}, u32[]{:S(2)}, u32[]{:S(2)}) collective-permute-start(bf16[64,128]{1,0:T(8,128)(2,1)S(1)} %get-tuple-element.31), channel_id=1, source_target_pairs={{0,8},{16,24},{32,40},{48,56},{64,72},{80,88},{96,104},{112,120},{... | collective-permute-start | bytes 49160 | tf_op jit(solution)/shard_map/ppermute | solution.py:296
  20.0 9.2 %collective-permute-start.5 = (bf16[64,128]{1,0:T(8,128)(2,1)S(1)}, bf16[64,128]{1,0:T(8,128)(2,1)S(1)}, u32[]{:S(2)}, u32[]{:S(2)}) collective-permute-start(bf16[64,128]{1,0:T(8,128)(2,1)S(1)} %get-tuple-element.32), channel_id=1, source_target_pairs={{8,16},{24,32},{40,48},{56,64},{72,80},{88,96},{104,112},{120,128}... | collective-permute-start | bytes 49160 | tf_op jit(solution)/shard_map/ppermute | solution.py:296
  28.2 35.5 %copy-start.1 = (bf16[3,3,3,128,128]{4,3,2,1,0:T(8,128)(2,1)S(1)}, bf16[3,3,3,128,128]{4,3,2,1,0:T(8,128)(2,1)}, u32[]{:S(2)}) copy-start(bf16[3,3,3,128,128]{4,3,2,1,0:T(8,128)(2,1)} %weight.9) | copy-start | bytes 2654212
  29.6 35.7 %copy-start.2 = (bf16[1,8,320,128]{3,2,1,0:T(8,128)(2,1)S(1)}, bf16[1,8,320,128]{3,2,1,0:T(8,128)(2,1)}, u32[]{:S(2)}) copy-start(bf16[1,8,320,128]{3,2,1,0:T(8,128)(2,1)} %param.13) | copy-start | bytes 1966084
  29.6 36.9 %collective-permute-start.6 = (bf16[12,352,128]{2,1,0:T(8,128)(2,1)S(1)}, bf16[12,352,128]{2,1,0:T(8,128)(2,1)S(1)}, u32[]{:S(2)}, u32[]{:S(2)}) collective-permute-start(bf16[12,352,128]{2,1,0:T(8,128)(2,1)S(1)} %get-tuple-element.33), channel_id=1, source_target_pairs={{0,1},{1,0},{2,3},{3,2},{4,5},{5,4},{6,7},{7,6},{8,9},{9,8},{10,11... | collective-permute-start | bytes 3244040 | tf_op jit(solution)/shard_map/ppermute | solution.py:300
  66.5 4.3 %copy-start.3 = (bf16[3,3,3,128,128]{4,3,2,1,0:T(8,128)(2,1)S(1)}, bf16[3,3,3,128,128]{4,3,2,1,0:T(8,128)(2,1)}, u32[]{:S(2)}) copy-start(bf16[3,3,3,128,128]{4,3,2,1,0:T(8,128)(2,1)} %weight.11) | copy-start | bytes 2654212
  68.8 4.4 %collective-permute-start.7 = (bf16[10,352,128]{2,1,0:T(8,128)(2,1)S(1)}, bf16[10,352,128]{2,1,0:T(8,128)(2,1)S(1)}, u32[]{:S(2)}, u32[]{:S(2)}) collective-permute-start(bf16[10,352,128]{2,1,0:T(8,128)(2,1)S(1)} %get-tuple-element.39), channel_id=1, source_target_pairs={{0,1},{1,0},{2,3},{3,2},{4,5},{5,4},{6,7},{7,6},{8,9},{9,8},{10,11... | collective-permute-start | bytes 2703368 | tf_op jit(solution)/shard_map/ppermute | solution.py:300

commit v6 on v5

--- a/solution.py
+++ b/solution.py
@@ -151,6 +151,27 @@
     return results
 
 
+def shift_rows(frame, rows, moved):
+    span = moved.shape[1]
+    for i in rows:
+        x = frame(i).astype(F32)
+        moved[i, :, 0:128] = pltpu.roll(x, 1, 0).astype(BF)
+        moved[i, :, 128:256] = pltpu.roll(x, span - 1, 0).astype(BF)
+
+
+def conv_pair(frame, moved, step, weight, k):
+    lhs, rhs = [], []
+    zero = jnp.zeros(weight.shape[3:], BF)
+    for p in range(4):
+        lhs += [moved[k + p], frame(k + p)]
+        for q in (0, 2, 1):
+            first = weight[step, p, q] if p < 3 else zero
+            second = weight[step, p - 1, q] if p else zero
+            rhs.append(jnp.concatenate([first, second], axis=1))
+    y = jnp.dot(jnp.concatenate(lhs, axis=1), jnp.concatenate(rhs, axis=0), preferred_element_type=F32)
+    return y[:, 0:128], y[:, 128:256]
+
+
 def joined(core, border):
     core, n = core
     return lambda i: border(i) if i < 2 else core(i - 2) if i < n + 2 else border(i - n)
@@ -253,10 +274,12 @@
     out[i, span - B :, :] = jnp.where(keep_right, v[span - B :], 0.0).astype(BF)
 
 
-def middle_kernel(middle, part_in, part_out, weight, bias, two_frame, out, send, sums):
+def middle_kernel(middle, part_in, part_out, weight, bias, two_frame, out, send, moved):
     n_out, _, _ = out.shape
+    row = lambda i: middle[i]
     for k in range(0, n_out, 2):
-        for h, v in enumerate(conv_rows((lambda i: middle[i],), (1,), weight, k, sums, k // 2 % 2)):
+        shift_rows(row, range(k + 2 if k else 0, k + 4), moved)
+        for h, v in enumerate(conv_pair(row, moved, 1, weight, k)):
             i = k + h
             part = part_in[i - 2] if 2 <= i < n_out - 2 else part_out[i if i < 2 else i - n_out + 4]
             finish_row(out, i, v + part + bias[...], i, n_out)
@@ -367,7 +390,12 @@
         nbytes=4 * 10**6,
     )(one, act_up, merged, act_edge, cache_border, act_border, conv_one, two, row_0, row_1, cor_0, cor_1)
     act_two, send_two = call(
-        middle_kernel, [((rows + 2, span, ch), BF)] * 2, [VMEM] * 6, scratch=[sums], flops=third, nbytes=6 * 10**6
+        middle_kernel,
+        [((rows + 2, span, ch), BF)] * 2,
+        [VMEM] * 6,
+        scratch=[pltpu.VMEM((rows + 4, span, 2 * ch), BF)],
+        flops=third,
+        nbytes=6 * 10**6,
     )(middle, part_in, part_out, conv_one, b_one, two_frame)
     middle_two = swap(send_two)
     (part_two,) = call(

time: 75.5 us -> 75.2 us (level)
  no operation moved by 1% of the time
where the time goes in v6:
time: 75.2 us; the launch traced here: 74.8 us
  starting transfers between devices  61.2 us (81%)
  Pallas kernels  10.9 us (14%)
  waiting for transfers between devices  2.48 us (3%)
    ppermute x2, starting transfers between devices, swap(): return lax.ppermute(x, 'frm', [(0, 1), (1, 0)])  36 us
    ppermute x6, starting transfers between devices, exchange(): return lax.ppermute(x, axis, pairs + [(j, i) for i, j in pairs])  25.2 us
    pallas_call x9, Pallas kernels, call(): run(*(held(v, spec) for v, spec in zip(args, specs, strict=True)))  10.9 us
    ppermute x6, waiting for transfers between devices, exchange(): return lax.ppermute(x, axis, pairs + [(j, i) for i, j in pairs])  2.23 us
  transfers between devices with their start and end apart: 8, of which 3 were waited for; matrix products, arithmetic and copies ran while one was open for 0% of the time, Pallas kernels for 7%

profile of v6, /device:TPU:99, one launch (start us, length us, event | category | flops | bytes accessed | tf_op | source)
XLA Modules:
  0.0 74.8 jit_solution(16174593798602365900)
XLA Ops:
  0.0 0.0 copy-start
  0.0 1.5 %shard_map.91 = (bf16[4,160,128]{2,1,0:T(8,128)(2,1)S(1)}, bf16[4,160,128]{2,1,0:T(8,128)(2,1)S(1)}, bf16[1120,128]{1,0:T(8,128)(2,1)S(1)}, bf16[1120,128]{1,0:T...) custom-call(bf16[4,160,256]{2,1,0:T(8,128)(2,1)} %bitcast.13, ...), custom_call_target="tpu_custom_call" | custom-call | flops 100000000 | bytes 2000000 | tf_op jit(solution)/shard_map/pallas_call | solution.py:29
  1.5 2.0 %collective-permute-start.2 = (bf16[1120,128]{1,0:T(8,128)(2,1)S(1)}, bf16[1120,128]{1,0:T(8,128)(2,1)S(1)}, u32[]{:S(2)}, u32[]{:S(2)}) collective-permute-start(bf16[1120,128]{1,0:T(8,128)(2,1)S(1)} %get-tuple-element.29), channel_id=1, source_target_pairs={{0,8},{16,24},{32,40},{48,56},{64,72},{80,88},{96,104},{112,120},{... | collective-permute-start | bytes 860168 | tf_op jit(solution)/shard_map/ppermute | solution.py:319
  3.5 6.9 %collective-permute-start.3 = (bf16[1120,128]{1,0:T(8,128)(2,1)S(1)}, bf16[1120,128]{1,0:T(8,128)(2,1)S(1)}, u32[]{:S(2)}, u32[]{:S(2)}) collective-permute-start(bf16[1120,128]{1,0:T(8,128)(2,1)S(1)} %get-tuple-element.30), channel_id=1, source_target_pairs={{8,16},{24,32},{40,48},{56,64},{72,80},{88,96},{104,112},{120,128}... | collective-permute-start | bytes 860168 | tf_op jit(solution)/shard_map/ppermute | solution.py:319
  10.4 2.1 %collective-permute-start = (bf16[20,8,128]{2,1,0:T(8,128)(2,1)S(1)}, bf16[20,8,128]{2,1,0:T(8,128)(2,1)S(1)}, u32[]{:S(2)}, u32[]{:S(2)}) collective-permute-start(bf16[20,8,128]{2,1,0:T(8,128)(2,1)S(1)} %get-tuple-element.25), channel_id=1, source_target_pairs={{0,2},{4,6},{2,0},{6,4},{1,3},{5,7},{3,1},{7,5},{8,10},{12,14},{10... | collective-permute-start | bytes 122888 | tf_op jit(solution)/shard_map/ppermute | solution.py:319
  12.5 4.2 %collective-permute-start.1 = (bf16[20,8,128]{2,1,0:T(8,128)(2,1)S(1)}, bf16[20,8,128]{2,1,0:T(8,128)(2,1)S(1)}, u32[]{:S(2)}, u32[]{:S(2)}) collective-permute-start(bf16[20,8,128]{2,1,0:T(8,128)(2,1)S(1)} %get-tuple-element.26), channel_id=1, source_target_pairs={{2,4},{4,2},{3,5},{5,3},{10,12},{12,10},{11,13},{13,11},{18,20},{2... | collective-permute-start | bytes 122888 | tf_op jit(solution)/shard_map/ppermute | solution.py:319
  16.7 0.0 collective-permute-done.got_0
  16.7 1.4 %collective-permute-done.1.got_1 = bf16[20,8,128]{2,1,0:T(8,128)(2,1)S(1)} collective-permute-done((bf16[20,8,128]{2,1,0:T(8,128)(2,1)S(1)}, bf16[20,8,128]{2,1,0:T(8,128)(2,1)S(1)}, u32[]{:S(2)}, u32[]{:S(2)}) %collective-permute-start.1) | collective-permute-done | bytes 40992 | tf_op jit(solution)/shard_map/ppermute | solution.py:319
  18.1 2.0 %collective-permute-start.4 = (bf16[64,128]{1,0:T(8,128)(2,1)S(1)}, bf16[64,128]{1,0:T(8,128)(2,1)S(1)}, u32[]{:S(2)}, u32[]{:S(2)}) collective-permute-start(bf16[64,128]{1,0:T(8,128)(2,1)S(1)} %get-tuple-element.31), channel_id=1, source_target_pairs={{0,8},{16,24},{32,40},{48,56},{64,72},{80,88},{96,104},{112,120},{... | collective-permute-start | bytes 49160 | tf_op jit(solution)/shard_map/ppermute | solution.py:319
  20.0 8.1 %collective-permute-start.5 = (bf16[64,128]{1,0:T(8,128)(2,1)S(1)}, bf16[64,128]{1,0:T(8,128)(2,1)S(1)}, u32[]{:S(2)}, u32[]{:S(2)}) collective-permute-start(bf16[64,128]{1,0:T(8,128)(2,1)S(1)} %get-tuple-element.32), channel_id=1, source_target_pairs={{8,16},{24,32},{40,48},{56,64},{72,80},{88,96},{104,112},{120,128}... | collective-permute-start | bytes 49160 | tf_op jit(solution)/shard_map/ppermute | solution.py:319
  28.2 0.0 copy-start.1
  28.2 0.2 shard_map.92.act_up
  28.4 0.0 collective-permute-done.4.cor_0
  28.4 0.8 %collective-permute-done.5.cor_1 = bf16[64,128]{1,0:T(8,128)(2,1)S(1)} collective-permute-done((bf16[64,128]{1,0:T(8,128)(2,1)S(1)}, bf16[64,128]{1,0:T(8,128)(2,1)S(1)}, u32[]{:S(2)}, u32[]{:S(2)}) %collective-permute-start.5) | collective-permute-done | bytes 16416 | tf_op jit(solution)/shard_map/ppermute | solution.py:319
  29.3 0.0 collective-permute-done.2.row_0
  29.3 0.0 collective-permute-done.3.row_1
  29.3 0.0 copy-done
  29.3 0.3 shard_map.94
  29.6 0.0 copy-start.2
  29.6 34.0 %collective-permute-start.6 = (bf16[12,352,128]{2,1,0:T(8,128)(2,1)S(1)}, bf16[12,352,128]{2,1,0:T(8,128)(2,1)S(1)}, u32[]{:S(2)}, u32[]{:S(2)}) collective-permute-start(bf16[12,352,128]{2,1,0:T(8,128)(2,1)S(1)} %get-tuple-element.33), channel_id=1, source_target_pairs={{0,1},{1,0},{2,3},{3,2},{4,5},{5,4},{6,7},{7,6},{8,9},{9,8},{10,11... | collective-permute-start | bytes 3244040 | tf_op jit(solution)/shard_map/ppermute | solution.py:323
  63.7 0.0 copy-done.1
  63.7 1.6 %shard_map.95.part_in = f32[6,352,128]{2,1,0:T(8,128)S(1)} custom-call(bf16[8,320,128]{2,1,0:T(8,128)(2,1)S(1)} %bitcast.9, bf16[4,320,128]{2,1,0:T(8,128)(2,1)S(1)} %shard_map.92.act_up, bf16[320,128]{1,0:T(8,128)(2,1)S(1)} %get-tuple-element.27.merged, bf16[64,128]{1,0:T(8,128)(2,1)S(1)} %get-tuple-element.28.act_edge, ...), custom_call_target="tpu_custom_call" | custom-call | flops 1509949440 | bytes 4000000 | tf_op jit(solution)/shard_map/pallas_call | solution.py:29
  65.3 0.0 copy-done.2
  65.3 1.2 %shard_map.96 = (f32[4,352,128]{2,1,0:T(8,128)S(1)}, bf16[10,352,128]{2,1,0:T(8,128)(2,1)S(1)}) custom-call(bf16[8,320,128]{2,1,0:T(8,128)(2,1)S(1)} %bitcast.10, bf16[4,320,128]{2,1,0:T(8,128)(2,1)S(1)} %shard_map.92.act_up, bf16[320,128]{1,0:T(8,128)(2,1)S(1)} %get-tuple-element.27.merged, bf16[64,128]{1,0:T(8,128)(2,1)S(1)} %get-tuple-element.28.act_edge, ...), custom_call_target="tpu_custom_call" | custom-call | flops 754974720 | bytes 4000000 | tf_op jit(solution)/shard_map/pallas_call | solution.py:29
  66.5 0.0 collective-permute-done.6.middle
  66.5 0.0 copy-start.3
  66.5 1.9 %shard_map.97 = (bf16[10,352,128]{2,1,0:T(8,128)(2,1)S(1)}, bf16[10,352,128]{2,1,0:T(8,128)(2,1)S(1)}) custom-call(bf16[12,352,128]{2,1,0:T(8,128)(2,1)S(1)} %collective-permute-done.6.middle, f32[6,352,128]{2,1,0:T(8,128)S(1)} %shard_map.95.part_in, f32[4,352,128]{2,1,0:T(8,128)S(1)} %get-tuple-element.36.part_out, ...), custom_call_target="tpu_custom_call" | custom-call | flops 754974720 | bytes 6000000 | tf_op jit(solution)/shard_map/pallas_call | solution.py:29
  68.5 2.0 %collective-permute-start.7 = (bf16[10,352,128]{2,1,0:T(8,128)(2,1)S(1)}, bf16[10,352,128]{2,1,0:T(8,128)(2,1)S(1)}, u32[]{:S(2)}, u32[]{:S(2)}) collective-permute-start(bf16[10,352,128]{2,1,0:T(8,128)(2,1)S(1)} %get-tuple-element.39), channel_id=1, source_target_pairs={{0,1},{1,0},{2,3},{3,2},{4,5},{5,4},{6,7},{7,6},{8,9},{9,8},{10,11... | collective-permute-start | bytes 2703368 | tf_op jit(solution)/shard_map/ppermute | solution.py:323
  70.4 0.0 copy-done.3
  70.4 2.1 %shard_map.98.part = f32[8,320,128]{2,1,0:T(8,128)S(1)} custom-call(bf16[10,352,128]{2,1,0:T(8,128)(2,1)S(1)} %get-tuple-element.38.two_frame, bf16[10,352,128]{2,1,0:T(8,128)(2,1)S(1)} %get-tuple-element.40.act_two, bf16[3,3,3,128,128]{4,3,2,1,0:T(8,128)(2,1)S(1)} %copy-done.3, bf16[4,160,128]{2,1,0:T(8,128)(2,1)S(1)} %get-tuple-element.41.proj, ...), custom_call_target="tpu_custom_call" | custom-call | flops 1509949440 | bytes 6000000 | tf_op jit(solution)/shard_map/pallas_call | solution.py:29
  72.6 0.3 collective-permute-done.7.middle
  72.8 2.0 %shard_map.99 = bf16[8,320,128]{2,1,0:T(8,128)(2,1)} custom-call(bf16[10,352,128]{2,1,0:T(8,128)(2,1)S(1)} %collective-permute-done.7.middle, f32[8,320,128]{2,1,0:T(8,128)S(1)} %shard_map.98.part, bf16[3,3,3,128,128]{4,3,2,1,0:T(8,128)(2,1)S(1)} %copy-done.3), custom_call_target="tpu_custom_call" | custom-call | flops 754974720 | bytes 6000000 | tf_op jit(solution)/shard_map/pallas_call | solution.py:29
  (1 shorter events, 0.0 us)
Async XLA Ops:
  0.0 29.3 %copy-start = (bf16[1,8,320,128]{3,2,1,0:T(8,128)(2,1)S(1)}, bf16[1,8,320,128]{3,2,1,0:T(8,128)(2,1)}, u32[]{:S(2)}) copy-start(bf16[1,8,320,128]{3,2,1,0:T(8,128)(2,1)} %param.12) | copy-start | bytes 1966084
  1.5 27.8 %collective-permute-start.2 = (bf16[1120,128]{1,0:T(8,128)(2,1)S(1)}, bf16[1120,128]{1,0:T(8,128)(2,1)S(1)}, u32[]{:S(2)}, u32[]{:S(2)}) collective-permute-start(bf16[1120,128]{1,0:T(8,128)(2,1)S(1)} %get-tuple-element.29), channel_id=1, source_target_pairs={{0,8},{16,24},{32,40},{48,56},{64,72},{80,88},{96,104},{112,120},{... | collective-permute-start | bytes 860168 | tf_op jit(solution)/shard_map/ppermute | solution.py:319
  3.5 25.8 %collective-permute-start.3 = (bf16[1120,128]{1,0:T(8,128)(2,1)S(1)}, bf16[1120,128]{1,0:T(8,128)(2,1)S(1)}, u32[]{:S(2)}, u32[]{:S(2)}) collective-permute-start(bf16[1120,128]{1,0:T(8,128)(2,1)S(1)} %get-tuple-element.30), channel_id=1, source_target_pairs={{8,16},{24,32},{40,48},{56,64},{72,80},{88,96},{104,112},{120,128}... | collective-permute-start | bytes 860168 | tf_op jit(solution)/shard_map/ppermute | solution.py:319
  10.4 6.3 %collective-permute-start = (bf16[20,8,128]{2,1,0:T(8,128)(2,1)S(1)}, bf16[20,8,128]{2,1,0:T(8,128)(2,1)S(1)}, u32[]{:S(2)}, u32[]{:S(2)}) collective-permute-start(bf16[20,8,128]{2,1,0:T(8,128)(2,1)S(1)} %get-tuple-element.25), channel_id=1, source_target_pairs={{0,2},{4,6},{2,0},{6,4},{1,3},{5,7},{3,1},{7,5},{8,10},{12,14},{10... | collective-permute-start | bytes 122888 | tf_op jit(solution)/shard_map/ppermute | solution.py:319
  12.5 5.6 %collective-permute-start.1 = (bf16[20,8,128]{2,1,0:T(8,128)(2,1)S(1)}, bf16[20,8,128]{2,1,0:T(8,128)(2,1)S(1)}, u32[]{:S(2)}, u32[]{:S(2)}) collective-permute-start(bf16[20,8,128]{2,1,0:T(8,128)(2,1)S(1)} %get-tuple-element.26), channel_id=1, source_target_pairs={{2,4},{4,2},{3,5},{5,3},{10,12},{12,10},{11,13},{13,11},{18,20},{2... | collective-permute-start | bytes 122888 | tf_op jit(solution)/shard_map/ppermute | solution.py:319
  18.1 10.3 %collective-permute-start.4 = (bf16[64,128]{1,0:T(8,128)(2,1)S(1)}, bf16[64,128]{1,0:T(8,128)(2,1)S(1)}, u32[]{:S(2)}, u32[]{:S(2)}) collective-permute-start(bf16[64,128]{1,0:T(8,128)(2,1)S(1)} %get-tuple-element.31), channel_id=1, source_target_pairs={{0,8},{16,24},{32,40},{48,56},{64,72},{80,88},{96,104},{112,120},{... | collective-permute-start | bytes 49160 | tf_op jit(solution)/shard_map/ppermute | solution.py:319
  20.0 9.2 %collective-permute-start.5 = (bf16[64,128]{1,0:T(8,128)(2,1)S(1)}, bf16[64,128]{1,0:T(8,128)(2,1)S(1)}, u32[]{:S(2)}, u32[]{:S(2)}) collective-permute-start(bf16[64,128]{1,0:T(8,128)(2,1)S(1)} %get-tuple-element.32), channel_id=1, source_target_pairs={{8,16},{24,32},{40,48},{56,64},{72,80},{88,96},{104,112},{120,128}... | collective-permute-start | bytes 49160 | tf_op jit(solution)/shard_map/ppermute | solution.py:319
  28.2 35.5 %copy-start.1 = (bf16[3,3,3,128,128]{4,3,2,1,0:T(8,128)(2,1)S(1)}, bf16[3,3,3,128,128]{4,3,2,1,0:T(8,128)(2,1)}, u32[]{:S(2)}) copy-start(bf16[3,3,3,128,128]{4,3,2,1,0:T(8,128)(2,1)} %weight.9) | copy-start | bytes 2654212
  29.6 35.7 %copy-start.2 = (bf16[1,8,320,128]{3,2,1,0:T(8,128)(2,1)S(1)}, bf16[1,8,320,128]{3,2,1,0:T(8,128)(2,1)}, u32[]{:S(2)}) copy-start(bf16[1,8,320,128]{3,2,1,0:T(8,128)(2,1)} %param.13) | copy-start | bytes 1966084
  29.6 36.9 %collective-permute-start.6 = (bf16[12,352,128]{2,1,0:T(8,128)(2,1)S(1)}, bf16[12,352,128]{2,1,0:T(8,128)(2,1)S(1)}, u32[]{:S(2)}, u32[]{:S(2)}) collective-permute-start(bf16[12,352,128]{2,1,0:T(8,128)(2,1)S(1)} %get-tuple-element.33), channel_id=1, source_target_pairs={{0,1},{1,0},{2,3},{3,2},{4,5},{5,4},{6,7},{7,6},{8,9},{9,8},{10,11... | collective-permute-start | bytes 3244040 | tf_op jit(solution)/shard_map/ppermute | solution.py:323
  66.5 3.9 %copy-start.3 = (bf16[3,3,3,128,128]{4,3,2,1,0:T(8,128)(2,1)S(1)}, bf16[3,3,3,128,128]{4,3,2,1,0:T(8,128)(2,1)}, u32[]{:S(2)}) copy-start(bf16[3,3,3,128,128]{4,3,2,1,0:T(8,128)(2,1)} %weight.11) | copy-start | bytes 2654212
  68.5 4.4 %collective-permute-start.7 = (bf16[10,352,128]{2,1,0:T(8,128)(2,1)S(1)}, bf16[10,352,128]{2,1,0:T(8,128)(2,1)S(1)}, u32[]{:S(2)}, u32[]{:S(2)}) collective-permute-start(bf16[10,352,128]{2,1,0:T(8,128)(2,1)S(1)} %get-tuple-element.39), channel_id=1, source_target_pairs={{0,1},{1,0},{2,3},{3,2},{4,5},{5,4},{6,7},{7,6},{8,9},{9,8},{10,11... | collective-permute-start | bytes 2703368 | tf_op jit(solution)/shard_map/ppermute | solution.py:323

commit v7 on v6

--- a/solution.py
+++ b/solution.py
@@ -51,28 +51,29 @@
     return pl.multiple_of(start, step) if step > 1 else start
 
 
+def project(x, weight, bias):
+    p = (jnp.dot(x, weight, preferred_element_type=F32) + bias).astype(BF)
+    return p, silu(p.astype(F32)).astype(BF)
+
+
 def first_kernel(
     latent, weight, bias, one, two, bias_one, bias_two,
-    proj, act, row_0, row_1, col_0, col_1, b_one, b_two,
-    latent_v, weight_v, bias_v, sems,
+    col_0, col_1, weight_v, bias_v, b_one, b_two,
+    latent_v, sems,
 ):
     rows, cols, _ = one.shape
     crows, ccols, _ = latent.shape
-    copies = [(latent, latent_v), (weight, weight_v), (bias, bias_v)]
+    copies = [(weight, weight_v), (bias, bias_v)]
+    sends = ((col_0, False), (col_1, True))
+    for n, (col_s, flip) in enumerate(sends):
+        lo, hi = (ccols - E, 0) if flip else (0, ccols - E)
+        copies.append((latent.at[:, pl.ds(pick("col", hi, lo, E), E)], latent_v.at[n]))
     n_first = len(copies)
-    t0 = 2 * cols + ccols
-    sends = ((row_0, col_0, False), (row_1, col_1, True))
-    for row_s, col_s, flip in sends:
+    for col_s, flip in sends:
         lo, hi = (cols - E, 0) if flip else (0, cols - E)
         c = pl.ds(pick("col", hi, lo, E), E)
         copies.append((one.at[:, c], col_s.at[0:rows]))
         copies.append((two.at[:, c], col_s.at[rows + crows :]))
-        lo, hi = (rows - 2, 0) if flip else (0, rows - 2)
-        r = pick("row", hi, lo)
-        for k in range(2):
-            copies.append((one.at[r + k], row_s.at[k * cols : (k + 1) * cols]))
-        lo, hi = (rows - 1, 0) if flip else (0, rows - 1)
-        copies.append((two.at[pick("row", hi, lo)], row_s.at[t0 : t0 + cols]))
     copies.append((bias_one, b_one))
     copies.append((bias_two, b_two))
     started = [pltpu.make_async_copy(s, d, sems.at[i]) for i, (s, d) in enumerate(copies)]
@@ -80,19 +81,31 @@
         c.start()
     for c in started[:n_first]:
         c.wait()
+    edges = jnp.concatenate([latent_v[n, i] for n in range(2) for i in range(crows)], axis=0)
+    _, a = project(edges, weight_v[...], bias_v[...])
+    for n, (col_s, _) in enumerate(sends):
+        for i in range(crows):
+            o = (n * crows + i) * E
+            col_s[rows + i] = a[o : o + E]
+    for c in started[n_first:]:
+        c.wait()
+
+
+def rows_kernel(latent, weight, bias, one, two, proj, act, row_0, row_1):
+    rows, cols, _ = one.shape
+    crows, ccols, _ = latent.shape
     for i in range(crows):
-        p = (jnp.dot(latent_v[i], weight_v[...], preferred_element_type=F32) + bias_v[...]).astype(BF)
-        proj[i] = p
-        act[i] = silu(p.astype(F32)).astype(BF)
-    for row_s, col_s, flip in sends:
+        proj[i], act[i] = project(latent[i], weight[...], bias[...])
+    t0 = 2 * cols + ccols
+    for row_s, flip in ((row_0, False), (row_1, True)):
+        lo, hi = (rows - 2, 0) if flip else (0, rows - 2)
+        r = pick("row", hi, lo)
+        for k in range(2):
+            row_s[k * cols : (k + 1) * cols, :] = one[r + k]
         lo, hi = (crows - 1, 0) if flip else (0, crows - 1)
         row_s[2 * cols : t0, :] = act[pick("row", hi, lo)]
-        lo, hi = (ccols - E, 0) if flip else (0, ccols - E)
-        c = pl.ds(pick("col", hi, lo, E), E)
-        for i in range(crows):
-            col_s[rows + i] = act[i, c, :]
-    for c in started[n_first:]:
-        c.wait()
+        lo, hi = (rows - 1, 0) if flip else (0, rows - 1)
+        row_s[t0:, :] = two[pick("row", hi, lo)]
 
 
 def corner_kernel(rows, crows, got_0, got_1, merged, act_edge, cor_0, cor_1):
@@ -332,29 +345,21 @@
     col_shape = (2 * rows + crows, E, ch)
     n_row = 3 * cols + ccols
     sums = pltpu.VMEM((4, span + 16, 2 * ch), F32)
-    proj, act, row_0, row_1, col_0, col_1, b_one, b_two = call(
+    col_0, col_1, weight_v, bias_v, b_one, b_two = call(
         first_kernel,
-        [
-            ((crows, ccols, ch), BF),
-            ((crows, ccols, ch), BF),
-            ((n_row, ch), BF),
-            ((n_row, ch), BF),
-            (col_shape, BF),
-            (col_shape, BF),
-            ((1, ch), F32),
-            ((1, ch), F32),
-        ],
+        [(col_shape, BF), (col_shape, BF), ((lch, ch), BF), ((1, ch), F32), ((1, ch), F32), ((1, ch), F32)],
         [HBM] * 7,
-        scratch=[
-            pltpu.VMEM((crows, ccols, lch), BF),
-            pltpu.VMEM((lch, ch), BF),
-            pltpu.VMEM((1, ch), F32),
-            pltpu.SemaphoreType.DMA((15,)),
-        ],
+        scratch=[pltpu.VMEM((2, crows, E, lch), BF), pltpu.SemaphoreType.DMA((10,))],
+        flops=10**7,
+        nbytes=5 * 10**5,
+    )(latent, proj_weight, proj_bias.reshape(1, ch), one, two, bias_one.reshape(1, ch), bias_two.reshape(1, ch))
+    proj, act, row_0, row_1 = call(
+        rows_kernel,
+        [((crows, ccols, ch), BF), ((crows, ccols, ch), BF), ((n_row, ch), BF), ((n_row, ch), BF)],
+        [VMEM] * 5,
         flops=10**8,
         nbytes=2 * 10**6,
-        limit=24,
-    )(latent, proj_weight, proj_bias.reshape(1, ch), one, two, bias_one.reshape(1, ch), bias_two.reshape(1, ch))
+    )(latent, weight_v, bias_v, one, two)
     got_1 = exchange(col_1, "col", 1)
     got_0 = exchange(col_0, "col", 0)
     row_1 = exchange(row_1, "row", 1)

time: 75.2 us -> 75.2 us (level)
    pallas_call x9 -> x10, Pallas kernels: 10.9 us -> 10.9 us  [call(): run(*(held(v, spec) for v, spec in zip(args, specs, strict=True)))]
where the time goes in v7:
time: 75.2 us; the launch traced here: 74.9 us
  starting transfers between devices  61.1 us (81%)
  Pallas kernels  10.9 us (14%)
  waiting for transfers between devices  2.47 us (3%)
    ppermute x2, starting transfers between devices, swap(): return lax.ppermute(x, 'frm', [(0, 1), (1, 0)])  35.9 us
    ppermute x6, starting transfers between devices, exchange(): return lax.ppermute(x, axis, pairs + [(j, i) for i, j in pairs])  25.2 us
    pallas_call x10, Pallas kernels, call(): run(*(held(v, spec) for v, spec in zip(args, specs, strict=True)))  10.9 us
    ppermute x6, waiting for transfers between devices, exchange(): return lax.ppermute(x, axis, pairs + [(j, i) for i, j in pairs])  2.23 us
  transfers between devices with their start and end apart: 8, of which 3 were waited for; matrix products, arithmetic and copies ran while one was open for 0% of the time, Pallas kernels for 7%

profile of v7, /device:TPU:99, one launch (start us, length us, event | category | flops | bytes accessed | tf_op | source)
XLA Modules:
  0.0 74.9 jit_solution(15559662872748223016)
XLA Ops:
  0.0 1.2 %shard_map.91 = (bf16[20,8,128]{2,1,0:T(8,128)(2,1)S(1)}, bf16[20,8,128]{2,1,0:T(8,128)(2,1)S(1)}, bf16[256,128]{1,0:T(8,128)(2,1)S(1)}, f32[1,128]{1,0:T(1,128)...) custom-call(bf16[4,160,256]{2,1,0:T(8,128)(2,1)} %bitcast.15, bf16[256,128]{1,0:T(8,128)(2,1)} %weight.6, ...), custom_call_target="tpu_custom_call" | custom-call | flops 10000000 | bytes 500000 | tf_op jit(solution)/shard_map/pallas_call | solution.py:29
  1.2 0.0 copy-done.1
  1.3 0.1 copy-done
  1.4 0.1 copy-done.3
  1.5 0.3 shard_map.92
  1.8 1.9 %collective-permute-start.2 = (bf16[1120,128]{1,0:T(8,128)(2,1)S(1)}, bf16[1120,128]{1,0:T(8,128)(2,1)S(1)}, u32[]{:S(2)}, u32[]{:S(2)}) collective-permute-start(bf16[1120,128]{1,0:T(8,128)(2,1)S(1)} %get-tuple-element.33), channel_id=1, source_target_pairs={{0,8},{16,24},{32,40},{48,56},{64,72},{80,88},{96,104},{112,120},{... | collective-permute-start | bytes 860168 | tf_op jit(solution)/shard_map/ppermute | solution.py:332
  3.7 6.9 %collective-permute-start.3 = (bf16[1120,128]{1,0:T(8,128)(2,1)S(1)}, bf16[1120,128]{1,0:T(8,128)(2,1)S(1)}, u32[]{:S(2)}, u32[]{:S(2)}) collective-permute-start(bf16[1120,128]{1,0:T(8,128)(2,1)S(1)} %get-tuple-element.34), channel_id=1, source_target_pairs={{8,16},{24,32},{40,48},{56,64},{72,80},{88,96},{104,112},{120,128}... | collective-permute-start | bytes 860168 | tf_op jit(solution)/shard_map/ppermute | solution.py:332
  10.7 2.1 %collective-permute-start = (bf16[20,8,128]{2,1,0:T(8,128)(2,1)S(1)}, bf16[20,8,128]{2,1,0:T(8,128)(2,1)S(1)}, u32[]{:S(2)}, u32[]{:S(2)}) collective-permute-start(bf16[20,8,128]{2,1,0:T(8,128)(2,1)S(1)} %get-tuple-element.29), channel_id=1, source_target_pairs={{0,2},{4,6},{2,0},{6,4},{1,3},{5,7},{3,1},{7,5},{8,10},{12,14},{10... | collective-permute-start | bytes 122888 | tf_op jit(solution)/shard_map/ppermute | solution.py:332
  12.7 4.2 %collective-permute-start.1 = (bf16[20,8,128]{2,1,0:T(8,128)(2,1)S(1)}, bf16[20,8,128]{2,1,0:T(8,128)(2,1)S(1)}, u32[]{:S(2)}, u32[]{:S(2)}) collective-permute-start(bf16[20,8,128]{2,1,0:T(8,128)(2,1)S(1)} %get-tuple-element.30), channel_id=1, source_target_pairs={{2,4},{4,2},{3,5},{5,3},{10,12},{12,10},{11,13},{13,11},{18,20},{2... | collective-permute-start | bytes 122888 | tf_op jit(solution)/shard_map/ppermute | solution.py:332
  16.9 0.0 collective-permute-done.got_0
  17.0 1.4 %collective-permute-done.1.got_1 = bf16[20,8,128]{2,1,0:T(8,128)(2,1)S(1)} collective-permute-done((bf16[20,8,128]{2,1,0:T(8,128)(2,1)S(1)}, bf16[20,8,128]{2,1,0:T(8,128)(2,1)S(1)}, u32[]{:S(2)}, u32[]{:S(2)}) %collective-permute-start.1) | collective-permute-done | bytes 40992 | tf_op jit(solution)/shard_map/ppermute | solution.py:332
  18.4 2.0 %collective-permute-start.4 = (bf16[64,128]{1,0:T(8,128)(2,1)S(1)}, bf16[64,128]{1,0:T(8,128)(2,1)S(1)}, u32[]{:S(2)}, u32[]{:S(2)}) collective-permute-start(bf16[64,128]{1,0:T(8,128)(2,1)S(1)} %get-tuple-element.35), channel_id=1, source_target_pairs={{0,8},{16,24},{32,40},{48,56},{64,72},{80,88},{96,104},{112,120},{... | collective-permute-start | bytes 49160 | tf_op jit(solution)/shard_map/ppermute | solution.py:332
  20.3 8.1 %collective-permute-start.5 = (bf16[64,128]{1,0:T(8,128)(2,1)S(1)}, bf16[64,128]{1,0:T(8,128)(2,1)S(1)}, u32[]{:S(2)}, u32[]{:S(2)}) collective-permute-start(bf16[64,128]{1,0:T(8,128)(2,1)S(1)} %get-tuple-element.36), channel_id=1, source_target_pairs={{8,16},{24,32},{40,48},{56,64},{72,80},{88,96},{104,112},{120,128}... | collective-permute-start | bytes 49160 | tf_op jit(solution)/shard_map/ppermute | solution.py:332
  28.5 0.0 copy-start.2
  28.5 0.2 shard_map.93.act_up
  28.7 0.0 collective-permute-done.4.cor_0
  28.7 0.8 %collective-permute-done.5.cor_1 = bf16[64,128]{1,0:T(8,128)(2,1)S(1)} collective-permute-done((bf16[64,128]{1,0:T(8,128)(2,1)S(1)}, bf16[64,128]{1,0:T(8,128)(2,1)S(1)}, u32[]{:S(2)}, u32[]{:S(2)}) %collective-permute-start.5) | collective-permute-done | bytes 16416 | tf_op jit(solution)/shard_map/ppermute | solution.py:332
  29.6 0.0 collective-permute-done.2.row_0
  29.6 0.0 collective-permute-done.3.row_1
  29.6 0.3 shard_map.95
  29.9 33.9 %collective-permute-start.6 = (bf16[12,352,128]{2,1,0:T(8,128)(2,1)S(1)}, bf16[12,352,128]{2,1,0:T(8,128)(2,1)S(1)}, u32[]{:S(2)}, u32[]{:S(2)}) collective-permute-start(bf16[12,352,128]{2,1,0:T(8,128)(2,1)S(1)} %get-tuple-element.37), channel_id=1, source_target_pairs={{0,1},{1,0},{2,3},{3,2},{4,5},{5,4},{6,7},{7,6},{8,9},{9,8},{10,11... | collective-permute-start | bytes 3244040 | tf_op jit(solution)/shard_map/ppermute | solution.py:336
  63.8 0.0 copy-done.2
  63.8 1.6 %shard_map.96.part_in = f32[6,352,128]{2,1,0:T(8,128)S(1)} custom-call(bf16[8,320,128]{2,1,0:T(8,128)(2,1)S(1)} %bitcast.10, bf16[4,320,128]{2,1,0:T(8,128)(2,1)S(1)} %shard_map.93.act_up, bf16[320,128]{1,0:T(8,128)(2,1)S(1)} %get-tuple-element.31.merged, bf16[64,128]{1,0:T(8,128)(2,1)S(1)} %get-tuple-element.32.act_edge, ...), custom_call_target="tpu_custom_call" | custom-call | flops 1509949440 | bytes 4000000 | tf_op jit(solution)/shard_map/pallas_call | solution.py:29
  65.4 1.2 %shard_map.97 = (f32[4,352,128]{2,1,0:T(8,128)S(1)}, bf16[10,352,128]{2,1,0:T(8,128)(2,1)S(1)}) custom-call(bf16[8,320,128]{2,1,0:T(8,128)(2,1)S(1)} %bitcast.11, bf16[4,320,128]{2,1,0:T(8,128)(2,1)S(1)} %shard_map.93.act_up, bf16[320,128]{1,0:T(8,128)(2,1)S(1)} %get-tuple-element.31.merged, bf16[64,128]{1,0:T(8,128)(2,1)S(1)} %get-tuple-element.32.act_edge, ...), custom_call_target="tpu_custom_call" | custom-call | flops 754974720 | bytes 4000000 | tf_op jit(solution)/shard_map/pallas_call | solution.py:29
  66.6 0.0 collective-permute-done.6.middle
  66.6 0.0 copy-start.4
  66.6 1.9 %shard_map.98 = (bf16[10,352,128]{2,1,0:T(8,128)(2,1)S(1)}, bf16[10,352,128]{2,1,0:T(8,128)(2,1)S(1)}) custom-call(bf16[12,352,128]{2,1,0:T(8,128)(2,1)S(1)} %collective-permute-done.6.middle, f32[6,352,128]{2,1,0:T(8,128)S(1)} %shard_map.96.part_in, f32[4,352,128]{2,1,0:T(8,128)S(1)} %get-tuple-element.40.part_out, ...), custom_call_target="tpu_custom_call" | custom-call | flops 754974720 | bytes 6000000 | tf_op jit(solution)/shard_map/pallas_call | solution.py:29
  68.5 2.0 %collective-permute-start.7 = (bf16[10,352,128]{2,1,0:T(8,128)(2,1)S(1)}, bf16[10,352,128]{2,1,0:T(8,128)(2,1)S(1)}, u32[]{:S(2)}, u32[]{:S(2)}) collective-permute-start(bf16[10,352,128]{2,1,0:T(8,128)(2,1)S(1)} %get-tuple-element.43), channel_id=1, source_target_pairs={{0,1},{1,0},{2,3},{3,2},{4,5},{5,4},{6,7},{7,6},{8,9},{9,8},{10,11... | collective-permute-start | bytes 2703368 | tf_op jit(solution)/shard_map/ppermute | solution.py:336
  70.4 0.0 copy-done.4
  70.4 2.2 %shard_map.99.part = f32[8,320,128]{2,1,0:T(8,128)S(1)} custom-call(bf16[10,352,128]{2,1,0:T(8,128)(2,1)S(1)} %get-tuple-element.42.two_frame, bf16[10,352,128]{2,1,0:T(8,128)(2,1)S(1)} %get-tuple-element.44.act_two, bf16[3,3,3,128,128]{4,3,2,1,0:T(8,128)(2,1)S(1)} %copy-done.4, bf16[4,160,128]{2,1,0:T(8,128)(2,1)S(1)} %get-tuple-element.45.proj, ...), custom_call_target="tpu_custom_call" | custom-call | flops 1509949440 | bytes 6000000 | tf_op jit(solution)/shard_map/pallas_call | solution.py:29
  72.6 0.2 collective-permute-done.7.middle
  72.9 2.0 %shard_map.100 = bf16[8,320,128]{2,1,0:T(8,128)(2,1)} custom-call(bf16[10,352,128]{2,1,0:T(8,128)(2,1)S(1)} %collective-permute-done.7.middle, f32[8,320,128]{2,1,0:T(8,128)S(1)} %shard_map.99.part, bf16[3,3,3,128,128]{4,3,2,1,0:T(8,128)(2,1)S(1)} %copy-done.4), custom_call_target="tpu_custom_call" | custom-call | flops 754974720 | bytes 6000000 | tf_op jit(solution)/shard_map/pallas_call | solution.py:29
  (4 shorter events, 0.0 us)
Async XLA Ops:
  0.0 1.2 %copy-start.1 = (bf16[1,8,320,128]{3,2,1,0:T(8,128)(2,1)S(1)}, bf16[1,8,320,128]{3,2,1,0:T(8,128)(2,1)}, u32[]{:S(2)}) copy-start(bf16[1,8,320,128]{3,2,1,0:T(8,128)(2,1)} %param.13) | copy-start | bytes 1966084
  0.0 1.4 %copy-start = (bf16[1,8,320,128]{3,2,1,0:T(8,128)(2,1)S(1)}, bf16[1,8,320,128]{3,2,1,0:T(8,128)(2,1)}, u32[]{:S(2)}) copy-start(bf16[1,8,320,128]{3,2,1,0:T(8,128)(2,1)} %param.12) | copy-start | bytes 1966084
  0.0 1.5 %copy-start.3 = (bf16[1,4,160,256]{3,2,1,0:T(8,128)(2,1)S(1)}, bf16[1,4,160,256]{3,2,1,0:T(8,128)(2,1)}, u32[]{:S(2)}) copy-start(bf16[1,4,160,256]{3,2,1,0:T(8,128)(2,1)} %param.9) | copy-start | bytes 983044
  1.8 27.8 %collective-permute-start.2 = (bf16[1120,128]{1,0:T(8,128)(2,1)S(1)}, bf16[1120,128]{1,0:T(8,128)(2,1)S(1)}, u32[]{:S(2)}, u32[]{:S(2)}) collective-permute-start(bf16[1120,128]{1,0:T(8,128)(2,1)S(1)} %get-tuple-element.33), channel_id=1, source_target_pairs={{0,8},{16,24},{32,40},{48,56},{64,72},{80,88},{96,104},{112,120},{... | collective-permute-start | bytes 860168 | tf_op jit(solution)/shard_map/ppermute | solution.py:332
  3.7 25.8 %collective-permute-start.3 = (bf16[1120,128]{1,0:T(8,128)(2,1)S(1)}, bf16[1120,128]{1,0:T(8,128)(2,1)S(1)}, u32[]{:S(2)}, u32[]{:S(2)}) collective-permute-start(bf16[1120,128]{1,0:T(8,128)(2,1)S(1)} %get-tuple-element.34), channel_id=1, source_target_pairs={{8,16},{24,32},{40,48},{56,64},{72,80},{88,96},{104,112},{120,128}... | collective-permute-start | bytes 860168 | tf_op jit(solution)/shard_map/ppermute | solution.py:332
  10.7 6.3 %collective-permute-start = (bf16[20,8,128]{2,1,0:T(8,128)(2,1)S(1)}, bf16[20,8,128]{2,1,0:T(8,128)(2,1)S(1)}, u32[]{:S(2)}, u32[]{:S(2)}) collective-permute-start(bf16[20,8,128]{2,1,0:T(8,128)(2,1)S(1)} %get-tuple-element.29), channel_id=1, source_target_pairs={{0,2},{4,6},{2,0},{6,4},{1,3},{5,7},{3,1},{7,5},{8,10},{12,14},{10... | collective-permute-start | bytes 122888 | tf_op jit(solution)/shard_map/ppermute | solution.py:332
  12.7 5.6 %collective-permute-start.1 = (bf16[20,8,128]{2,1,0:T(8,128)(2,1)S(1)}, bf16[20,8,128]{2,1,0:T(8,128)(2,1)S(1)}, u32[]{:S(2)}, u32[]{:S(2)}) collective-permute-start(bf16[20,8,128]{2,1,0:T(8,128)(2,1)S(1)} %get-tuple-element.30), channel_id=1, source_target_pairs={{2,4},{4,2},{3,5},{5,3},{10,12},{12,10},{11,13},{13,11},{18,20},{2... | collective-permute-start | bytes 122888 | tf_op jit(solution)/shard_map/ppermute | solution.py:332
  18.4 10.4 %collective-permute-start.4 = (bf16[64,128]{1,0:T(8,128)(2,1)S(1)}, bf16[64,128]{1,0:T(8,128)(2,1)S(1)}, u32[]{:S(2)}, u32[]{:S(2)}) collective-permute-start(bf16[64,128]{1,0:T(8,128)(2,1)S(1)} %get-tuple-element.35), channel_id=1, source_target_pairs={{0,8},{16,24},{32,40},{48,56},{64,72},{80,88},{96,104},{112,120},{... | collective-permute-start | bytes 49160 | tf_op jit(solution)/shard_map/ppermute | solution.py:332
  20.3 9.3 %collective-permute-start.5 = (bf16[64,128]{1,0:T(8,128)(2,1)S(1)}, bf16[64,128]{1,0:T(8,128)(2,1)S(1)}, u32[]{:S(2)}, u32[]{:S(2)}) collective-permute-start(bf16[64,128]{1,0:T(8,128)(2,1)S(1)} %get-tuple-element.36), channel_id=1, source_target_pairs={{8,16},{24,32},{40,48},{56,64},{72,80},{88,96},{104,112},{120,128}... | collective-permute-start | bytes 49160 | tf_op jit(solution)/shard_map/ppermute | solution.py:332
  28.5 35.3 %copy-start.2 = (bf16[3,3,3,128,128]{4,3,2,1,0:T(8,128)(2,1)S(1)}, bf16[3,3,3,128,128]{4,3,2,1,0:T(8,128)(2,1)}, u32[]{:S(2)}) copy-start(bf16[3,3,3,128,128]{4,3,2,1,0:T(8,128)(2,1)} %weight.9) | copy-start | bytes 2654212
  29.9 36.7 %collective-permute-start.6 = (bf16[12,352,128]{2,1,0:T(8,128)(2,1)S(1)}, bf16[12,352,128]{2,1,0:T(8,128)(2,1)S(1)}, u32[]{:S(2)}, u32[]{:S(2)}) collective-permute-start(bf16[12,352,128]{2,1,0:T(8,128)(2,1)S(1)} %get-tuple-element.37), channel_id=1, source_target_pairs={{0,1},{1,0},{2,3},{3,2},{4,5},{5,4},{6,7},{7,6},{8,9},{9,8},{10,11... | collective-permute-start | bytes 3244040 | tf_op jit(solution)/shard_map/ppermute | solution.py:336
  66.6 3.9 %copy-start.4 = (bf16[3,3,3,128,128]{4,3,2,1,0:T(8,128)(2,1)S(1)}, bf16[3,3,3,128,128]{4,3,2,1,0:T(8,128)(2,1)}, u32[]{:S(2)}) copy-start(bf16[3,3,3,128,128]{4,3,2,1,0:T(8,128)(2,1)} %weight.11) | copy-start | bytes 2654212
  68.5 4.4 %collective-permute-start.7 = (bf16[10,352,128]{2,1,0:T(8,128)(2,1)S(1)}, bf16[10,352,128]{2,1,0:T(8,128)(2,1)S(1)}, u32[]{:S(2)}, u32[]{:S(2)}) collective-permute-start(bf16[10,352,128]{2,1,0:T(8,128)(2,1)S(1)} %get-tuple-element.43), channel_id=1, source_target_pairs={{0,1},{1,0},{2,3},{3,2},{4,5},{5,4},{6,7},{7,6},{8,9},{9,8},{10,11... | collective-permute-start | bytes 2703368 | tf_op jit(solution)/shard_map/ppermute | solution.py:336

commit v8 on v7

--- a/solution.py
+++ b/solution.py
@@ -232,21 +232,12 @@
                 put_row(act_border, h, wide[:, h * 128 : (h + 1) * 128], spread_edge(block(cor, 2)))
 
     lead = lax.axis_index("frm") == 0
-
-    @pl.when(lead)
-    def _():
-        for i in range(4):
-            send[i if i < 2 else rows + i] = act_border[i // 2]
-        for i in range(rows):
-            m = i // 2
-            put_row(send, i + 2, act_up[m], act_edge[m * B : (m + 1) * B, :])
-
-    @pl.when(jnp.logical_not(lead))
-    def _():
-        for i in range(4):
-            send[i if i < 2 else rows + i] = cache_border[i]
-        for i in range(rows):
-            put_row(send, i + 2, one[i], merged[i * B : (i + 1) * B, :])
+    for i in range(4):
+        send[i if i < 2 else rows + i] = jnp.where(lead, act_border[i // 2], cache_border[i])
+    for i in range(rows):
+        m = i // 2
+        edges = jnp.where(lead, act_edge[m * B : (m + 1) * B, :], merged[i * B : (i + 1) * B, :])
+        put_row(send, i + 2, jnp.where(lead, act_up[m], one[i]), edges)
 
 
 def outer_kernel(

time: 75.2 us -> 75.3 us (level)
  no operation moved by 1% of the time
where the time goes in v8:
time: 75.3 us; the launch traced here: 75 us
  starting transfers between devices  61 us (81%)
  Pallas kernels  11 us (15%)
  waiting for transfers between devices  2.47 us (3%)
    ppermute x2, starting transfers between devices, swap(): return lax.ppermute(x, 'frm', [(0, 1), (1, 0)])  35.8 us
    ppermute x6, starting transfers between devices, exchange(): return lax.ppermute(x, axis, pairs + [(j, i) for i, j in pairs])  25.2 us
    pallas_call x10, Pallas kernels, call(): run(*(held(v, spec) for v, spec in zip(args, specs, strict=True)))  11 us
    ppermute x6, waiting for transfers between devices, exchange(): return lax.ppermute(x, axis, pairs + [(j, i) for i, j in pairs])  2.23 us
  transfers between devices with their start and end apart: 8, of which 3 were waited for; matrix products, arithmetic and copies ran while one was open for 0% of the time, Pallas kernels for 7%

profile of v8, /device:TPU:99, one launch (start us, length us, event | category | flops | bytes accessed | tf_op | source)
XLA Modules:
  0.0 75.0 jit_solution(17556968965719093755)
XLA Ops:
  0.0 1.2 %shard_map.91 = (bf16[20,8,128]{2,1,0:T(8,128)(2,1)S(1)}, bf16[20,8,128]{2,1,0:T(8,128)(2,1)S(1)}, bf16[256,128]{1,0:T(8,128)(2,1)S(1)}, f32[1,128]{1,0:T(1,128)...) custom-call(bf16[4,160,256]{2,1,0:T(8,128)(2,1)} %bitcast.15, bf16[256,128]{1,0:T(8,128)(2,1)} %weight.6, ...), custom_call_target="tpu_custom_call" | custom-call | flops 10000000 | bytes 500000 | tf_op jit(solution)/shard_map/pallas_call | solution.py:29
  1.2 0.0 copy-done.1
  1.3 0.1 copy-done
  1.4 0.1 copy-done.3
  1.5 0.3 shard_map.92
  1.8 1.9 %collective-permute-start.2 = (bf16[1120,128]{1,0:T(8,128)(2,1)S(1)}, bf16[1120,128]{1,0:T(8,128)(2,1)S(1)}, u32[]{:S(2)}, u32[]{:S(2)}) collective-permute-start(bf16[1120,128]{1,0:T(8,128)(2,1)S(1)} %get-tuple-element.33), channel_id=1, source_target_pairs={{0,8},{16,24},{32,40},{48,56},{64,72},{80,88},{96,104},{112,120},{... | collective-permute-start | bytes 860168 | tf_op jit(solution)/shard_map/ppermute | solution.py:323
  3.7 6.9 %collective-permute-start.3 = (bf16[1120,128]{1,0:T(8,128)(2,1)S(1)}, bf16[1120,128]{1,0:T(8,128)(2,1)S(1)}, u32[]{:S(2)}, u32[]{:S(2)}) collective-permute-start(bf16[1120,128]{1,0:T(8,128)(2,1)S(1)} %get-tuple-element.34), channel_id=1, source_target_pairs={{8,16},{24,32},{40,48},{56,64},{72,80},{88,96},{104,112},{120,128}... | collective-permute-start | bytes 860168 | tf_op jit(solution)/shard_map/ppermute | solution.py:323
  10.7 2.1 %collective-permute-start = (bf16[20,8,128]{2,1,0:T(8,128)(2,1)S(1)}, bf16[20,8,128]{2,1,0:T(8,128)(2,1)S(1)}, u32[]{:S(2)}, u32[]{:S(2)}) collective-permute-start(bf16[20,8,128]{2,1,0:T(8,128)(2,1)S(1)} %get-tuple-element.29), channel_id=1, source_target_pairs={{0,2},{4,6},{2,0},{6,4},{1,3},{5,7},{3,1},{7,5},{8,10},{12,14},{10... | collective-permute-start | bytes 122888 | tf_op jit(solution)/shard_map/ppermute | solution.py:323
  12.7 4.2 %collective-permute-start.1 = (bf16[20,8,128]{2,1,0:T(8,128)(2,1)S(1)}, bf16[20,8,128]{2,1,0:T(8,128)(2,1)S(1)}, u32[]{:S(2)}, u32[]{:S(2)}) collective-permute-start(bf16[20,8,128]{2,1,0:T(8,128)(2,1)S(1)} %get-tuple-element.30), channel_id=1, source_target_pairs={{2,4},{4,2},{3,5},{5,3},{10,12},{12,10},{11,13},{13,11},{18,20},{2... | collective-permute-start | bytes 122888 | tf_op jit(solution)/shard_map/ppermute | solution.py:323
  16.9 0.0 collective-permute-done.got_0
  17.0 1.4 %collective-permute-done.1.got_1 = bf16[20,8,128]{2,1,0:T(8,128)(2,1)S(1)} collective-permute-done((bf16[20,8,128]{2,1,0:T(8,128)(2,1)S(1)}, bf16[20,8,128]{2,1,0:T(8,128)(2,1)S(1)}, u32[]{:S(2)}, u32[]{:S(2)}) %collective-permute-start.1) | collective-permute-done | bytes 40992 | tf_op jit(solution)/shard_map/ppermute | solution.py:323
  18.4 2.0 %collective-permute-start.4 = (bf16[64,128]{1,0:T(8,128)(2,1)S(1)}, bf16[64,128]{1,0:T(8,128)(2,1)S(1)}, u32[]{:S(2)}, u32[]{:S(2)}) collective-permute-start(bf16[64,128]{1,0:T(8,128)(2,1)S(1)} %get-tuple-element.35), channel_id=1, source_target_pairs={{0,8},{16,24},{32,40},{48,56},{64,72},{80,88},{96,104},{112,120},{... | collective-permute-start | bytes 49160 | tf_op jit(solution)/shard_map/ppermute | solution.py:323
  20.3 8.1 %collective-permute-start.5 = (bf16[64,128]{1,0:T(8,128)(2,1)S(1)}, bf16[64,128]{1,0:T(8,128)(2,1)S(1)}, u32[]{:S(2)}, u32[]{:S(2)}) collective-permute-start(bf16[64,128]{1,0:T(8,128)(2,1)S(1)} %get-tuple-element.36), channel_id=1, source_target_pairs={{8,16},{24,32},{40,48},{56,64},{72,80},{88,96},{104,112},{120,128}... | collective-permute-start | bytes 49160 | tf_op jit(solution)/shard_map/ppermute | solution.py:323
  28.5 0.0 copy-start.2
  28.5 0.2 shard_map.93.act_up
  28.7 0.0 collective-permute-done.4.cor_0
  28.7 0.8 %collective-permute-done.5.cor_1 = bf16[64,128]{1,0:T(8,128)(2,1)S(1)} collective-permute-done((bf16[64,128]{1,0:T(8,128)(2,1)S(1)}, bf16[64,128]{1,0:T(8,128)(2,1)S(1)}, u32[]{:S(2)}, u32[]{:S(2)}) %collective-permute-start.5) | collective-permute-done | bytes 16416 | tf_op jit(solution)/shard_map/ppermute | solution.py:323
  29.6 0.0 collective-permute-done.2.row_0
  29.6 0.0 collective-permute-done.3.row_1
  29.6 0.4 shard_map.95
  30.0 33.8 %collective-permute-start.6 = (bf16[12,352,128]{2,1,0:T(8,128)(2,1)S(1)}, bf16[12,352,128]{2,1,0:T(8,128)(2,1)S(1)}, u32[]{:S(2)}, u32[]{:S(2)}) collective-permute-start(bf16[12,352,128]{2,1,0:T(8,128)(2,1)S(1)} %get-tuple-element.37), channel_id=1, source_target_pairs={{0,1},{1,0},{2,3},{3,2},{4,5},{5,4},{6,7},{7,6},{8,9},{9,8},{10,11... | collective-permute-start | bytes 3244040 | tf_op jit(solution)/shard_map/ppermute | solution.py:327
  63.9 0.0 copy-done.2
  63.9 1.6 %shard_map.96.part_in = f32[6,352,128]{2,1,0:T(8,128)S(1)} custom-call(bf16[8,320,128]{2,1,0:T(8,128)(2,1)S(1)} %bitcast.10, bf16[4,320,128]{2,1,0:T(8,128)(2,1)S(1)} %shard_map.93.act_up, bf16[320,128]{1,0:T(8,128)(2,1)S(1)} %get-tuple-element.31.merged, bf16[64,128]{1,0:T(8,128)(2,1)S(1)} %get-tuple-element.32.act_edge, ...), custom_call_target="tpu_custom_call" | custom-call | flops 1509949440 | bytes 4000000 | tf_op jit(solution)/shard_map/pallas_call | solution.py:29
  65.5 1.2 %shard_map.97 = (f32[4,352,128]{2,1,0:T(8,128)S(1)}, bf16[10,352,128]{2,1,0:T(8,128)(2,1)S(1)}) custom-call(bf16[8,320,128]{2,1,0:T(8,128)(2,1)S(1)} %bitcast.11, bf16[4,320,128]{2,1,0:T(8,128)(2,1)S(1)} %shard_map.93.act_up, bf16[320,128]{1,0:T(8,128)(2,1)S(1)} %get-tuple-element.31.merged, bf16[64,128]{1,0:T(8,128)(2,1)S(1)} %get-tuple-element.32.act_edge, ...), custom_call_target="tpu_custom_call" | custom-call | flops 754974720 | bytes 4000000 | tf_op jit(solution)/shard_map/pallas_call | solution.py:29
  66.7 0.0 collective-permute-done.6.middle
  66.7 0.0 copy-start.4
  66.7 1.9 %shard_map.98 = (bf16[10,352,128]{2,1,0:T(8,128)(2,1)S(1)}, bf16[10,352,128]{2,1,0:T(8,128)(2,1)S(1)}) custom-call(bf16[12,352,128]{2,1,0:T(8,128)(2,1)S(1)} %collective-permute-done.6.middle, f32[6,352,128]{2,1,0:T(8,128)S(1)} %shard_map.96.part_in, f32[4,352,128]{2,1,0:T(8,128)S(1)} %get-tuple-element.40.part_out, ...), custom_call_target="tpu_custom_call" | custom-call | flops 754974720 | bytes 6000000 | tf_op jit(solution)/shard_map/pallas_call | solution.py:29
  68.6 2.0 %collective-permute-start.7 = (bf16[10,352,128]{2,1,0:T(8,128)(2,1)S(1)}, bf16[10,352,128]{2,1,0:T(8,128)(2,1)S(1)}, u32[]{:S(2)}, u32[]{:S(2)}) collective-permute-start(bf16[10,352,128]{2,1,0:T(8,128)(2,1)S(1)} %get-tuple-element.43), channel_id=1, source_target_pairs={{0,1},{1,0},{2,3},{3,2},{4,5},{5,4},{6,7},{7,6},{8,9},{9,8},{10,11... | collective-permute-start | bytes 2703368 | tf_op jit(solution)/shard_map/ppermute | solution.py:327
  70.5 0.0 copy-done.4
  70.6 2.2 %shard_map.99.part = f32[8,320,128]{2,1,0:T(8,128)S(1)} custom-call(bf16[10,352,128]{2,1,0:T(8,128)(2,1)S(1)} %get-tuple-element.42.two_frame, bf16[10,352,128]{2,1,0:T(8,128)(2,1)S(1)} %get-tuple-element.44.act_two, bf16[3,3,3,128,128]{4,3,2,1,0:T(8,128)(2,1)S(1)} %copy-done.4, bf16[4,160,128]{2,1,0:T(8,128)(2,1)S(1)} %get-tuple-element.45.proj, ...), custom_call_target="tpu_custom_call" | custom-call | flops 1509949440 | bytes 6000000 | tf_op jit(solution)/shard_map/pallas_call | solution.py:29
  72.7 0.2 collective-permute-done.7.middle
  73.0 2.0 %shard_map.100 = bf16[8,320,128]{2,1,0:T(8,128)(2,1)} custom-call(bf16[10,352,128]{2,1,0:T(8,128)(2,1)S(1)} %collective-permute-done.7.middle, f32[8,320,128]{2,1,0:T(8,128)S(1)} %shard_map.99.part, bf16[3,3,3,128,128]{4,3,2,1,0:T(8,128)(2,1)S(1)} %copy-done.4), custom_call_target="tpu_custom_call" | custom-call | flops 754974720 | bytes 6000000 | tf_op jit(solution)/shard_map/pallas_call | solution.py:29
  (4 shorter events, 0.0 us)
Async XLA Ops:
  0.0 1.2 %copy-start.1 = (bf16[1,8,320,128]{3,2,1,0:T(8,128)(2,1)S(1)}, bf16[1,8,320,128]{3,2,1,0:T(8,128)(2,1)}, u32[]{:S(2)}) copy-start(bf16[1,8,320,128]{3,2,1,0:T(8,128)(2,1)} %param.13) | copy-start | bytes 1966084
  0.0 1.4 %copy-start = (bf16[1,8,320,128]{3,2,1,0:T(8,128)(2,1)S(1)}, bf16[1,8,320,128]{3,2,1,0:T(8,128)(2,1)}, u32[]{:S(2)}) copy-start(bf16[1,8,320,128]{3,2,1,0:T(8,128)(2,1)} %param.12) | copy-start | bytes 1966084
  0.0 1.5 %copy-start.3 = (bf16[1,4,160,256]{3,2,1,0:T(8,128)(2,1)S(1)}, bf16[1,4,160,256]{3,2,1,0:T(8,128)(2,1)}, u32[]{:S(2)}) copy-start(bf16[1,4,160,256]{3,2,1,0:T(8,128)(2,1)} %param.9) | copy-start | bytes 983044
  1.8 27.8 %collective-permute-start.2 = (bf16[1120,128]{1,0:T(8,128)(2,1)S(1)}, bf16[1120,128]{1,0:T(8,128)(2,1)S(1)}, u32[]{:S(2)}, u32[]{:S(2)}) collective-permute-start(bf16[1120,128]{1,0:T(8,128)(2,1)S(1)} %get-tuple-element.33), channel_id=1, source_target_pairs={{0,8},{16,24},{32,40},{48,56},{64,72},{80,88},{96,104},{112,120},{... | collective-permute-start | bytes 860168 | tf_op jit(solution)/shard_map/ppermute | solution.py:323
  3.7 25.8 %collective-permute-start.3 = (bf16[1120,128]{1,0:T(8,128)(2,1)S(1)}, bf16[1120,128]{1,0:T(8,128)(2,1)S(1)}, u32[]{:S(2)}, u32[]{:S(2)}) collective-permute-start(bf16[1120,128]{1,0:T(8,128)(2,1)S(1)} %get-tuple-element.34), channel_id=1, source_target_pairs={{8,16},{24,32},{40,48},{56,64},{72,80},{88,96},{104,112},{120,128}... | collective-permute-start | bytes 860168 | tf_op jit(solution)/shard_map/ppermute | solution.py:323
  10.7 6.3 %collective-permute-start = (bf16[20,8,128]{2,1,0:T(8,128)(2,1)S(1)}, bf16[20,8,128]{2,1,0:T(8,128)(2,1)S(1)}, u32[]{:S(2)}, u32[]{:S(2)}) collective-permute-start(bf16[20,8,128]{2,1,0:T(8,128)(2,1)S(1)} %get-tuple-element.29), channel_id=1, source_target_pairs={{0,2},{4,6},{2,0},{6,4},{1,3},{5,7},{3,1},{7,5},{8,10},{12,14},{10... | collective-permute-start | bytes 122888 | tf_op jit(solution)/shard_map/ppermute | solution.py:323
  12.7 5.6 %collective-permute-start.1 = (bf16[20,8,128]{2,1,0:T(8,128)(2,1)S(1)}, bf16[20,8,128]{2,1,0:T(8,128)(2,1)S(1)}, u32[]{:S(2)}, u32[]{:S(2)}) collective-permute-start(bf16[20,8,128]{2,1,0:T(8,128)(2,1)S(1)} %get-tuple-element.30), channel_id=1, source_target_pairs={{2,4},{4,2},{3,5},{5,3},{10,12},{12,10},{11,13},{13,11},{18,20},{2... | collective-permute-start | bytes 122888 | tf_op jit(solution)/shard_map/ppermute | solution.py:323
  18.4 10.4 %collective-permute-start.4 = (bf16[64,128]{1,0:T(8,128)(2,1)S(1)}, bf16[64,128]{1,0:T(8,128)(2,1)S(1)}, u32[]{:S(2)}, u32[]{:S(2)}) collective-permute-start(bf16[64,128]{1,0:T(8,128)(2,1)S(1)} %get-tuple-element.35), channel_id=1, source_target_pairs={{0,8},{16,24},{32,40},{48,56},{64,72},{80,88},{96,104},{112,120},{... | collective-permute-start | bytes 49160 | tf_op jit(solution)/shard_map/ppermute | solution.py:323
  20.3 9.3 %collective-permute-start.5 = (bf16[64,128]{1,0:T(8,128)(2,1)S(1)}, bf16[64,128]{1,0:T(8,128)(2,1)S(1)}, u32[]{:S(2)}, u32[]{:S(2)}) collective-permute-start(bf16[64,128]{1,0:T(8,128)(2,1)S(1)} %get-tuple-element.36), channel_id=1, source_target_pairs={{8,16},{24,32},{40,48},{56,64},{72,80},{88,96},{104,112},{120,128}... | collective-permute-start | bytes 49160 | tf_op jit(solution)/shard_map/ppermute | solution.py:323
  28.5 35.4 %copy-start.2 = (bf16[3,3,3,128,128]{4,3,2,1,0:T(8,128)(2,1)S(1)}, bf16[3,3,3,128,128]{4,3,2,1,0:T(8,128)(2,1)}, u32[]{:S(2)}) copy-start(bf16[3,3,3,128,128]{4,3,2,1,0:T(8,128)(2,1)} %weight.9) | copy-start | bytes 2654212
  30.0 36.6 %collective-permute-start.6 = (bf16[12,352,128]{2,1,0:T(8,128)(2,1)S(1)}, bf16[12,352,128]{2,1,0:T(8,128)(2,1)S(1)}, u32[]{:S(2)}, u32[]{:S(2)}) collective-permute-start(bf16[12,352,128]{2,1,0:T(8,128)(2,1)S(1)} %get-tuple-element.37), channel_id=1, source_target_pairs={{0,1},{1,0},{2,3},{3,2},{4,5},{5,4},{6,7},{7,6},{8,9},{9,8},{10,11... | collective-permute-start | bytes 3244040 | tf_op jit(solution)/shard_map/ppermute | solution.py:327
  66.7 3.9 %copy-start.4 = (bf16[3,3,3,128,128]{4,3,2,1,0:T(8,128)(2,1)S(1)}, bf16[3,3,3,128,128]{4,3,2,1,0:T(8,128)(2,1)}, u32[]{:S(2)}) copy-start(bf16[3,3,3,128,128]{4,3,2,1,0:T(8,128)(2,1)} %weight.11) | copy-start | bytes 2654212
  68.6 4.4 %collective-permute-start.7 = (bf16[10,352,128]{2,1,0:T(8,128)(2,1)S(1)}, bf16[10,352,128]{2,1,0:T(8,128)(2,1)S(1)}, u32[]{:S(2)}, u32[]{:S(2)}) collective-permute-start(bf16[10,352,128]{2,1,0:T(8,128)(2,1)S(1)} %get-tuple-element.43), channel_id=1, source_target_pairs={{0,1},{1,0},{2,3},{3,2},{4,5},{5,4},{6,7},{7,6},{8,9},{9,8},{10,11... | collective-permute-start | bytes 2703368 | tf_op jit(solution)/shard_map/ppermute | solution.py:327
